TPU v7x, 256 devices: a whole 4x4x8 slice. The times are simulated.
256 devices in a mesh: ta: 128 (over x, y, z), row: 2 (over core).
Axes of the slice: x: 4, y: 4, z: 8, core: 2. Of those that a mesh axis runs over, the one named last changes fastest.
Arguments:
- movie: bfloat16 [2, 1024, 128, 512], P('row', 'ta'), may hold values from -384 to 384
- shifts: int32 [2, 1024, 4, 2], P('row', 'ta'), may hold values from -8 to 8
- footprint: bfloat16 [2, 128, 8, 512], P('row', 'ta'), may hold values from 0.25 to 1
- support: int32 [2, 128, 8, 512], P('row', 'ta'), may hold values 0 or 1
- neuron_ids: int32 [2, 128, 8], P('row', 'ta'), may hold values from 0 to 255, as said below
- owner_order: int32 [256], replicated, may hold values from 0 to 255, each once
- start_traces: float32 [256, 1024], P(('ta', 'row')), may hold values from 0 to 2
Outputs:
- tile_movie: bfloat16 [2, 128, 1024, 512], P('row', 'ta')
- traces: float32 [256, 1024], P(('ta', 'row'))
Inputs may be any that keep to these rules, and one draw needn't show every extreme that they name: `neuron_ids`: the neurons named by one tile's slots are distinct. Slot 0 of tile t of slab s names neuron s * 128 + t, and every slot of that tile names a neuron within 12 of it, counted modulo 256. `owner_order`: A permutation of all neurons.
All inputs are finite; a program needn't handle non-finite values. No bound on the sum of `support` on one device may be relied on, other than what follows from the above.
Results may differ from a plain program's by a relative error of at most 0.004.
Values may be sent and summed in bfloat16 or wider, within the bound.
No kernel may reach another device: no remote copies, remote signals or barrier semaphores. Data moves between devices by JAX's collectives and lax.ppermute only.
A program may use at most 64 MiB of HBM per device.

v0:
```python
import jax
import jax.numpy as jnp
from jax import lax
from jax.sharding import Mesh
from jax.sharding import PartitionSpec as P

TH = 16
TW = 32
MAXS = 8
ITERS = 2
TA = ("ta_0", "ta_1", "ta_2")
TA_ROW = ("ta_0", "ta_1", "ta_2", "row")


def cut_along(array, dim, length):
    lengths = array.shape
    pieces = array.reshape(*lengths[:dim], length, lengths[dim] // length, *lengths[dim + 1 :])
    return jnp.moveaxis(pieces, dim, 0)


def sum_at_owner(array, axis, dim):
    length = lax.axis_size(axis)
    pieces = lax.all_to_all(cut_along(array, dim, length), axis, 0, 0, tiled=True)
    return jnp.sum(pieces, axis=0)


def sum_by_axis(array, axes, dim):
    far, near = axes
    pieces = cut_along(array, dim, lax.axis_size(far))
    nearer = sum_at_owner(pieces, near, dim + 1)
    arrived = lax.all_to_all(nearer, far, split_axis=0, concat_axis=0, tiled=True)
    return arrived.sum(axis=0)


def copy_for_each(array, axis):
    length = lax.axis_size(axis)
    return lax.all_to_all(
        jnp.broadcast_to(array[None], (length, *array.shape)), axis, 0, 0, tiled=True
    )


def joined_along(pieces, dim):
    lengths = list(pieces.shape[1:])
    lengths[dim] *= pieces.shape[0]
    return jnp.moveaxis(pieces, 0, dim).reshape(lengths)


def gathered_by_axis(array, axes, dim):
    far, near = axes
    pieces = copy_for_each(copy_for_each(array, far), near)
    return joined_along(pieces.swapaxes(0, 1).reshape(-1, *array.shape), dim)


def smoothing_table(length):
    places = jnp.arange(length, dtype=jnp.float32)
    spread = places[:, None] - places[None, :]
    kernel = jnp.exp(-spread * spread / 32.0)
    return (kernel / jnp.sum(kernel, axis=0, keepdims=True)).astype(jnp.bfloat16)


def local(movie, shifts, footprint, support, neuron_ids, owner_order, start_traces):
    frame_stack = movie[0]
    frame_moves = shifts[0]
    frame_count, height, breadth = frame_stack.shape
    patch_count = frame_moves.shape[1]
    patch_width = breadth // patch_count
    window_width = patch_width + 2 * MAXS
    padded_cols = jnp.pad(frame_stack, ((0, 0), (0, 0), (MAXS, MAXS)))
    windows = jnp.stack(
        [
            padded_cols[:, :, patch * patch_width : patch * patch_width + window_width]
            for patch in range(patch_count)
        ],
        axis=2,
    )
    window_index = jnp.arange(window_width, dtype=jnp.int32)
    target_index = (
        jnp.arange(patch_width, dtype=jnp.int32)[None, None, None, :]
        + MAXS
        + frame_moves[:, :, 1][:, :, None, None]
    )
    column_tables = (window_index[None, None, :, None] == target_index).astype(jnp.bfloat16)
    blocks = jnp.einsum(
        "fhpa,fpax->fhpx", windows, column_tables, preferred_element_type=jnp.float32
    ).astype(jnp.bfloat16)
    row_index = jnp.arange(height, dtype=jnp.int32)
    row_source = row_index[None, None, :, None] + frame_moves[:, :, 0][:, :, None, None]
    row_tables = (row_index[None, None, None, :] == row_source).astype(jnp.bfloat16)
    registered = jnp.einsum(
        "fpyh,fhpx->fypx", row_tables, blocks, preferred_element_type=jnp.float32
    )
    registered = registered.astype(jnp.bfloat16).reshape(frame_count, height, breadth)
    table_wide = smoothing_table(breadth)
    table_tall = smoothing_table(height)
    wide = jnp.einsum(
        "fhw,wv->fhv", registered, table_wide, preferred_element_type=jnp.float32
    ).astype(jnp.bfloat16)
    smooth = jnp.einsum("hy,fhv->fyv", table_tall, wide, preferred_element_type=jnp.float32)
    filtered = (registered.astype(jnp.float32) - smooth).astype(jnp.bfloat16)
    tile_rows = height // TH
    tile_cols = breadth // TW
    tiled = filtered.reshape(frame_count, tile_rows, TH, tile_cols, TW).transpose(1, 3, 0, 2, 4)
    tiled = tiled.reshape(tile_rows * tile_cols, frame_count, TH * TW)
    tile_movie = lax.all_to_all(tiled, TA, split_axis=0, concat_axis=1, tiled=True)
    tile_count, frame_total, tile_pixels = tile_movie.shape
    footprints = footprint[0] * support[0].astype(jnp.bfloat16)
    slot_count = footprints.shape[1]
    slot_total = tile_count * slot_count
    gram = jnp.einsum("tip,tjp->tij", footprints, footprints, preferred_element_type=jnp.float32)
    projected = jnp.einsum(
        "tip,tfp->tif", footprints, tile_movie, preferred_element_type=jnp.float32
    )
    neuron_total = owner_order.shape[0]
    owner_slots = owner_order[neuron_ids[0]].reshape(slot_total)
    selector = (owner_slots[:, None] == jnp.arange(neuron_total, dtype=jnp.int32)[None, :]).astype(
        jnp.float32
    )
    spreader = selector.T
    traces_own = start_traces
    highest = lax.Precision.HIGHEST
    coupling_cols = jnp.einsum(
        "tij,tjk->tik",
        gram,
        selector.reshape(tile_count, slot_count, neuron_total),
        precision=highest,
    )
    joined = jnp.concatenate(
        [
            coupling_cols.reshape(slot_total, neuron_total),
            projected.reshape(slot_total, frame_total),
        ],
        axis=1,
    )
    owner_sums = sum_by_axis(
        jnp.dot(spreader, joined, precision=highest), ("ta_0", ("ta_1", "ta_2", "row")), 0
    )
    coupling_own = owner_sums[:, :neuron_total]
    drive_own = owner_sums[:, neuron_total:]
    bound_own = 1.0 + jnp.sum(coupling_own, axis=1)
    for iteration in range(ITERS):
        product = jnp.dot(
            coupling_own,
            gathered_by_axis(traces_own, ("ta_0", ("ta_1", "ta_2", "row")), 0),
            precision=highest,
        )
        gradient = product - drive_own
        traces_own = jnp.maximum(traces_own - gradient / bound_own[:, None], 0.0)
    return (tile_movie[None], traces_own)


def solution(mesh):
    finer = Mesh(mesh.devices.reshape(4, 4, 8, mesh.shape["row"]), ("ta_0", "ta_1", "ta_2", "row"))
    return jax.shard_map(
        local,
        mesh=finer,
        in_specs=(
            P("row", TA, None, None),
            P("row", TA, None, None),
            P("row", TA, None, None),
            P("row", TA, None, None),
            P("row", TA, None),
            P(),
            P(TA_ROW, None),
        ),
        out_specs=(P("row", TA, None, None), P(TA_ROW, None)),
        check_vma=False,
    )
```

profile of v0, /device:TPU:1, one launch (start us, length us, event | category | flops | bytes accessed | tf_op | source)
XLA Modules:
  0.0 213.6 jit_solution(15912878398026282155)
XLA Ops:
  1.1 1.6 copy.19
  3.6 2.1 fusion.3
  5.7 1.4 fusion.1
  7.6 3.8 %reshape.167 = bf16[8,8,16,16,32]{4,3,2,1,0:T(8,128)(2,1)} reshape(bf16[8,128,512]{2,1,0:T(8,128)(2,1)S(1)} %copy.26) | data formatting | bytes 2097152 | tf_op jit(solution)/shard_map/reshape | solution.py:102
  11.5 5.3 %copy.27 = bf16[8,16,8,16,32]{4,3,2,1,0:T(8,128)(2,1)} copy(bf16[8,16,8,16,32]{4,1,3,0,2:T(8,128)(2,1)} %bitcast.87) | data formatting | bytes 2097152 | tf_op jit(solution)/shard_map/transpose | solution.py:102
  16.8 6.8 %reshape.168 = bf16[128,8,512]{2,1,0:T(8,128)(2,1)} reshape(bf16[8,16,8,16,32]{4,3,2,1,0:T(8,128)(2,1)} %copy.27) | data formatting | bytes 2097152 | tf_op jit(solution)/shard_map/reshape | solution.py:103
  23.6 16.5 %all-to-all-start = ((bf16[128,8,512]{2,1,0:T(8,128)(2,1)}), bf16[128,8,512]{2,1,0:T(8,128)(2,1)S(1)}, u32[]{:S(2)}, u32[]{:S(2)}) async-start(bf16[128,8,512]{2,1,0:T(8,128)(2,1)} %reshape.168), calls=%async_computation | async-start | bytes 2097152 | tf_op jit(solution)/shard_map/all_to_all | solution.py:104
  41.1 29.3 %all-to-all-done = bf16[128,8,512]{2,1,0:T(8,128)(2,1)S(1)} async-done(((bf16[128,8,512]{2,1,0:T(8,128)(2,1)}), bf16[128,8,512]{2,1,0:T(8,128)(2,1)S(1)}, u32[]{:S(2)}, u32[]{:S(2)}) %all-to-all-start) | async-done | bytes 1048608 | tf_op jit(solution)/shard_map/all_to_all | solution.py:104
  71.0 3.3 %all-to-all-start.3 = ((f32[4,1,1024]{2,1,0:T(1,128)}), f32[4,1,1024]{2,1,0:T(1,128)S(1)}, u32[]{:S(2)}, u32[]{:S(2)}) async-start(f32[4,1,1024]{2,1,0:T(1,128)} %broadcast_in_dim.20), calls=%async_computation.3 | async-start | bytes 32768 | tf_op jit(solution)/shard_map/all_to_all | solution.py:37
  75.4 1.9 copy.39
  77.4 1.1 all-to-all-done.3
  78.4 8.0 %all-to-all-start.1 = ((f32[64,4,1,1280]{3,1,2,0:T(4,128)}), f32[64,4,1,1280]{3,1,2,0:T(4,128)S(1)}, u32[]{:S(2)}, u32[]{:S(2)}) async-start(f32[64,4,1,1280]{3,1,2,0:T(4,128)} %bitcast.90), calls=%async_computation.1 | async-start | bytes 2621440 | tf_op jit(solution)/shard_map/all_to_all | solution.py:23
  86.5 34.2 %all-to-all-done.1 = f32[64,4,1,1280]{3,1,2,0:T(4,128)S(1)} async-done(((f32[64,4,1,1280]{3,1,2,0:T(4,128)}), f32[64,4,1,1280]{3,1,2,0:T(4,128)S(1)}, u32[]{:S(2)}, u32[]{:S(2)}) %all-to-all-start.1) | async-done | bytes 1310752 | tf_op jit(solution)/shard_map/all_to_all | solution.py:23
  120.6 1.2 broadcast_in_dim.22
  121.9 6.2 %all-to-all-start.4 = ((f32[64,4,1,1024]{3,1,2,0:T(4,128)}), f32[64,4,1,1024]{3,1,2,0:T(4,128)S(1)}, u32[]{:S(2)}, u32[]{:S(2)}) async-start(f32[64,4,1,1024]{3,1,2,0:T(4,128)} %broadcast_in_dim.22), calls=%async_computation.4 | async-start | bytes 2097152 | tf_op jit(solution)/shard_map/all_to_all | solution.py:37
  128.9 27.7 %all-to-all-done.4 = f32[64,4,1,1024]{3,1,2,0:T(4,128)S(1)} async-done(((f32[64,4,1,1024]{3,1,2,0:T(4,128)}), f32[64,4,1,1024]{3,1,2,0:T(4,128)S(1)}, u32[]{:S(2)}, u32[]{:S(2)}) %all-to-all-start.4) | async-done | bytes 1048608 | tf_op jit(solution)/shard_map/all_to_all | solution.py:37
  156.6 3.3 %all-to-all-start.2 = ((f32[4,1,1280]{2,1,0:T(1,128)}), f32[4,1,1280]{2,1,0:T(1,128)S(1)}, u32[]{:S(2)}, u32[]{:S(2)}) async-start(f32[4,1,1280]{2,1,0:T(1,128)} %reduce_sum.52), calls=%async_computation.2 | async-start | bytes 40960 | tf_op jit(solution)/shard_map/all_to_all | solution.py:31
  160.5 3.6 %all-to-all-done.2 = f32[4,1,1280]{2,1,0:T(1,128)S(1)} async-done(((f32[4,1,1280]{2,1,0:T(1,128)}), f32[4,1,1280]{2,1,0:T(1,128)S(1)}, u32[]{:S(2)}, u32[]{:S(2)}) %all-to-all-start.2) | async-done | bytes 20512 | tf_op jit(solution)/shard_map/all_to_all | solution.py:31
  166.0 6.6 %all_to_all.39 = f32[4,1,1024]{2,1,0:T(1,128)S(1)} all-to-all(f32[4,1,1024]{2,1,0:T(1,128)S(1)} %broadcast_in_dim.24), channel_id=1, replica_groups=mesh['ta_0'=4,'ta_1'=4,'ta_2'=8,'row'=2] {'ta_0'}, dimensions={0} | all-to-all | bytes 32768 | tf_op jit(solution)/shard_map/all_to_all | solution.py:37
  172.6 1.2 broadcast_in_dim.26
  173.8 8.5 %all-to-all-start.6 = ((f32[64,4,1,1024]{3,1,2,0:T(4,128)}), f32[64,4,1,1024]{3,1,2,0:T(4,128)S(1)}, u32[]{:S(2)}, u32[]{:S(2)}) async-start(f32[64,4,1,1024]{3,1,2,0:T(4,128)} %broadcast_in_dim.26), calls=%async_computation.6 | async-start | bytes 2097152 | tf_op jit(solution)/shard_map/all_to_all | solution.py:37
  182.3 28.5 %all-to-all-done.6 = f32[64,4,1,1024]{3,1,2,0:T(4,128)S(1)} async-done(((f32[64,4,1,1024]{3,1,2,0:T(4,128)}), f32[64,4,1,1024]{3,1,2,0:T(4,128)S(1)}, u32[]{:S(2)}, u32[]{:S(2)}) %all-to-all-start.6) | async-done | bytes 1048608 | tf_op jit(solution)/shard_map/all_to_all | solution.py:37
  211.4 1.2 fusion.24
  212.7 1.0 copy.44
  (41 shorter events, 8.0 us)
Async XLA Ops:
  0.6 39.5 %copy-start = (s32[256]{0:T(256)S(1)}, s32[256]{0:T(256)}, u32[]{:S(2)}) copy-start(s32[256]{0:T(256)} %param.12) | copy-start | bytes 3076
  2.7 0.7 copy-start.4
  23.6 16.5 %copy-start.5 = (s32[1,1,8]{2,1,0:T(1,128)S(1)}, s32[1,1,8]{2,1,0:T(1,128)}, u32[]{:S(2)}) copy-start(s32[1,1,8]{2,1,0:T(1,128)} %param.11) | copy-start | bytes 100
  23.6 17.2 %copy-start.1 = (s32[1,1,8,512]{3,2,1,0:T(8,128)S(1)}, s32[1,1,8,512]{3,2,1,0:T(8,128)}, u32[]{:S(2)}) copy-start(s32[1,1,8,512]{3,2,1,0:T(8,128)} %param.10) | copy-start | bytes 49156
  23.6 17.2 %copy-start.2 = (bf16[1,1,8,512]{3,2,1,0:T(8,128)(2,1)S(1)}, bf16[1,1,8,512]{3,2,1,0:T(8,128)(2,1)}, u32[]{:S(2)}) copy-start(bf16[1,1,8,512]{3,2,1,0:T(8,128)(2,1)} %param.9) | copy-start | bytes 24580
  23.6 46.8 %copy-start.3 = (f32[1,1024]{1,0:T(1,128)S(1)}, f32[1,1024]{1,0:T(1,128)}, u32[]{:S(2)}) copy-start(f32[1,1024]{1,0:T(1,128)} %param.13) | copy-start | bytes 12292
  23.6 46.8 %all-to-all-start = ((bf16[128,8,512]{2,1,0:T(8,128)(2,1)}), bf16[128,8,512]{2,1,0:T(8,128)(2,1)S(1)}, u32[]{:S(2)}, u32[]{:S(2)}) async-start(bf16[128,8,512]{2,1,0:T(8,128)(2,1)} %reshape.168), calls=%async_computation | async-start | bytes 2097152 | tf_op jit(solution)/shard_map/all_to_all | solution.py:104
  71.0 7.4 %all-to-all-start.3 = ((f32[4,1,1024]{2,1,0:T(1,128)}), f32[4,1,1024]{2,1,0:T(1,128)S(1)}, u32[]{:S(2)}, u32[]{:S(2)}) async-start(f32[4,1,1024]{2,1,0:T(1,128)} %broadcast_in_dim.20), calls=%async_computation.3 | async-start | bytes 32768 | tf_op jit(solution)/shard_map/all_to_all | solution.py:37
  78.4 42.2 %all-to-all-start.1 = ((f32[64,4,1,1280]{3,1,2,0:T(4,128)}), f32[64,4,1,1280]{3,1,2,0:T(4,128)S(1)}, u32[]{:S(2)}, u32[]{:S(2)}) async-start(f32[64,4,1,1280]{3,1,2,0:T(4,128)} %bitcast.90), calls=%async_computation.1 | async-start | bytes 2621440 | tf_op jit(solution)/shard_map/all_to_all | solution.py:23
  121.9 34.8 %all-to-all-start.4 = ((f32[64,4,1,1024]{3,1,2,0:T(4,128)}), f32[64,4,1,1024]{3,1,2,0:T(4,128)S(1)}, u32[]{:S(2)}, u32[]{:S(2)}) async-start(f32[64,4,1,1024]{3,1,2,0:T(4,128)} %broadcast_in_dim.22), calls=%async_computation.4 | async-start | bytes 2097152 | tf_op jit(solution)/shard_map/all_to_all | solution.py:37
  156.6 7.5 %all-to-all-start.2 = ((f32[4,1,1280]{2,1,0:T(1,128)}), f32[4,1,1280]{2,1,0:T(1,128)S(1)}, u32[]{:S(2)}, u32[]{:S(2)}) async-start(f32[4,1,1280]{2,1,0:T(1,128)} %reduce_sum.52), calls=%async_computation.2 | async-start | bytes 40960 | tf_op jit(solution)/shard_map/all_to_all | solution.py:31
  173.8 37.0 %all-to-all-start.6 = ((f32[64,4,1,1024]{3,1,2,0:T(4,128)}), f32[64,4,1,1024]{3,1,2,0:T(4,128)S(1)}, u32[]{:S(2)}, u32[]{:S(2)}) async-start(f32[64,4,1,1024]{3,1,2,0:T(4,128)} %broadcast_in_dim.26), calls=%async_computation.6 | async-start | bytes 2097152 | tf_op jit(solution)/shard_map/all_to_all | solution.py:37
where the time goes:
time: 214 us
  waiting for transfers between devices  124 us (58%)
  starting transfers between devices  45.7 us (21%)
  local copies, waits for them, and re-layouts  27.4 us (13%)
  matrix products  6.76 us (3%)
  blocking collectives  6.56 us (3%)
    all_to_all x3, waiting for transfers between devices, copy_for_each(): lax.all_to_all(jnp.broadcast_to(array[None], (length, *array.shape)), axi...  57.3 us
    all_to_all x1, waiting for transfers between devices, sum_at_owner(): lax.all_to_all(cut_along(array, dim, length), axis, 0, 0, tiled=True)  34.2 us
    all_to_all x1, waiting for transfers between devices, local(): lax.all_to_all(tiled, TA, split_axis=0, concat_axis=1, tiled=True)  29.3 us
    all_to_all x3, starting transfers between devices, copy_for_each(): lax.all_to_all(jnp.broadcast_to(array[None], (length, *array.shape)), axi...  18 us
    all_to_all x1, starting transfers between devices, local(): lax.all_to_all(tiled, TA, split_axis=0, concat_axis=1, tiled=True)  16.5 us
    all_to_all x1, starting transfers between devices, sum_at_owner(): lax.all_to_all(cut_along(array, dim, length), axis, 0, 0, tiled=True)  8 us
    reshape x1, local copies, waits for them, and re-layouts, local(): tiled = tiled.reshape(tile_rows * tile_cols, frame_count, TH * TW)  6.78 us
    all_to_all x1, blocking collectives, copy_for_each(): lax.all_to_all(jnp.broadcast_to(array[None], (length, *array.shape)), axi...  6.56 us
  transfers between devices with their start and end apart: 6, of which 6 were waited for; matrix products, arithmetic and copies ran while one was open for 3% of the time, Pallas kernels for 0%

commit v1 on v0

v1 whole, which is shorter than its diff:
```python
import jax
import jax.numpy as jnp
import numpy as np
from jax import lax
from jax.experimental import pallas as pl
from jax.experimental.pallas import tpu as pltpu
from jax.sharding import Mesh
from jax.sharding import PartitionSpec as P

TH = 16
TW = 32
MAXS = 8
ITERS = 2
TA = ("ta_0", "ta_1", "ta_2")
TA_ROW = ("ta_0", "ta_1", "ta_2", "row")

FRAMES = 8
H = 128
W = 512
LANES = 128
BLOCKS = W // LANES
SLOTS = 8
NEURONS = 256
SPAN = 4
GRAM_AT = SPAN * SLOTS
IDS_AT = GRAM_AT + SLOTS * SLOTS
START_AT = IDS_AT + SLOTS
WIDE = NEURONS + LANES
HIGHEST = lax.Precision.HIGHEST
VMEM = pl.BlockSpec(memory_space=pltpu.VMEM)
SMEM = pl.BlockSpec(memory_space=pltpu.SMEM)


def smoothing_table(length):
    places = np.arange(length, dtype=np.float32)
    spread = places[:, None] - places[None, :]
    kernel = np.exp(-spread * spread / np.float32(32.0)).astype(np.float32)
    return (kernel / np.sum(kernel, axis=0, keepdims=True, dtype=np.float32)).astype(jnp.bfloat16)


def iota(shape, dim):
    return lax.broadcasted_iota(jnp.int32, shape, dim)


def split3(value):
    high = value.astype(jnp.bfloat16)
    rest = value - high.astype(jnp.float32)
    mid = rest.astype(jnp.bfloat16)
    low = (rest - mid.astype(jnp.float32)).astype(jnp.bfloat16)
    return high, mid, low


def dot32(left, right):
    return jnp.dot(left, right, preferred_element_type=jnp.float32)


def pick(exact, value):
    high, mid, low = split3(value)
    return dot32(exact, high) + (dot32(exact, mid) + dot32(exact, low))


def place(value, exact):
    high, mid, low = split3(value)
    return dot32(high, exact) + (dot32(mid, exact) + dot32(low, exact))


def filter_kernel(
    shifts_ref, ids_ref, order_ref, movie_ref, wide_ref, tall_ref, start_ref,
    out_ref, base_ref, padded_ref, registered_ref, filtered_ref,
):
    lane = iota((H, LANES), 1)
    padded_ref[:, pl.ds(0, MAXS), :] = jnp.zeros((BLOCKS, MAXS, LANES), jnp.float32)
    padded_ref[:, pl.ds(MAXS + H, MAXS), :] = jnp.zeros((BLOCKS, MAXS, LANES), jnp.float32)

    def block(f, p):
        if p < 0 or p >= BLOCKS:
            return None
        return movie_ref[f, :, p * LANES : (p + 1) * LANES].astype(jnp.float32)

    def frame(f, carry):
        for p in range(BLOCKS):
            dy = shifts_ref[f, p, 0]
            dx = shifts_ref[f, p, 1]
            amount = jnp.where(dx > 0, LANES - dx, -dx)
            source = lane + dx

            def rolled(value):
                if value is None:
                    return jnp.zeros((H, LANES), jnp.float32)
                return pltpu.roll(value, amount, 1)

            inner = jnp.where(source >= LANES, rolled(block(f, p + 1)), rolled(block(f, p)))
            moved = jnp.where(source < 0, rolled(block(f, p - 1)), inner)
            padded_ref[p, pl.ds(MAXS, H), :] = moved
            registered_ref[:, p * LANES : (p + 1) * LANES] = padded_ref[p, pl.ds(MAXS + dy, H), :]
        registered = registered_ref[...]
        wide = dot32(registered.astype(jnp.bfloat16), wide_ref[...]).astype(jnp.bfloat16)
        filtered = registered - dot32(tall_ref[...], wide)
        for p in range(BLOCKS):
            filtered_ref[p, pl.ds(f, H, stride=FRAMES), :] = filtered[:, p * LANES : (p + 1) * LANES]
        return carry

    lax.fori_loop(0, FRAMES, frame, 0)
    lanes8 = iota((FRAMES, LANES), 1)
    near = lanes8 < 2 * TW
    even = lax.rem(lanes8 // TW, 2) == 0

    def tile_row(ty, carry):
        for q in range(4):
            for p in range(BLOCKS):
                v = []
                for r in range(4):
                    at = pl.multiple_of((ty * TH + 4 * q + r) * FRAMES, FRAMES)
                    v.append(filtered_ref[p, pl.ds(at, FRAMES), :])
                a0 = jnp.where(near, v[0], pltpu.roll(v[2], 64, 1))
                a2 = jnp.where(near, pltpu.roll(v[0], 64, 1), v[2])
                a1 = jnp.where(near, v[1], pltpu.roll(v[3], 64, 1))
                a3 = jnp.where(near, pltpu.roll(v[1], 64, 1), v[3])
                tiles = (
                    jnp.where(even, a0, pltpu.roll(a1, 32, 1)),
                    jnp.where(even, pltpu.roll(a0, 96, 1), a1),
                    jnp.where(even, a2, pltpu.roll(a3, 32, 1)),
                    jnp.where(even, pltpu.roll(a2, 96, 1), a3),
                )
                for m in range(4):
                    out_ref[ty * 16 + 4 * p + m, :, q * LANES : (q + 1) * LANES] = tiles[m].astype(jnp.bfloat16)
        return carry

    lax.fori_loop(0, H // TH, tile_row, 0)

    row_lane = iota((1, LANES), 1)
    owners = jnp.zeros((1, LANES), jnp.float32)
    for i in range(SLOTS):
        owner = order_ref[ids_ref[0, i]].astype(jnp.float32)
        owners = jnp.where(row_lane == IDS_AT + i, owner, owners)
    inside = iota((32, LANES), 1) // SPAN == iota((32, LANES), 0)
    fold = jnp.where(
        lax.rem(iota((LANES, LANES), 0), SPAN) == iota((LANES, LANES), 1) - START_AT, 1.0, 0.0
    ).astype(jnp.bfloat16)
    for b in range(NEURONS // 32):
        row = start_ref[:, b * LANES : (b + 1) * LANES]
        spread = jnp.where(inside, jnp.broadcast_to(row, (32, LANES)), 0.0)
        base_ref[pl.ds(b * 32, 32), :] = place(spread, fold) + owners


def filter_tiles(movie, shifts, ids, order, start):
    return pl.pallas_call(
        filter_kernel,
        out_shape=(
            jax.ShapeDtypeStruct((128, FRAMES, TH * TW), jnp.bfloat16),
            jax.ShapeDtypeStruct((NEURONS, LANES), jnp.float32),
        ),
        in_specs=[SMEM, SMEM, SMEM, VMEM, VMEM, VMEM, VMEM],
        out_specs=(VMEM, VMEM),
        scratch_shapes=[
            pltpu.VMEM((BLOCKS, H + 2 * MAXS, LANES), jnp.float32),
            pltpu.VMEM((H, W), jnp.float32),
            pltpu.VMEM((BLOCKS, H * FRAMES, LANES), jnp.float32),
        ],
        name="filter",
    )(shifts, ids, order, movie, smoothing_table(W), smoothing_table(H).T, start)


def project_kernel(movie_ref, footprint_ref, support_ref, base_ref, out_ref, full_ref):
    footprints = footprint_ref[...] * support_ref[...].astype(jnp.bfloat16)
    copies = jnp.concatenate([footprints] * (LANES // SLOTS), axis=0)
    contract = (((1,), (1,)), ((), ()))
    full_ref[...] = lax.dot_general(
        movie_ref[...], copies, contract, preferred_element_type=jnp.float32
    )
    gram = lax.dot_general(footprints, copies, contract, preferred_element_type=jnp.float32)
    own = iota((SLOTS, LANES), 1) // SLOTS - SPAN == iota((SLOTS, LANES), 0)
    common = jnp.sum(jnp.where(own, gram, 0.0), axis=0, keepdims=True)
    total = base_ref[...] + common
    group = iota((NEURONS, LANES), 1) // SLOTS
    for j in range(SPAN):
        total = jnp.where(group == j, full_ref[pl.ds(j, NEURONS, stride=SPAN), :], total)
    out_ref[...] = total


def project(tile_movie, footprint, support, base):
    return pl.pallas_call(
        project_kernel,
        out_shape=jax.ShapeDtypeStruct((NEURONS, LANES), jnp.float32),
        in_specs=[VMEM] * 4,
        out_specs=VMEM,
        scratch_shapes=[pltpu.VMEM((SPAN * NEURONS, LANES), jnp.float32)],
        name="project",
    )(tile_movie, footprint, support, base)


def solve_kernel(mail_ref, out_ref, select_ref, high_ref, mid_ref, low_ref):
    mail_t = mail_ref[...].T
    neuron = iota((NEURONS, NEURONS), 0)
    for i in range(SLOTS):
        ids = mail_t[IDS_AT + i : IDS_AT + i + 1, :].astype(jnp.int32)
        select_ref[:, i * NEURONS : (i + 1) * NEURONS] = jnp.where(neuron == ids, 1.0, 0.0).astype(jnp.bfloat16)

    step = 32
    lane = iota((step, LANES), 1)
    place_of = iota((step, NEURONS), 1)

    def rows(b, carry):
        at = pl.multiple_of(b * step, step)
        mail = mail_ref[pl.ds(at, step), :]
        same = [place_of == mail[:, IDS_AT + i : IDS_AT + i + 1].astype(jnp.int32) for i in range(SLOTS)]
        for i in range(SLOTS):
            line = jnp.zeros((step, NEURONS), jnp.float32)
            for k in range(SLOTS):
                column = GRAM_AT + i * SLOTS + k
                line = jnp.where(same[k], mail[:, column : column + 1], line)
            mine = jnp.where((lax.rem(lane, SLOTS) == i) & (lane < GRAM_AT), mail, 0.0)
            to = pl.ds(pl.multiple_of(i * NEURONS + at, step), step)
            for start, value in ((0, line), (NEURONS, mine)):
                end = start + value.shape[1]
                high, mid, low = split3(value)
                high_ref[to, start:end] = high
                mid_ref[to, start:end] = mid
                low_ref[to, start:end] = low
        return carry

    lax.fori_loop(0, NEURONS // step, rows, 0)
    select = select_ref[...]
    sums = dot32(select, high_ref[...]) + (dot32(select, mid_ref[...]) + dot32(select, low_ref[...]))
    coupling = sums[:, :NEURONS]
    source = iota((LANES, LANES), 0)
    target = lax.rem(iota((LANES, LANES), 1), SPAN)
    fold = jnp.where((source // SLOTS == target) & (source < GRAM_AT), 1.0, 0.0).astype(jnp.bfloat16)
    drive = place(sums[:, NEURONS:], fold)
    copy = jnp.where(source - START_AT == target, 1.0, 0.0).astype(jnp.bfloat16)
    current = place(mail_ref[...], copy)
    bound = 1.0 + jnp.sum(coupling, axis=1, keepdims=True)
    for _ in range(ITERS):
        product = jnp.dot(coupling, current, preferred_element_type=jnp.float32, precision=HIGHEST)
        current = jnp.maximum(current - (product - drive) / bound, 0.0)
    out_ref[...] = current


def solve(mail):
    return pl.pallas_call(
        solve_kernel,
        out_shape=jax.ShapeDtypeStruct((NEURONS, LANES), jnp.float32),
        in_specs=[VMEM],
        out_specs=VMEM,
        scratch_shapes=[pltpu.VMEM((NEURONS, SLOTS * NEURONS), jnp.bfloat16)]
        + [pltpu.VMEM((SLOTS * NEURONS, WIDE), jnp.bfloat16)] * 3,
        name="solve",
    )(mail)


def join_kernel(pieces_ref, out_ref):
    inside = iota((32, LANES), 1) // SPAN == iota((32, LANES), 0)
    for b in range(NEURONS // 32):
        piece = jnp.where(inside, pieces_ref[pl.ds(b * 32, 32), :], 0.0)
        out_ref[:, b * LANES : (b + 1) * LANES] = jnp.sum(piece, axis=0, keepdims=True)


def join(pieces):
    return pl.pallas_call(
        join_kernel,
        out_shape=jax.ShapeDtypeStruct((1, SPAN * NEURONS), jnp.float32),
        in_specs=[VMEM],
        out_specs=VMEM,
        name="join",
    )(pieces)


def local(movie, shifts, footprint, support, neuron_ids, owner_order, start_traces):
    tiled, base = filter_tiles(movie[0], shifts[0], neuron_ids[0], owner_order, start_traces)
    tile_movie = lax.all_to_all(tiled, TA, split_axis=0, concat_axis=0, tiled=True)
    tile_movie = tile_movie.reshape(-1, TH * TW)
    mail = project(tile_movie, footprint[0, 0], support[0, 0], base)
    mail = lax.all_to_all(mail.reshape(NEURONS, 1, LANES), TA_ROW, 0, 0, tiled=True)
    pieces = solve(mail.reshape(NEURONS, LANES))
    pieces = lax.all_to_all(pieces.reshape(NEURONS, 1, LANES), TA_ROW, 0, 0, tiled=True)
    return (tile_movie[None, None], join(pieces.reshape(NEURONS, LANES)))


def solution(mesh):
    finer = Mesh(mesh.devices.reshape(4, 4, 8, mesh.shape["row"]), ("ta_0", "ta_1", "ta_2", "row"))
    return jax.shard_map(
        local,
        mesh=finer,
        in_specs=(
            P("row", TA, None, None),
            P("row", TA, None, None),
            P("row", TA, None, None),
            P("row", TA, None, None),
            P("row", TA, None),
            P(),
            P(TA_ROW, None),
        ),
        out_specs=(P("row", TA, None, None), P(TA_ROW, None)),
        check_vma=False,
    )
```

time: 214 us -> 113 us (0.53)
  waiting for transfers between devices: 124 us -> 13 us
  blocking collectives: 6.56 us -> 69.2 us
  starting transfers between devices: 45.7 us -> 5.56 us
  local copies, waits for them, and re-layouts: 27.4 us -> 3 us
  Pallas kernels: 0 us -> 21.3 us
  matrix products: 6.76 us -> 0 us
    all_to_all x6 -> x1, waiting for transfers between devices: 124 us -> 13 us  [local(): lax.all_to_all(pieces.reshape(NEURONS, 1, LANES), TA_ROW, 0, 0, tiled=True)]
    all_to_all x1 -> x2, blocking collectives: 6.56 us -> 69.2 us  [the longest x1 46.7 us: local(): lax.all_to_all(tiled, TA, split_axis=0, concat_axis=0, tiled=True)]
    all_to_all x6 -> x1, starting transfers between devices: 45.7 us -> 5.56 us  [local(): lax.all_to_all(pieces.reshape(NEURONS, 1, LANES), TA_ROW, 0, 0, tiled=True)]
    pallas_call x0 -> x4, Pallas kernels: none -> 21.3 us  [the longest x1 9.27 us: solve(): pl.pallas_call(solve_kernel, out_shape=jax.ShapeDtypeStruct((NEURONS, LAN...]
    reshape x2 -> x0, local copies, waits for them, and re-layouts: 10.6 us -> none  [the longest x1 6.78 us: local(): tiled = tiled.reshape(tile_rows * tile_cols, frame_count, TH * TW)]
    dot_general x8 -> x0, matrix products: 6.76 us -> none  [the longest x1 2.07 us: local(): jnp.einsum('fpyh,fhpx->fypx', row_tables, blocks, preferred_element_type=...]
    transpose x1 -> x0, local copies, waits for them, and re-layouts: 5.33 us -> none  [local(): filtered.reshape(frame_count, tile_rows, TH, tile_cols, TW)]
    broadcast_in_dim x4 -> x0, local copies, waits for them, and re-layouts: 3.07 us -> none  [copy_for_each(): jnp.broadcast_to(array[None], (length, *array.shape))]
  transfers between devices with their start and end apart: 6 -> 1, of which waited for: 6 -> 1; matrix products, arithmetic and copies ran while one was open for 3% -> 0% of each run, Pallas kernels for 0% -> 0%
where the time goes in v1:
time: 113 us
  blocking collectives  69.2 us (61%)
  Pallas kernels  21.3 us (19%)
  waiting for transfers between devices  13 us (12%)
  starting transfers between devices  5.56 us (5%)
  local copies, waits for them, and re-layouts  3 us (3%)
    all_to_all x1, blocking collectives, local(): lax.all_to_all(tiled, TA, split_axis=0, concat_axis=0, tiled=True)  46.7 us
    all_to_all x1, blocking collectives, local(): lax.all_to_all(mail.reshape(NEURONS, 1, LANES), TA_ROW, 0, 0, tiled=True)  22.5 us
    all_to_all x1, waiting for transfers between devices, local(): lax.all_to_all(pieces.reshape(NEURONS, 1, LANES), TA_ROW, 0, 0, tiled=True)  13 us
    pallas_call x1, Pallas kernels, solve(): pl.pallas_call(solve_kernel, out_shape=jax.ShapeDtypeStruct((NEURONS, LAN...  9.27 us
    pallas_call x1, Pallas kernels, filter_tiles(): pl.pallas_call(filter_kernel, out_shape=(jax.ShapeDtypeStruct((128, FRAME...  8.06 us
    all_to_all x1, starting transfers between devices, local(): lax.all_to_all(pieces.reshape(NEURONS, 1, LANES), TA_ROW, 0, 0, tiled=True)  5.56 us
    pallas_call x1, Pallas kernels, project(): pl.pallas_call(project_kernel, out_shape=jax.ShapeDtypeStruct((NEURONS, L...  2.49 us
  transfers between devices with their start and end apart: 1, of which 1 were waited for; matrix products, arithmetic and copies ran while one was open for 0% of the time, Pallas kernels for 0%

profile of v1, /device:TPU:1, one launch (start us, length us, event | category | flops | bytes accessed | tf_op | source)
XLA Modules:
  0.0 112.8 jit_solution(4981403748501044470)
XLA Ops:
  0.6 1.4 %copy.14.shifts_ref = s32[8,4,2]{2,1,0:T(4,128)} copy(s32[8,4,2]{0,2,1:T(2,128)} %bitcast.24) | data formatting | bytes 512 | tf_op jit(solution)/shard_map/squeeze | solution.py:269
  2.0 8.1 %filter.1 = (bf16[128,8,512]{2,1,0:T(8,128)(2,1)}, f32[256,128]{1,0:T(8,128)}) custom-call(s32[8,4,2]{2,1,0:T(4,128)} %copy.14.shifts_ref, s32[1,8]{1,0:T(1,128)} %bitcast.25, s32[256]{0:T(256)} %order_ref.1, bf16[8,128,512]{2,1,0:T(8,128)(2,1)} %bitcast.17, bf16[512,512]{1,0:T(8,128)(2,1)} %constant.4.clone.wide_ref, ...), custom_call_target="tpu_custom_call" | custom-call | tf_op jit(solution)/shard_map/filter/pallas_call | solution.py:147
  10.1 46.7 %all_to_all.15 = bf16[128,8,512]{2,1,0:T(8,128)(2,1)} all-to-all(bf16[128,8,512]{2,1,0:T(8,128)(2,1)} %get-tuple-element.4), channel_id=1, replica_groups=mesh['ta_0'=4,'ta_1'=4,'ta_2'=8,'row'=2] {'ta_0','ta_1','ta_2'}, dimensions={0} | all-to-all | bytes 2097152 | tf_op jit(solution)/shard_map/all_to_all | solution.py:270
  56.8 0.0 copy-start
  56.8 2.5 %project.1 = f32[256,128]{1,0:T(8,128)} custom-call(bf16[1024,512]{1,0:T(8,128)(2,1)} %bitcast.15, bf16[8,512]{1,0:T(8,128)(2,1)} %bitcast.23, s32[8,512]{1,0:T(8,128)} %bitcast.22, f32[256,128]{1,0:T(8,128)} %get-tuple-element.5.base_ref), custom_call_target="tpu_custom_call" | custom-call | tf_op jit(solution)/shard_map/project/pallas_call | solution.py:182
  59.3 22.5 %all_to_all.16 = f32[256,1,128]{2,1,0:T(1,128)} all-to-all(f32[256,1,128]{2,1,0:T(1,128)} %bitcast.21), channel_id=1, replica_groups=mesh['ta_0'=4,'ta_1'=4,'ta_2'=8,'row'=2] {'ta_0','ta_1','ta_2','row'}, dimensions={0} | all-to-all | bytes 262144 | tf_op jit(solution)/shard_map/all_to_all | solution.py:273
  81.8 9.3 %solve.1 = f32[256,128]{1,0:T(8,128)} custom-call(f32[256,128]{1,0:T(8,128)} %bitcast.20), custom_call_target="tpu_custom_call" | custom-call | tf_op jit(solution)/shard_map/solve/pallas_call | solution.py:240
  91.1 5.6 %all-to-all-start.2 = ((f32[256,1,128]{2,1,0:T(1,128)}), f32[256,1,128]{2,1,0:T(1,128)S(1)}, u32[]{:S(2)}, u32[]{:S(2)}) async-start(f32[256,1,128]{2,1,0:T(1,128)} %bitcast.19), calls=%async_computation.2 | async-start | bytes 262144 | tf_op jit(solution)/shard_map/all_to_all | solution.py:275
  96.6 13.0 %all-to-all-done.2 = f32[256,1,128]{2,1,0:T(1,128)S(1)} async-done(((f32[256,1,128]{2,1,0:T(1,128)}), f32[256,1,128]{2,1,0:T(1,128)S(1)}, u32[]{:S(2)}, u32[]{:S(2)}) %all-to-all-start.2) | async-done | bytes 131104 | tf_op jit(solution)/shard_map/all_to_all | solution.py:275
  109.6 0.0 copy-start.1
  109.6 0.7 copy-done.1
  110.3 1.5 %join.1 = f32[1,1024]{1,0:T(1,128)} custom-call(f32[256,128]{1,0:T(8,128)} %bitcast.18), custom_call_target="tpu_custom_call" | custom-call | tf_op jit(solution)/shard_map/join/pallas_call | solution.py:259
  111.8 0.0 copy-done
  111.8 1.0 copy.20
Async XLA Ops:
  56.8 55.0 %copy-start = (bf16[128,8,512]{2,1,0:T(8,128)(2,1)S(1)}, bf16[128,8,512]{2,1,0:T(8,128)(2,1)}, u32[]{:S(2)}) copy-start(bf16[128,8,512]{2,1,0:T(8,128)(2,1)} %all_to_all.15) | copy-start | bytes 3145732
  91.1 18.6 %all-to-all-start.2 = ((f32[256,1,128]{2,1,0:T(1,128)}), f32[256,1,128]{2,1,0:T(1,128)S(1)}, u32[]{:S(2)}, u32[]{:S(2)}) async-start(f32[256,1,128]{2,1,0:T(1,128)} %bitcast.19), calls=%async_computation.2 | async-start | bytes 262144 | tf_op jit(solution)/shard_map/all_to_all | solution.py:275
  109.6 0.7 copy-start.1

commit v2 on v1

v2 whole, which is shorter than its diff:
```python
import jax
import jax.numpy as jnp
import numpy as np
from jax import lax
from jax.experimental import pallas as pl
from jax.experimental.pallas import tpu as pltpu
from jax.sharding import Mesh
from jax.sharding import PartitionSpec as P

TH = 16
TW = 32
MAXS = 8
ITERS = 2
TA = ("ta_0", "ta_1", "ta_2")
TA_ROW = ("ta_0", "ta_1", "ta_2", "row")

FRAMES = 8
H = 128
W = 512
LANES = 128
BLOCKS = W // LANES
SLOTS = 8
NEURONS = 256
TILES = 128
PIXELS = TH * TW
LINE = 8
MESSAGE = PIXELS + LANES
ID_LANE = 64
HIGHEST = lax.Precision.HIGHEST
VMEM = pl.BlockSpec(memory_space=pltpu.VMEM)
SMEM = pl.BlockSpec(memory_space=pltpu.SMEM)


def smoothing_table(length):
    places = np.arange(length, dtype=np.float32)
    spread = places[:, None] - places[None, :]
    kernel = np.exp(-spread * spread / np.float32(32.0)).astype(np.float32)
    return (kernel / np.sum(kernel, axis=0, keepdims=True, dtype=np.float32)).astype(jnp.bfloat16)


def iota(shape, dim):
    return lax.broadcasted_iota(jnp.int32, shape, dim)


def split3(value):
    high = value.astype(jnp.bfloat16)
    rest = value - high.astype(jnp.float32)
    mid = rest.astype(jnp.bfloat16)
    low = (rest - mid.astype(jnp.float32)).astype(jnp.bfloat16)
    return high, mid, low


def dot32(left, right):
    return jnp.dot(left, right, preferred_element_type=jnp.float32)


def place(value, exact):
    high, mid, low = split3(value)
    return dot32(high, exact) + (dot32(mid, exact) + dot32(low, exact))


def filter_kernel(
    shifts_ref, movie_ref, wide_ref, tall_ref, out_ref, padded_ref, registered_ref, filtered_ref,
):
    lane = iota((H, LANES), 1)
    padded_ref[:, pl.ds(0, MAXS), :] = jnp.zeros((BLOCKS, MAXS, LANES), jnp.float32)
    padded_ref[:, pl.ds(MAXS + H, MAXS), :] = jnp.zeros((BLOCKS, MAXS, LANES), jnp.float32)

    def block(f, p):
        if p < 0 or p >= BLOCKS:
            return None
        return movie_ref[f, :, p * LANES : (p + 1) * LANES].astype(jnp.float32)

    def frame(f, carry):
        for p in range(BLOCKS):
            dy = shifts_ref[f, p, 0]
            dx = shifts_ref[f, p, 1]
            amount = jnp.where(dx > 0, LANES - dx, -dx)
            source = lane + dx

            def rolled(value):
                if value is None:
                    return jnp.zeros((H, LANES), jnp.float32)
                return pltpu.roll(value, amount, 1)

            inner = jnp.where(source >= LANES, rolled(block(f, p + 1)), rolled(block(f, p)))
            moved = jnp.where(source < 0, rolled(block(f, p - 1)), inner)
            padded_ref[p, pl.ds(MAXS, H), :] = moved
            registered_ref[:, p * LANES : (p + 1) * LANES] = padded_ref[p, pl.ds(MAXS + dy, H), :]
        registered = registered_ref[...]
        wide = dot32(registered.astype(jnp.bfloat16), wide_ref[...]).astype(jnp.bfloat16)
        filtered = registered - dot32(tall_ref[...], wide)
        for p in range(BLOCKS):
            filtered_ref[p, pl.ds(f, H, stride=FRAMES), :] = filtered[:, p * LANES : (p + 1) * LANES]
        return carry

    lax.fori_loop(0, FRAMES, frame, 0)
    lanes8 = iota((FRAMES, LANES), 1)
    near = lanes8 < 2 * TW
    even = lax.rem(lanes8 // TW, 2) == 0

    def tile_row(ty, carry):
        for q in range(4):
            for p in range(BLOCKS):
                v = []
                for r in range(4):
                    at = pl.multiple_of((ty * TH + 4 * q + r) * FRAMES, FRAMES)
                    v.append(filtered_ref[p, pl.ds(at, FRAMES), :])
                a0 = jnp.where(near, v[0], pltpu.roll(v[2], 64, 1))
                a2 = jnp.where(near, pltpu.roll(v[0], 64, 1), v[2])
                a1 = jnp.where(near, v[1], pltpu.roll(v[3], 64, 1))
                a3 = jnp.where(near, pltpu.roll(v[1], 64, 1), v[3])
                tiles = (
                    jnp.where(even, a0, pltpu.roll(a1, 32, 1)),
                    jnp.where(even, pltpu.roll(a0, 96, 1), a1),
                    jnp.where(even, a2, pltpu.roll(a3, 32, 1)),
                    jnp.where(even, pltpu.roll(a2, 96, 1), a3),
                )
                for m in range(4):
                    out_ref[ty * 16 + 4 * p + m, :, q * LANES : (q + 1) * LANES] = tiles[m].astype(jnp.bfloat16)
        return carry

    lax.fori_loop(0, H // TH, tile_row, 0)


def filter_tiles(movie, shifts):
    return pl.pallas_call(
        filter_kernel,
        out_shape=jax.ShapeDtypeStruct((TILES, FRAMES, PIXELS), jnp.bfloat16),
        in_specs=[SMEM, VMEM, VMEM, VMEM],
        out_specs=VMEM,
        scratch_shapes=[
            pltpu.VMEM((BLOCKS, H + 2 * MAXS, LANES), jnp.float32),
            pltpu.VMEM((H, W), jnp.float32),
            pltpu.VMEM((BLOCKS, H * FRAMES, LANES), jnp.float32),
        ],
        cost_estimate=pl.CostEstimate(flops=4_000_000_000, bytes_accessed=3_000_000, transcendentals=0),
        name="filter",
    )(shifts, movie, smoothing_table(W), smoothing_table(H).T)


def pack_kernel(ids_ref, order_ref, footprint_ref, support_ref, start_ref, out_ref):
    footprints = footprint_ref[...] * support_ref[...].astype(jnp.bfloat16)
    parts = jnp.concatenate(split3(start_ref[...]), axis=1)
    source = iota((3 * LANES, LINE * LANES), 0)
    target = iota((3 * LANES, LINE * LANES), 1)
    part, lane = source // LANES, lax.rem(source, LANES)
    half, z, frame = lane // 64, lax.rem(lane, 64) // FRAMES, lax.rem(lane, FRAMES)
    exact = jnp.where(target == z * LANES + part * 16 + half * FRAMES + frame, 1.0, 0.0).astype(jnp.bfloat16)
    pieces = dot32(parts, exact)
    row = iota((SLOTS, LANES), 0)
    lanes8 = iota((SLOTS, LANES), 1)
    owners = jnp.zeros((SLOTS, LANES), jnp.float32)
    for i in range(SLOTS):
        owner = order_ref[ids_ref[0, i]].astype(jnp.float32)
        owners = jnp.where((row == i) & (lanes8 == ID_LANE), owner, owners)
    for z in range(LINE):
        out_ref[z, :, :PIXELS] = footprints
        out_ref[z, :, PIXELS:] = (pieces[:, z * LANES : (z + 1) * LANES] + owners).astype(jnp.bfloat16)


def pack(ids, order, footprint, support, start):
    return pl.pallas_call(
        pack_kernel,
        out_shape=jax.ShapeDtypeStruct((LINE, SLOTS, MESSAGE), jnp.bfloat16),
        in_specs=[SMEM, SMEM, VMEM, VMEM, VMEM],
        out_specs=VMEM,
        cost_estimate=pl.CostEstimate(flops=200_000_000, bytes_accessed=200_000, transcendentals=0),
        name="pack",
    )(ids, order, footprint, support, start)


def project_kernel(
    where_ref, tiled_ref, here_ref, left_ref, right_ref, far_ref, far2_ref,
    out_ref, select_ref, high_ref, mid_ref, low_ref,
):
    x, y = where_ref[0], where_ref[1]
    rows = LINE * SLOTS
    same = iota((rows, LANES), 0) // SLOTS == lax.rem(iota((rows, LANES), 1), rows) // SLOTS
    mine = 4 * x + y
    own_row = iota((LINE, SLOTS, LANES), 1) == mine // 2
    back = lax.rem(LANES - FRAMES * lax.rem(mine, 2), LANES)
    contract = (((1,), (1,)), ((), ()))
    neuron = iota((rows, NEURONS), 1)
    out_ref[:, NEURONS + LANES :] = jnp.zeros((NEURONS, LANES), jnp.float32)
    blocks = []
    for ky in range(4):
        blocks.append((here_ref, ky, 0, ky))
        blocks.append((left_ref, ky, 1, ky))
        blocks.append((right_ref, ky, 3, ky))
        blocks.append((far_ref, ky, 2, ky) if ky < 2 else (far2_ref, ky - 2, 2, ky))
    for at, (ref, index, kx, ky) in enumerate(blocks):
        message = ref[index]
        tile = pl.multiple_of(LINE * (4 * lax.rem(x + 4 - kx, 4) + lax.rem(y + 4 - ky, 4)), LINE)
        frames = tiled_ref[pl.ds(tile, LINE)].reshape(LINE * FRAMES, PIXELS)
        prints = message[:, :, :PIXELS].reshape(rows, PIXELS)
        extra = message[:, :, PIXELS:].astype(jnp.float32)
        both = jnp.concatenate([frames, prints], axis=0)
        found = lax.dot_general(prints, both, contract, preferred_element_type=jnp.float32)
        found = jnp.where(same, found, 0.0)
        ids = extra.reshape(rows, LANES)[:, ID_LANE : ID_LANE + 1].astype(jnp.int32)
        select = jnp.where(neuron == ids, 1.0, 0.0).astype(jnp.bfloat16)
        spread = place(found[:, rows:], select)
        span = pl.ds(at * rows, rows)
        select_ref[span, :] = select
        for start, value in ((0, spread), (NEURONS, found)):
            end = start + value.shape[1]
            high, mid, low = split3(value)
            high_ref[span, start:end] = high
            mid_ref[span, start:end] = mid
            low_ref[span, start:end] = low
        piece = jnp.sum(jnp.where(own_row, extra, 0.0), axis=1)
        piece = pltpu.roll(piece, back, 1)
        piece = piece + (pltpu.roll(piece, LANES - 16, 1) + pltpu.roll(piece, LANES - 32, 1))
        out_ref[pl.ds(tile, LINE), NEURONS + LANES :] = piece
    select = select_ref[...]
    turn = (((0,), (0,)), ((), ()))

    def add(ref):
        return lax.dot_general(select, ref[...], turn, preferred_element_type=jnp.float32)

    out_ref[:, : NEURONS + LANES] = add(high_ref) + (add(mid_ref) + add(low_ref))


def project(where, tiled, here, left, right, far, far2):
    rows = TILES * SLOTS
    return pl.pallas_call(
        project_kernel,
        out_shape=jax.ShapeDtypeStruct((NEURONS, NEURONS + 2 * LANES), jnp.float32),
        in_specs=[SMEM] + [VMEM] * 6,
        out_specs=VMEM,
        scratch_shapes=[pltpu.VMEM((rows, NEURONS), jnp.bfloat16)]
        + [pltpu.VMEM((rows, NEURONS + LANES), jnp.bfloat16)] * 3,
        cost_estimate=pl.CostEstimate(flops=2_000_000_000, bytes_accessed=3_000_000, transcendentals=0),
        name="project",
    )(where, tiled, here, left, right, far, far2)


def solve_kernel(where_ref, mine_ref, other_ref, out_ref, current_ref):
    core = where_ref[2]
    sums = mine_ref[:, : NEURONS + LANES] + other_ref[:, : NEURONS + LANES]
    coupling = sums[:, :NEURONS]
    source = iota((LANES, LANES), 0)
    target = lax.rem(iota((LANES, LANES), 1), FRAMES)
    fold = jnp.where((lax.rem(source, FRAMES) == target) & (source < LINE * FRAMES), 1.0, 0.0)
    drive = place(sums[:, NEURONS:], fold.astype(jnp.bfloat16))
    copy = jnp.where(source == target, 1.0, 0.0).astype(jnp.bfloat16)
    here = mine_ref[:TILES, NEURONS + LANES :]
    there = other_ref[:TILES, NEURONS + LANES :]
    current_ref[pl.ds(0, TILES, stride=2), :] = place(jnp.where(core == 0, here, there), copy)
    current_ref[pl.ds(1, TILES, stride=2), :] = place(jnp.where(core == 0, there, here), copy)
    current = current_ref[...]
    bound = 1.0 + jnp.sum(coupling, axis=1, keepdims=True)
    for _ in range(ITERS):
        product = jnp.dot(coupling, current, preferred_element_type=jnp.float32, precision=HIGHEST)
        current = jnp.maximum(current - (product - drive) / bound, 0.0)
    current_ref[...] = current
    even = current_ref[pl.ds(0, TILES, stride=2), :]
    odd = current_ref[pl.ds(1, TILES, stride=2), :]
    out_ref[...] = jnp.where(core == 0, even, odd)


def solve(where, mine, other):
    return pl.pallas_call(
        solve_kernel,
        out_shape=jax.ShapeDtypeStruct((TILES, LANES), jnp.float32),
        in_specs=[SMEM, VMEM, VMEM],
        out_specs=VMEM,
        scratch_shapes=[pltpu.VMEM((NEURONS, LANES), jnp.float32)],
        cost_estimate=pl.CostEstimate(flops=2_000_000_000, bytes_accessed=1_000_000, transcendentals=0),
        name="solve",
    )(where, mine, other)


def join_kernel(pieces_ref, out_ref):
    near = LANES // FRAMES
    inside = iota((near, LANES), 1) // FRAMES == iota((near, LANES), 0)
    for b in range(TILES // near):
        piece = jnp.where(inside, pieces_ref[pl.ds(b * near, near), :], 0.0)
        out_ref[:, b * LANES : (b + 1) * LANES] = jnp.sum(piece, axis=0, keepdims=True)


def join(pieces):
    return pl.pallas_call(
        join_kernel,
        out_shape=jax.ShapeDtypeStruct((1, TILES * FRAMES), jnp.float32),
        in_specs=[VMEM],
        out_specs=VMEM,
        name="join",
    )(pieces)


def moved(array, axis, by):
    count = lax.axis_size(axis)
    return lax.ppermute(array, axis, [(i, (i + by) % count) for i in range(count)])


def local(movie, shifts, footprint, support, neuron_ids, owner_order, start_traces):
    where = jnp.stack([lax.axis_index(axis) for axis in ("ta_0", "ta_1", "row")]).astype(jnp.int32)
    packed = pack(neuron_ids[0], owner_order, footprint[0, 0], support[0, 0], start_traces.reshape(8, LANES))
    line = lax.all_to_all(packed, "ta_2", 0, 0, tiled=True)
    tiled = filter_tiles(movie[0], shifts[0])
    tile_movie = lax.all_to_all(tiled, TA, split_axis=0, concat_axis=0, tiled=True)
    here = jnp.stack([line] + [moved(line, "ta_1", by) for by in range(1, 4)])
    left = moved(here, "ta_0", 1)
    right = moved(here, "ta_0", 3)
    far = moved(left[:2], "ta_0", 1)
    far2 = moved(right[2:], "ta_0", 3)
    mine = project(where, tiled, here, left, right, far, far2)
    other = moved(mine, "row", 1)
    pieces = solve(where, mine, other)
    pieces = lax.all_to_all(pieces.reshape(TILES, 1, LANES), TA, 0, 0, tiled=True)
    traces = join(pieces.reshape(TILES, LANES))
    return (tile_movie.reshape(1, 1, -1, PIXELS), traces)


def solution(mesh):
    finer = Mesh(mesh.devices.reshape(4, 4, 8, mesh.shape["row"]), TA_ROW)
    return jax.shard_map(
        local,
        mesh=finer,
        in_specs=(
            P("row", TA, None, None),
            P("row", TA, None, None),
            P("row", TA, None, None),
            P("row", TA, None, None),
            P("row", TA, None),
            P(),
            P(TA_ROW, None),
        ),
        out_specs=(P("row", TA, None, None), P(TA_ROW, None)),
        check_vma=False,
    )
```

time: 113 us -> 122 us (1.080)
  blocking collectives: 69.2 us -> 34.8 us
  waiting for transfers between devices: 13 us -> 37.3 us
  starting transfers between devices: 5.56 us -> 20.9 us
    all_to_all x2, blocking collectives: 69.2 us -> 34.8 us  [the longest x1 18.3 us: local(): lax.all_to_all(pieces.reshape(TILES, 1, LANES), TA, 0, 0, tiled=True)]
    ppermute x0 -> x8, starting transfers between devices: none -> 14.7 us  [moved(): lax.ppermute(array, axis, [(i, (i + by) % count) for i in range(count)])]
    all_to_all x1, waiting for transfers between devices: 13 us -> 27.6 us  [local(): lax.all_to_all(tiled, TA, split_axis=0, concat_axis=0, tiled=True)]
    ppermute x0 -> x8, waiting for transfers between devices: none -> 9.71 us  [moved(): lax.ppermute(array, axis, [(i, (i + by) % count) for i in range(count)])]
    unnamed x5 -> x15, local copies, waits for them, and re-layouts: 1.63 us -> 3.1 us
    pallas_call x4 -> x5, Pallas kernels: 21.3 us -> 22.3 us  [the longest x1 8.02 us: filter_tiles(): pl.pallas_call(filter_kernel, out_shape=jax.ShapeDtypeStruct((TILES, FRAM...]
  transfers between devices with their start and end apart: 1 -> 9, of which waited for: 1 -> 6; matrix products, arithmetic and copies ran while one was open for 0% -> 1% of each run, Pallas kernels for 0% -> 8%
where the time goes in v2:
time: 122 us; the launch traced here: 121 us
  waiting for transfers between devices  37.3 us (31%)
  blocking collectives  34.8 us (29%)
  Pallas kernels  22.3 us (18%)
  starting transfers between devices  20.9 us (17%)
  local copies, waits for them, and re-layouts  3.82 us (3%)
    all_to_all x1, waiting for transfers between devices, local(): lax.all_to_all(tiled, TA, split_axis=0, concat_axis=0, tiled=True)  27.6 us
    all_to_all x1, blocking collectives, local(): lax.all_to_all(pieces.reshape(TILES, 1, LANES), TA, 0, 0, tiled=True)  18.3 us
    all_to_all x1, blocking collectives, local(): line = lax.all_to_all(packed, 'ta_2', 0, 0, tiled=True)  16.5 us
    ppermute x8, starting transfers between devices, moved(): lax.ppermute(array, axis, [(i, (i + by) % count) for i in range(count)])  14.7 us
    ppermute x8, waiting for transfers between devices, moved(): lax.ppermute(array, axis, [(i, (i + by) % count) for i in range(count)])  9.71 us
    pallas_call x1, Pallas kernels, filter_tiles(): pl.pallas_call(filter_kernel, out_shape=jax.ShapeDtypeStruct((TILES, FRAM...  8.02 us
    pallas_call x1, Pallas kernels, project(): pl.pallas_call(project_kernel, out_shape=jax.ShapeDtypeStruct((NEURONS, N...  7.91 us
    all_to_all x1, starting transfers between devices, local(): lax.all_to_all(tiled, TA, split_axis=0, concat_axis=0, tiled=True)  6.19 us
  transfers between devices with their start and end apart: 9, of which 6 were waited for; matrix products, arithmetic and copies ran while one was open for 1% of the time, Pallas kernels for 8%

profile of v2, /device:TPU:1, one launch (start us, length us, event | category | flops | bytes accessed | tf_op | source)
XLA Modules:
  0.0 120.6 jit_solution(16662998117424950401)
XLA Ops:
  0.6 1.8 %pack.1 = bf16[8,8,640]{2,1,0:T(8,128)(2,1)} custom-call(s32[1,8]{1,0:T(1,128)} %bitcast.30, s32[256]{0:T(256)} %order_ref.1, bf16[8,512]{1,0:T(8,128)(2,1)} %bitcast.28, s32[8,512]{1,0:T(8,128)} %bitcast.27, f32[8,128]{1,0:T(8,128)} %bitcast.29), custom_call_target="tpu_custom_call" | custom-call | flops 200000000 | bytes 200000 | tf_op jit(solution)/shard_map/pack/pallas_call | solution.py:163
  2.4 16.5 %all_to_all.15 = bf16[8,8,640]{2,1,0:T(8,128)(2,1)S(1)} all-to-all(bf16[8,8,640]{2,1,0:T(8,128)(2,1)} %pack.1), channel_id=1, replica_groups=mesh['ta_0'=4,'ta_1'=4,'ta_2'=8,'row'=2] {'ta_2'}, dimensions={0} | all-to-all | bytes 163840 | tf_op jit(solution)/shard_map/all_to_all | solution.py:301
  18.9 2.7 %collective-permute-start.2 = (bf16[8,8,640]{2,1,0:T(8,128)(2,1)S(1)}, bf16[8,8,640]{2,1,0:T(8,128)(2,1)S(1)}, u32[]{:S(2)}, u32[]{:S(2)}) collective-permute-start(bf16[8,8,640]{2,1,0:T(8,128)(2,1)S(1)} %all_to_all.15), channel_id=1, source_target_pairs={{0,48},{16,0},{32,16},{48,32},{1,49},{17,1},{33,17},{49,33},{2,50}... | collective-permute-start | bytes 245768 | tf_op jit(solution)/shard_map/ppermute | solution.py:295
  22.0 0.7 collective-permute-start
  23.1 3.4 %collective-permute-done.1 = bf16[8,8,640]{2,1,0:T(8,128)(2,1)S(1)} collective-permute-done((bf16[8,8,640]{2,1,0:T(8,128)(2,1)S(1)}, bf16[8,8,640]{2,1,0:T(8,128)(2,1)S(1)}, u32[]{:S(2)}, u32[]{:S(2)}) %collective-permute-start.1) | collective-permute-done | bytes 81952 | tf_op jit(solution)/shard_map/ppermute | solution.py:295
  26.5 0.8 collective-permute-done
  27.4 2.6 %collective-permute-start.4 = (bf16[4,8,8,640]{3,2,1,0:T(8,128)(2,1)S(1)}, bf16[4,8,8,640]{3,2,1,0:T(8,128)(2,1)S(1)}, u32[]{:S(2)}, u32[]{:S(2)}) collective-permute-start(bf16[4,8,8,640]{3,2,1,0:T(8,128)(2,1)S(1)} %pad_maximum_fusion.here_ref), channel_id=1, source_target_pairs={{0,192},{64,0},{128,64},{192,128},{1,193},{65,1},{129,65},{193,129... | collective-permute-start | bytes 983048 | tf_op jit(solution)/shard_map/ppermute | solution.py:295
  30.0 0.7 copy.14.shifts_ref
  30.7 3.3 %collective-permute-done.4.right_ref = bf16[4,8,8,640]{3,2,1,0:T(8,128)(2,1)S(1)} collective-permute-done((bf16[4,8,8,640]{3,2,1,0:T(8,128)(2,1)S(1)}, bf16[4,8,8,640]{3,2,1,0:T(8,128)(2,1)S(1)}, u32[]{:S(2)}, u32[]{:S(2)}) %collective-permute-start.4) | collective-permute-done | bytes 327712 | tf_op jit(solution)/shard_map/ppermute | solution.py:295
  34.0 3.2 %collective-permute-start.6 = (bf16[2,8,8,640]{3,2,1,0:T(8,128)(2,1)S(1)}, bf16[2,8,8,640]{3,2,1,0:T(8,128)(2,1)S(1)}, u32[]{:S(2)}, u32[]{:S(2)}) collective-permute-start(bf16[2,8,8,640]{3,2,1,0:T(8,128)(2,1)S(1)} %slice.9), channel_id=1, source_target_pairs={{0,192},{64,0},{128,64},{192,128},{1,193},{65,1},{129,65},{193,129... | collective-permute-start | bytes 491528 | tf_op jit(solution)/shard_map/ppermute | solution.py:295
  37.3 8.0 %filter.1.tiled_ref = bf16[128,8,512]{2,1,0:T(8,128)(2,1)} custom-call(s32[8,4,2]{2,1,0:T(4,128)} %copy.14.shifts_ref, bf16[8,128,512]{2,1,0:T(8,128)(2,1)} %bitcast.26, bf16[512,512]{1,0:T(8,128)(2,1)} %constant.18.clone.wide_ref, bf16[128,128]{1,0:T(8,128)(2,1)} %constant.19.clone.tall_ref), custom_call_target="tpu_custom_call" | custom-call | flops 4000000000 | bytes 3000000 | tf_op jit(solution)/shard_map/filter/pallas_call | solution.py:127
  45.3 0.6 pad_add_fusion.where_ref
  46.0 0.7 copy-done.5
  46.6 0.7 copy-done.6
  47.3 7.9 %project.1.mine_ref = f32[256,512]{1,0:T(8,128)} custom-call(s32[3]{0:T(128)} %pad_add_fusion.where_ref, bf16[128,8,512]{2,1,0:T(8,128)(2,1)} %filter.1.tiled_ref, bf16[4,8,8,640]{3,2,1,0:T(8,128)(2,1)} %copy-done, bf16[4,8,8,640]{3,2,1,0:T(8,128)(2,1)} %copy-done.2, bf16[4,8,8,640]{3,2,1,0:T(8,128)(2,1)} %copy-done.1, bf16[2,8,8,640]{3,2,1,0:T(8,128)(2,1)} %copy-done.6, ...), custom_call_target="tpu_custom_call" | custom-call | flops 2000000000 | bytes 3000000 | tf_op jit(solution)/shard_map/project/pallas_call | solution.py:227
  55.2 5.1 %collective-permute-start.7 = (f32[256,512]{1,0:T(8,128)}, f32[256,512]{1,0:T(8,128)S(1)}, u32[]{:S(2)}, u32[]{:S(2)}) collective-permute-start(f32[256,512]{1,0:T(8,128)} %project.1.mine_ref), channel_id=1, source_target_pairs={{0,1},{1,0},{2,3},{3,2},{4,5},{5,4},{6,7},{7,6},{8,9},{9,8},{10,11... | collective-permute-start | bytes 1572872 | tf_op jit(solution)/shard_map/ppermute | solution.py:295
  60.3 1.7 %collective-permute-done.7.other_ref = f32[256,512]{1,0:T(8,128)S(1)} collective-permute-done((f32[256,512]{1,0:T(8,128)}, f32[256,512]{1,0:T(8,128)S(1)}, u32[]{:S(2)}, u32[]{:S(2)}) %collective-permute-start.7) | collective-permute-done | bytes 524320 | tf_op jit(solution)/shard_map/ppermute | solution.py:295
  62.1 0.8 copy-done.4
  62.9 3.2 %solve.1 = f32[128,128]{1,0:T(8,128)} custom-call(s32[3]{0:T(128)} %pad_add_fusion.where_ref, f32[256,512]{1,0:T(8,128)} %project.1.mine_ref, f32[256,512]{1,0:T(8,128)} %copy-done.4), custom_call_target="tpu_custom_call" | custom-call | flops 2000000000 | bytes 1000000 | tf_op jit(solution)/shard_map/solve/pallas_call | solution.py:264
  66.0 18.3 %all_to_all.16 = f32[128,1,128]{2,1,0:T(1,128)} all-to-all(f32[128,1,128]{2,1,0:T(1,128)} %bitcast.24), channel_id=1, replica_groups=mesh['ta_0'=4,'ta_1'=4,'ta_2'=8,'row'=2] {'ta_0','ta_1','ta_2'}, dimensions={0} | all-to-all | bytes 131072 | tf_op jit(solution)/shard_map/all_to_all | solution.py:312
  84.4 6.2 %all-to-all-start = ((bf16[128,8,512]{2,1,0:T(8,128)(2,1)}), bf16[128,8,512]{2,1,0:T(8,128)(2,1)S(1)}, u32[]{:S(2)}, u32[]{:S(2)}) async-start(bf16[128,8,512]{2,1,0:T(8,128)(2,1)} %filter.1.tiled_ref), calls=%async_computation | async-start | bytes 2097152 | tf_op jit(solution)/shard_map/all_to_all | solution.py:303
  90.6 1.5 %join.1 = f32[1,1024]{1,0:T(1,128)} custom-call(f32[128,128]{1,0:T(8,128)} %bitcast.20), custom_call_target="tpu_custom_call" | custom-call | tf_op jit(solution)/shard_map/join/pallas_call | solution.py:284
  92.0 27.6 %all-to-all-done = bf16[128,8,512]{2,1,0:T(8,128)(2,1)S(1)} async-done(((bf16[128,8,512]{2,1,0:T(8,128)(2,1)}), bf16[128,8,512]{2,1,0:T(8,128)(2,1)S(1)}, u32[]{:S(2)}, u32[]{:S(2)}) %all-to-all-start) | async-done | bytes 1048608 | tf_op jit(solution)/shard_map/all_to_all | solution.py:303
  119.6 1.0 copy.19
  (21 shorter events, 1.0 us)
Async XLA Ops:
  18.9 4.2 %collective-permute-start.2 = (bf16[8,8,640]{2,1,0:T(8,128)(2,1)S(1)}, bf16[8,8,640]{2,1,0:T(8,128)(2,1)S(1)}, u32[]{:S(2)}, u32[]{:S(2)}) collective-permute-start(bf16[8,8,640]{2,1,0:T(8,128)(2,1)S(1)} %all_to_all.15), channel_id=1, source_target_pairs={{0,48},{16,0},{32,16},{48,32},{1,49},{17,1},{33,17},{49,33},{2,50}... | collective-permute-start | bytes 245768 | tf_op jit(solution)/shard_map/ppermute | solution.py:295
  21.7 4.9 %collective-permute-start.1 = (bf16[8,8,640]{2,1,0:T(8,128)(2,1)S(1)}, bf16[8,8,640]{2,1,0:T(8,128)(2,1)S(1)}, u32[]{:S(2)}, u32[]{:S(2)}) collective-permute-start(bf16[8,8,640]{2,1,0:T(8,128)(2,1)S(1)} %all_to_all.15), channel_id=1, source_target_pairs={{0,32},{16,48},{32,0},{48,16},{1,33},{17,49},{33,1},{49,17},{2,34}... | collective-permute-start | bytes 245768 | tf_op jit(solution)/shard_map/ppermute | solution.py:295
  22.0 5.3 %collective-permute-start = (bf16[8,8,640]{2,1,0:T(8,128)(2,1)S(1)}, bf16[8,8,640]{2,1,0:T(8,128)(2,1)S(1)}, u32[]{:S(2)}, u32[]{:S(2)}) collective-permute-start(bf16[8,8,640]{2,1,0:T(8,128)(2,1)S(1)} %all_to_all.15), channel_id=1, source_target_pairs={{0,16},{16,32},{32,48},{48,0},{1,17},{17,33},{33,49},{49,1},{2,18}... | collective-permute-start | bytes 245768 | tf_op jit(solution)/shard_map/ppermute | solution.py:295
  27.3 2.6 %copy-start.3 = (s32[1,8,4,2]{1,3,2,0:T(2,128)S(1)}, s32[1,8,4,2]{1,3,2,0:T(2,128)}, u32[]{:S(2)}) copy-start(s32[1,8,4,2]{1,3,2,0:T(2,128)} %param.10) | copy-start | bytes 772
  27.4 9.8 %copy-start = (bf16[4,8,8,640]{3,2,1,0:T(8,128)(2,1)}, bf16[4,8,8,640]{3,2,1,0:T(8,128)(2,1)S(1)}, u32[]{:S(2)}) copy-start(bf16[4,8,8,640]{3,2,1,0:T(8,128)(2,1)S(1)} %pad_maximum_fusion.here_ref) | copy-start | bytes 983044
  27.4 6.6 %collective-permute-start.4 = (bf16[4,8,8,640]{3,2,1,0:T(8,128)(2,1)S(1)}, bf16[4,8,8,640]{3,2,1,0:T(8,128)(2,1)S(1)}, u32[]{:S(2)}, u32[]{:S(2)}) collective-permute-start(bf16[4,8,8,640]{3,2,1,0:T(8,128)(2,1)S(1)} %pad_maximum_fusion.here_ref), channel_id=1, source_target_pairs={{0,192},{64,0},{128,64},{192,128},{1,193},{65,1},{129,65},{193,129... | collective-permute-start | bytes 983048 | tf_op jit(solution)/shard_map/ppermute | solution.py:295
  30.0 7.2 %collective-permute-start.3 = (bf16[4,8,8,640]{3,2,1,0:T(8,128)(2,1)S(1)}, bf16[4,8,8,640]{3,2,1,0:T(8,128)(2,1)S(1)}, u32[]{:S(2)}, u32[]{:S(2)}) collective-permute-start(bf16[4,8,8,640]{3,2,1,0:T(8,128)(2,1)S(1)} %pad_maximum_fusion.here_ref), channel_id=1, source_target_pairs={{0,64},{64,128},{128,192},{192,0},{1,65},{65,129},{129,193},{193,1... | collective-permute-start | bytes 983048 | tf_op jit(solution)/shard_map/ppermute | solution.py:295
  34.0 3.3 %copy-start.1 = (bf16[4,8,8,640]{3,2,1,0:T(8,128)(2,1)}, bf16[4,8,8,640]{3,2,1,0:T(8,128)(2,1)S(1)}, u32[]{:S(2)}) copy-start(bf16[4,8,8,640]{3,2,1,0:T(8,128)(2,1)S(1)} %collective-permute-done.4.right_ref) | copy-start | bytes 983044
  34.0 12.0 %collective-permute-start.6 = (bf16[2,8,8,640]{3,2,1,0:T(8,128)(2,1)S(1)}, bf16[2,8,8,640]{3,2,1,0:T(8,128)(2,1)S(1)}, u32[]{:S(2)}, u32[]{:S(2)}) collective-permute-start(bf16[2,8,8,640]{3,2,1,0:T(8,128)(2,1)S(1)} %slice.9), channel_id=1, source_target_pairs={{0,192},{64,0},{128,64},{192,128},{1,193},{65,1},{129,65},{193,129... | collective-permute-start | bytes 491528 | tf_op jit(solution)/shard_map/ppermute | solution.py:295
  37.2 8.2 %copy-start.2 = (bf16[4,8,8,640]{3,2,1,0:T(8,128)(2,1)}, bf16[4,8,8,640]{3,2,1,0:T(8,128)(2,1)S(1)}, u32[]{:S(2)}) copy-start(bf16[4,8,8,640]{3,2,1,0:T(8,128)(2,1)S(1)} %collective-permute-done.3.left_ref) | copy-start | bytes 983044
  37.2 8.7 %collective-permute-start.5 = (bf16[2,8,8,640]{3,2,1,0:T(8,128)(2,1)S(1)}, bf16[2,8,8,640]{3,2,1,0:T(8,128)(2,1)S(1)}, u32[]{:S(2)}, u32[]{:S(2)}) collective-permute-start(bf16[2,8,8,640]{3,2,1,0:T(8,128)(2,1)S(1)} %slice.8), channel_id=1, source_target_pairs={{0,64},{64,128},{128,192},{192,0},{1,65},{65,129},{129,193},{193,1... | collective-permute-start | bytes 491528 | tf_op jit(solution)/shard_map/ppermute | solution.py:295
  46.0 0.7 copy-start.5
  46.6 0.7 copy-start.6
  55.2 6.9 %collective-permute-start.7 = (f32[256,512]{1,0:T(8,128)}, f32[256,512]{1,0:T(8,128)S(1)}, u32[]{:S(2)}, u32[]{:S(2)}) collective-permute-start(f32[256,512]{1,0:T(8,128)} %project.1.mine_ref), channel_id=1, source_target_pairs={{0,1},{1,0},{2,3},{3,2},{4,5},{5,4},{6,7},{7,6},{8,9},{9,8},{10,11... | collective-permute-start | bytes 1572872 | tf_op jit(solution)/shard_map/ppermute | solution.py:295
  62.1 0.8 copy-start.4
  84.4 35.3 %all-to-all-start = ((bf16[128,8,512]{2,1,0:T(8,128)(2,1)}), bf16[128,8,512]{2,1,0:T(8,128)(2,1)S(1)}, u32[]{:S(2)}, u32[]{:S(2)}) async-start(bf16[128,8,512]{2,1,0:T(8,128)(2,1)} %filter.1.tiled_ref), calls=%async_computation | async-start | bytes 2097152 | tf_op jit(solution)/shard_map/all_to_all | solution.py:303

commit v3 on v2

--- a/solution.py
+++ b/solution.py
@@ -135,6 +135,7 @@
             pltpu.VMEM((BLOCKS, H * FRAMES, LANES), jnp.float32),
         ],
         cost_estimate=pl.CostEstimate(flops=4_000_000_000, bytes_accessed=3_000_000, transcendentals=0),
+        compiler_params=pltpu.CompilerParams(vmem_limit_bytes=16 << 20),
         name="filter",
     )(shifts, movie, smoothing_table(W), smoothing_table(H).T)
 
@@ -166,74 +167,74 @@
         in_specs=[SMEM, SMEM, VMEM, VMEM, VMEM],
         out_specs=VMEM,
         cost_estimate=pl.CostEstimate(flops=200_000_000, bytes_accessed=200_000, transcendentals=0),
+        compiler_params=pltpu.CompilerParams(vmem_limit_bytes=4 << 20),
         name="pack",
     )(ids, order, footprint, support, start)
 
 
 def project_kernel(
-    where_ref, tiled_ref, here_ref, left_ref, right_ref, far_ref, far2_ref,
-    out_ref, select_ref, high_ref, mid_ref, low_ref,
+    where_ref, tiled_ref, here_ref, left_ref, far_ref, right_ref, out_ref, select_ref, terms_ref
 ):
     x, y = where_ref[0], where_ref[1]
-    rows = LINE * SLOTS
-    same = iota((rows, LANES), 0) // SLOTS == lax.rem(iota((rows, LANES), 1), rows) // SLOTS
+    rows = 2 * LINE * SLOTS
+    width = NEURONS + LANES
+    same = iota((rows, 2 * rows), 0) // SLOTS == lax.rem(iota((rows, 2 * rows), 1), rows) // SLOTS
     mine = 4 * x + y
-    own_row = iota((LINE, SLOTS, LANES), 1) == mine // 2
+    own_row = iota((2 * LINE, SLOTS, LANES), 1) == mine // 2
     back = lax.rem(LANES - FRAMES * lax.rem(mine, 2), LANES)
     contract = (((1,), (1,)), ((), ()))
     neuron = iota((rows, NEURONS), 1)
-    out_ref[:, NEURONS + LANES :] = jnp.zeros((NEURONS, LANES), jnp.float32)
-    blocks = []
-    for ky in range(4):
-        blocks.append((here_ref, ky, 0, ky))
-        blocks.append((left_ref, ky, 1, ky))
-        blocks.append((right_ref, ky, 3, ky))
-        blocks.append((far_ref, ky, 2, ky) if ky < 2 else (far2_ref, ky - 2, 2, ky))
-    for at, (ref, index, kx, ky) in enumerate(blocks):
-        message = ref[index]
-        tile = pl.multiple_of(LINE * (4 * lax.rem(x + 4 - kx, 4) + lax.rem(y + 4 - ky, 4)), LINE)
-        frames = tiled_ref[pl.ds(tile, LINE)].reshape(LINE * FRAMES, PIXELS)
-        prints = message[:, :, :PIXELS].reshape(rows, PIXELS)
-        extra = message[:, :, PIXELS:].astype(jnp.float32)
-        both = jnp.concatenate([frames, prints], axis=0)
-        found = lax.dot_general(prints, both, contract, preferred_element_type=jnp.float32)
+    neuron_t = iota((NEURONS, rows), 0)
+    diagonal = iota((rows, rows), 0) == iota((rows, rows), 1)
+    out_ref[:, width:] = jnp.zeros((NEURONS, LANES), jnp.float32)
+    for at in range(8):
+        kx, first = at // 2, 2 * (at % 2)
+        ref = (here_ref, left_ref, far_ref, right_ref)[kx]
+        tiles = [
+            pl.multiple_of(LINE * (4 * lax.rem(x + 4 - kx, 4) + lax.rem(y + 4 - ky, 4)), LINE)
+            for ky in (first, first + 1)
+        ]
+        message = ref[first : first + 2]
+        frames = [tiled_ref[pl.ds(tile, LINE)].reshape(rows // 2, PIXELS) for tile in tiles]
+        prints = message[:, :, :, :PIXELS].reshape(rows, PIXELS)
+        extra = message[:, :, :, PIXELS:].astype(jnp.float32).reshape(rows, LANES)
+        found = lax.dot_general(
+            prints, jnp.concatenate(frames + [prints], axis=0), contract, preferred_element_type=jnp.float32
+        )
         found = jnp.where(same, found, 0.0)
-        ids = extra.reshape(rows, LANES)[:, ID_LANE : ID_LANE + 1].astype(jnp.int32)
-        select = jnp.where(neuron == ids, 1.0, 0.0).astype(jnp.bfloat16)
+        ids = extra[:, ID_LANE : ID_LANE + 1]
+        select = jnp.where(neuron == ids.astype(jnp.int32), 1.0, 0.0).astype(jnp.bfloat16)
+        ids_row = jnp.sum(jnp.where(diagonal, ids, 0.0), axis=0, keepdims=True).astype(jnp.int32)
+        span = slice(at * rows, (at + 1) * rows)
+        select_ref[:, span] = jnp.where(neuron_t == ids_row, 1.0, 0.0).astype(jnp.bfloat16)
         spread = place(found[:, rows:], select)
-        span = pl.ds(at * rows, rows)
-        select_ref[span, :] = select
-        for start, value in ((0, spread), (NEURONS, found)):
-            end = start + value.shape[1]
-            high, mid, low = split3(value)
-            high_ref[span, start:end] = high
-            mid_ref[span, start:end] = mid
-            low_ref[span, start:end] = low
-        piece = jnp.sum(jnp.where(own_row, extra, 0.0), axis=1)
+        for k, (one, two) in enumerate(zip(split3(spread), split3(found[:, :rows]), strict=True)):
+            terms_ref[span, k * width : k * width + NEURONS] = one
+            terms_ref[span, k * width + NEURONS : (k + 1) * width] = two
+        piece = jnp.sum(jnp.where(own_row, extra.reshape(2 * LINE, SLOTS, LANES), 0.0), axis=1)
         piece = pltpu.roll(piece, back, 1)
         piece = piece + (pltpu.roll(piece, LANES - 16, 1) + pltpu.roll(piece, LANES - 32, 1))
-        out_ref[pl.ds(tile, LINE), NEURONS + LANES :] = piece
-    select = select_ref[...]
-    turn = (((0,), (0,)), ((), ()))
-
-    def add(ref):
-        return lax.dot_general(select, ref[...], turn, preferred_element_type=jnp.float32)
-
-    out_ref[:, : NEURONS + LANES] = add(high_ref) + (add(mid_ref) + add(low_ref))
-
-
-def project(where, tiled, here, left, right, far, far2):
+        for k in range(2):
+            out_ref[pl.ds(tiles[k], LINE), width:] = piece[k * LINE : (k + 1) * LINE]
+    sums = dot32(select_ref[...], terms_ref[...])
+    out_ref[:, :width] = sums[:, :width] + (sums[:, width : 2 * width] + sums[:, 2 * width :])
+
+
+def project(where, tiled, here, left, far, right):
     rows = TILES * SLOTS
     return pl.pallas_call(
         project_kernel,
         out_shape=jax.ShapeDtypeStruct((NEURONS, NEURONS + 2 * LANES), jnp.float32),
-        in_specs=[SMEM] + [VMEM] * 6,
-        out_specs=VMEM,
-        scratch_shapes=[pltpu.VMEM((rows, NEURONS), jnp.bfloat16)]
-        + [pltpu.VMEM((rows, NEURONS + LANES), jnp.bfloat16)] * 3,
+        in_specs=[SMEM] + [VMEM] * 5,
+        out_specs=VMEM,
+        scratch_shapes=[
+            pltpu.VMEM((NEURONS, rows), jnp.bfloat16),
+            pltpu.VMEM((rows, 3 * (NEURONS + LANES)), jnp.bfloat16),
+        ],
         cost_estimate=pl.CostEstimate(flops=2_000_000_000, bytes_accessed=3_000_000, transcendentals=0),
+        compiler_params=pltpu.CompilerParams(vmem_limit_bytes=16 << 20),
         name="project",
-    )(where, tiled, here, left, right, far, far2)
+    )(where, tiled, here, left, far, right)
 
 
 def solve_kernel(where_ref, mine_ref, other_ref, out_ref, current_ref):
@@ -242,7 +243,7 @@
     coupling = sums[:, :NEURONS]
     source = iota((LANES, LANES), 0)
     target = lax.rem(iota((LANES, LANES), 1), FRAMES)
-    fold = jnp.where((lax.rem(source, FRAMES) == target) & (source < LINE * FRAMES), 1.0, 0.0)
+    fold = jnp.where(lax.rem(source, FRAMES) == target, 1.0, 0.0)
     drive = place(sums[:, NEURONS:], fold.astype(jnp.bfloat16))
     copy = jnp.where(source == target, 1.0, 0.0).astype(jnp.bfloat16)
     here = mine_ref[:TILES, NEURONS + LANES :]
@@ -268,6 +269,7 @@
         out_specs=VMEM,
         scratch_shapes=[pltpu.VMEM((NEURONS, LANES), jnp.float32)],
         cost_estimate=pl.CostEstimate(flops=2_000_000_000, bytes_accessed=1_000_000, transcendentals=0),
+        compiler_params=pltpu.CompilerParams(vmem_limit_bytes=8 << 20),
         name="solve",
     )(where, mine, other)
 
@@ -286,6 +288,7 @@
         out_shape=jax.ShapeDtypeStruct((1, TILES * FRAMES), jnp.float32),
         in_specs=[VMEM],
         out_specs=VMEM,
+        compiler_params=pltpu.CompilerParams(vmem_limit_bytes=2 << 20),
         name="join",
     )(pieces)
 
@@ -302,11 +305,8 @@
     tiled = filter_tiles(movie[0], shifts[0])
     tile_movie = lax.all_to_all(tiled, TA, split_axis=0, concat_axis=0, tiled=True)
     here = jnp.stack([line] + [moved(line, "ta_1", by) for by in range(1, 4)])
-    left = moved(here, "ta_0", 1)
-    right = moved(here, "ta_0", 3)
-    far = moved(left[:2], "ta_0", 1)
-    far2 = moved(right[2:], "ta_0", 3)
-    mine = project(where, tiled, here, left, right, far, far2)
+    left, far, right = [moved(here, "ta_0", by) for by in range(1, 4)]
+    mine = project(where, tiled, here, left, far, right)
     other = moved(mine, "row", 1)
     pieces = solve(where, mine, other)
     pieces = lax.all_to_all(pieces.reshape(TILES, 1, LANES), TA, 0, 0, tiled=True)

time: 122 us -> 114 us (0.934)
  blocking collectives: 34.8 us -> 16.1 us
  waiting for transfers between devices: 37.3 us -> 50.3 us
  Pallas kernels: 22.3 us -> 16.1 us
  starting transfers between devices: 20.9 us -> 24.2 us
  local copies, waits for them, and re-layouts: 3.82 us -> 5.28 us
    all_to_all x1 -> x0, blocking collectives: 16.5 us -> none  [local(): line = lax.all_to_all(packed, 'ta_2', 0, 0, tiled=True)]
    all_to_all x0 -> x1, starting transfers between devices: none -> 9.13 us  [local(): line = lax.all_to_all(packed, 'ta_2', 0, 0, tiled=True)]
    all_to_all x0 -> x1, waiting for transfers between devices: none -> 6.72 us  [local(): line = lax.all_to_all(packed, 'ta_2', 0, 0, tiled=True)]
    ppermute x8 -> x7, starting transfers between devices: 14.7 us -> 8.86 us  [moved(): lax.ppermute(array, axis, [(i, (i + by) % count) for i in range(count)])]
    ppermute x8 -> x7, waiting for transfers between devices: 9.71 us -> 14.9 us  [moved(): lax.ppermute(array, axis, [(i, (i + by) % count) for i in range(count)])]
    pallas_call x1, Pallas kernels: 7.91 us -> 4.69 us  [project(): pl.pallas_call(project_kernel, out_shape=jax.ShapeDtypeStruct((NEURONS, N...]
    all_to_all x1, blocking collectives: 18.3 us -> 16.1 us  [local(): lax.all_to_all(pieces.reshape(TILES, 1, LANES), TA, 0, 0, tiled=True)]
    unnamed x15 -> x17, local copies, waits for them, and re-layouts: 3.1 us -> 4.5 us
  transfers between devices with their start and end apart: 9 -> 9, of which waited for: 6 -> 7; matrix products, arithmetic and copies ran while one was open for 1% -> 1% of each run, Pallas kernels for 8% -> 7%
where the time goes in v3:
time: 114 us; the launch traced here: 113 us
  waiting for transfers between devices  50.3 us (44%)
  starting transfers between devices  24.2 us (21%)
  Pallas kernels  16.1 us (14%)
  blocking collectives  16.1 us (14%)
  local copies, waits for them, and re-layouts  5.28 us (5%)
    all_to_all x1, waiting for transfers between devices, local(): lax.all_to_all(tiled, TA, split_axis=0, concat_axis=0, tiled=True)  28.7 us
    all_to_all x1, blocking collectives, local(): lax.all_to_all(pieces.reshape(TILES, 1, LANES), TA, 0, 0, tiled=True)  16.1 us
    ppermute x7, waiting for transfers between devices, moved(): lax.ppermute(array, axis, [(i, (i + by) % count) for i in range(count)])  14.9 us
    all_to_all x1, starting transfers between devices, local(): line = lax.all_to_all(packed, 'ta_2', 0, 0, tiled=True)  9.13 us
    ppermute x7, starting transfers between devices, moved(): lax.ppermute(array, axis, [(i, (i + by) % count) for i in range(count)])  8.86 us
    pallas_call x1, Pallas kernels, filter_tiles(): pl.pallas_call(filter_kernel, out_shape=jax.ShapeDtypeStruct((TILES, FRAM...  7.41 us
    all_to_all x1, waiting for transfers between devices, local(): line = lax.all_to_all(packed, 'ta_2', 0, 0, tiled=True)  6.72 us
    all_to_all x1, starting transfers between devices, local(): lax.all_to_all(tiled, TA, split_axis=0, concat_axis=0, tiled=True)  6.19 us
  transfers between devices with their start and end apart: 9, of which 7 were waited for; matrix products, arithmetic and copies ran while one was open for 1% of the time, Pallas kernels for 7%

profile of v3, /device:TPU:1, one launch (start us, length us, event | category | flops | bytes accessed | tf_op | source)
XLA Modules:
  0.0 112.9 jit_solution(4057369714645351756)
XLA Ops:
  0.7 0.8 copy-done.1
  1.4 0.7 copy-done.2
  2.1 0.7 copy-done.3
  2.8 0.7 copy-done.4
  3.5 0.7 copy-done.5
  4.2 1.5 %pack.1 = bf16[8,8,640]{2,1,0:T(8,128)(2,1)} custom-call(s32[1,8]{1,0:T(1,128)S(1)} %bitcast.24, s32[256]{0:T(256)S(1)} %copy-done.4, bf16[8,512]{1,0:T(8,128)(2,1)S(1)} %bitcast.22, s32[8,512]{1,0:T(8,128)S(1)} %bitcast.21, f32[8,128]{1,0:T(8,128)S(1)} %bitcast.23), custom_call_target="tpu_custom_call" | custom-call | flops 200000000 | bytes 200000 | tf_op jit(solution)/shard_map/pack/pallas_call | solution.py:164
  5.7 9.1 %all-to-all-start.1 = ((bf16[8,8,640]{2,1,0:T(8,128)(2,1)}), bf16[8,8,640]{2,1,0:T(8,128)(2,1)S(1)}, u32[]{:S(2)}, u32[]{:S(2)}) async-start(bf16[8,8,640]{2,1,0:T(8,128)(2,1)} %pack.1), calls=%async_computation.1 | async-start | bytes 163840 | tf_op jit(solution)/shard_map/all_to_all | solution.py:304
  14.8 0.8 copy.14.shifts_ref
  15.6 6.7 %all-to-all-done.1 = bf16[8,8,640]{2,1,0:T(8,128)(2,1)S(1)} async-done(((bf16[8,8,640]{2,1,0:T(8,128)(2,1)}), bf16[8,8,640]{2,1,0:T(8,128)(2,1)S(1)}, u32[]{:S(2)}, u32[]{:S(2)}) %all-to-all-start.1) | async-done | bytes 81952 | tf_op jit(solution)/shard_map/all_to_all | solution.py:304
  22.3 2.7 %collective-permute-start.2 = (bf16[8,8,640]{2,1,0:T(8,128)(2,1)S(1)}, bf16[8,8,640]{2,1,0:T(8,128)(2,1)S(1)}, u32[]{:S(2)}, u32[]{:S(2)}) collective-permute-start(bf16[8,8,640]{2,1,0:T(8,128)(2,1)S(1)} %all-to-all-done.1), channel_id=1, source_target_pairs={{0,48},{16,0},{32,16},{48,32},{1,49},{17,1},{33,17},{49,33},{2,50}... | collective-permute-start | bytes 245768 | tf_op jit(solution)/shard_map/ppermute | solution.py:298
  25.4 0.7 collective-permute-start
  26.5 3.4 %collective-permute-done.1 = bf16[8,8,640]{2,1,0:T(8,128)(2,1)S(1)} collective-permute-done((bf16[8,8,640]{2,1,0:T(8,128)(2,1)S(1)}, bf16[8,8,640]{2,1,0:T(8,128)(2,1)S(1)}, u32[]{:S(2)}, u32[]{:S(2)}) %collective-permute-start.1) | collective-permute-done | bytes 81952 | tf_op jit(solution)/shard_map/ppermute | solution.py:298
  29.9 0.8 collective-permute-done
  30.8 2.6 %collective-permute-start.5 = (bf16[4,8,8,640]{3,2,1,0:T(8,128)(2,1)S(1)}, bf16[4,8,8,640]{3,2,1,0:T(8,128)(2,1)S(1)}, u32[]{:S(2)}, u32[]{:S(2)}) collective-permute-start(bf16[4,8,8,640]{3,2,1,0:T(8,128)(2,1)S(1)} %pad_maximum_fusion.here_ref), channel_id=1, source_target_pairs={{0,192},{64,0},{128,64},{192,128},{1,193},{65,1},{129,65},{193,129... | collective-permute-start | bytes 983048 | tf_op jit(solution)/shard_map/ppermute | solution.py:298
  34.5 7.4 %filter.1.tiled_ref = bf16[128,8,512]{2,1,0:T(8,128)(2,1)} custom-call(s32[8,4,2]{2,1,0:T(4,128)S(1)} %copy.14.shifts_ref, bf16[8,128,512]{2,1,0:T(8,128)(2,1)S(1)} %bitcast.20, bf16[512,512]{1,0:T(8,128)(2,1)S(1)} %copy-done.6, bf16[128,128]{1,0:T(8,128)(2,1)S(1)} %copy-done.7), custom_call_target="tpu_custom_call" | custom-call | flops 4000000000 | bytes 3000000 | tf_op jit(solution)/shard_map/filter/pallas_call | solution.py:127
  41.9 8.8 %collective-permute-done.3.left_ref = bf16[4,8,8,640]{3,2,1,0:T(8,128)(2,1)S(1)} collective-permute-done((bf16[4,8,8,640]{3,2,1,0:T(8,128)(2,1)S(1)}, bf16[4,8,8,640]{3,2,1,0:T(8,128)(2,1)S(1)}, u32[]{:S(2)}, u32[]{:S(2)}) %collective-permute-start.3) | collective-permute-done | bytes 327712 | tf_op jit(solution)/shard_map/ppermute | solution.py:298
  50.7 4.7 %project.1.mine_ref = f32[256,512]{1,0:T(8,128)S(1)} custom-call(s32[3]{0:T(128)S(1)} %pad_add_fusion.where_ref, bf16[128,8,512]{2,1,0:T(8,128)(2,1)} %filter.1.tiled_ref, bf16[4,8,8,640]{3,2,1,0:T(8,128)(2,1)S(1)} %pad_maximum_fusion.here_ref, bf16[4,8,8,640]{3,2,1,0:T(8,128)(2,1)S(1)} %collective-permute-done.3.left_ref, ...), custom_call_target="tpu_custom_call" | custom-call | flops 2000000000 | bytes 3000000 | tf_op jit(solution)/shard_map/project/pallas_call | solution.py:225
  55.4 1.4 %collective-permute-start.6 = (f32[256,512]{1,0:T(8,128)S(1)}, f32[256,512]{1,0:T(8,128)S(1)}, u32[]{:S(2)}, u32[]{:S(2)}) collective-permute-start(f32[256,512]{1,0:T(8,128)S(1)} %project.1.mine_ref), channel_id=1, source_target_pairs={{0,1},{1,0},{2,3},{3,2},{4,5},{5,4},{6,7},{7,6},{8,9},{9,8},{10,11... | collective-permute-start | bytes 1572872 | tf_op jit(solution)/shard_map/ppermute | solution.py:298
  56.8 1.5 %collective-permute-done.6.other_ref = f32[256,512]{1,0:T(8,128)S(1)} collective-permute-done((f32[256,512]{1,0:T(8,128)S(1)}, f32[256,512]{1,0:T(8,128)S(1)}, u32[]{:S(2)}, u32[]{:S(2)}) %collective-permute-start.6) | collective-permute-done | bytes 524320 | tf_op jit(solution)/shard_map/ppermute | solution.py:298
  58.3 1.9 %solve.1 = f32[128,128]{1,0:T(8,128)S(1)} custom-call(s32[3]{0:T(128)S(1)} %pad_add_fusion.where_ref, f32[256,512]{1,0:T(8,128)S(1)} %project.1.mine_ref, f32[256,512]{1,0:T(8,128)S(1)} %collective-permute-done.6.other_ref), custom_call_target="tpu_custom_call" | custom-call | flops 2000000000 | bytes 1000000 | tf_op jit(solution)/shard_map/solve/pallas_call | solution.py:265
  60.2 16.1 %all_to_all.15 = f32[128,1,128]{2,1,0:T(1,128)S(1)} all-to-all(f32[128,1,128]{2,1,0:T(1,128)S(1)} %bitcast.19), channel_id=1, replica_groups=mesh['ta_0'=4,'ta_1'=4,'ta_2'=8,'row'=2] {'ta_0','ta_1','ta_2'}, dimensions={0} | all-to-all | bytes 131072 | tf_op jit(solution)/shard_map/all_to_all | solution.py:312
  76.3 6.2 %all-to-all-start = ((bf16[128,8,512]{2,1,0:T(8,128)(2,1)}), bf16[128,8,512]{2,1,0:T(8,128)(2,1)S(1)}, u32[]{:S(2)}, u32[]{:S(2)}) async-start(bf16[128,8,512]{2,1,0:T(8,128)(2,1)} %filter.1.tiled_ref), calls=%async_computation | async-start | bytes 2097152 | tf_op jit(solution)/shard_map/all_to_all | solution.py:306
  83.2 28.7 %all-to-all-done = bf16[128,8,512]{2,1,0:T(8,128)(2,1)S(1)} async-done(((bf16[128,8,512]{2,1,0:T(8,128)(2,1)}), bf16[128,8,512]{2,1,0:T(8,128)(2,1)S(1)}, u32[]{:S(2)}, u32[]{:S(2)}) %all-to-all-start) | async-done | bytes 1048608 | tf_op jit(solution)/shard_map/all_to_all | solution.py:306
  111.9 1.0 copy.19
  (20 shorter events, 2.6 us)
Async XLA Ops:
  0.6 33.8 %copy-start = (bf16[1,8,128,512]{3,2,1,0:T(8,128)(2,1)S(1)}, bf16[1,8,128,512]{3,2,1,0:T(8,128)(2,1)}, u32[]{:S(2)}) copy-start(bf16[1,8,128,512]{3,2,1,0:T(8,128)(2,1)} %param.9) | copy-start | bytes 3145732
  0.6 0.8 copy-start.1
  1.4 0.7 copy-start.2
  2.1 0.7 copy-start.3
  2.8 0.7 copy-start.4
  3.5 0.7 copy-start.5
  5.7 28.8 %copy-start.6 = (bf16[512,512]{1,0:T(8,128)(2,1)S(1)}, bf16[512,512]{1,0:T(8,128)(2,1)}, u32[]{:S(2)}) copy-start(bf16[512,512]{1,0:T(8,128)(2,1)} %constant.18.clone.wide_ref) | copy-start | bytes 1572868
  5.7 16.6 %all-to-all-start.1 = ((bf16[8,8,640]{2,1,0:T(8,128)(2,1)}), bf16[8,8,640]{2,1,0:T(8,128)(2,1)S(1)}, u32[]{:S(2)}, u32[]{:S(2)}) async-start(bf16[8,8,640]{2,1,0:T(8,128)(2,1)} %pack.1), calls=%async_computation.1 | async-start | bytes 163840 | tf_op jit(solution)/shard_map/all_to_all | solution.py:304
  22.3 4.2 %collective-permute-start.2 = (bf16[8,8,640]{2,1,0:T(8,128)(2,1)S(1)}, bf16[8,8,640]{2,1,0:T(8,128)(2,1)S(1)}, u32[]{:S(2)}, u32[]{:S(2)}) collective-permute-start(bf16[8,8,640]{2,1,0:T(8,128)(2,1)S(1)} %all-to-all-done.1), channel_id=1, source_target_pairs={{0,48},{16,0},{32,16},{48,32},{1,49},{17,1},{33,17},{49,33},{2,50}... | collective-permute-start | bytes 245768 | tf_op jit(solution)/shard_map/ppermute | solution.py:298
  25.0 4.9 %collective-permute-start.1 = (bf16[8,8,640]{2,1,0:T(8,128)(2,1)S(1)}, bf16[8,8,640]{2,1,0:T(8,128)(2,1)S(1)}, u32[]{:S(2)}, u32[]{:S(2)}) collective-permute-start(bf16[8,8,640]{2,1,0:T(8,128)(2,1)S(1)} %all-to-all-done.1), channel_id=1, source_target_pairs={{0,32},{16,48},{32,0},{48,16},{1,33},{17,49},{33,1},{49,17},{2,34}... | collective-permute-start | bytes 245768 | tf_op jit(solution)/shard_map/ppermute | solution.py:298
  25.4 5.3 %collective-permute-start = (bf16[8,8,640]{2,1,0:T(8,128)(2,1)S(1)}, bf16[8,8,640]{2,1,0:T(8,128)(2,1)S(1)}, u32[]{:S(2)}, u32[]{:S(2)}) collective-permute-start(bf16[8,8,640]{2,1,0:T(8,128)(2,1)S(1)} %all-to-all-done.1), channel_id=1, source_target_pairs={{0,16},{16,32},{32,48},{48,0},{1,17},{17,33},{33,49},{49,1},{2,18}... | collective-permute-start | bytes 245768 | tf_op jit(solution)/shard_map/ppermute | solution.py:298
  30.7 3.7 %copy-start.7 = (bf16[128,128]{1,0:T(8,128)(2,1)S(1)}, bf16[128,128]{1,0:T(8,128)(2,1)}, u32[]{:S(2)}) copy-start(bf16[128,128]{1,0:T(8,128)(2,1)} %constant.19.clone.tall_ref) | copy-start | bytes 98308
  30.8 11.1 %collective-permute-start.5 = (bf16[4,8,8,640]{3,2,1,0:T(8,128)(2,1)S(1)}, bf16[4,8,8,640]{3,2,1,0:T(8,128)(2,1)S(1)}, u32[]{:S(2)}, u32[]{:S(2)}) collective-permute-start(bf16[4,8,8,640]{3,2,1,0:T(8,128)(2,1)S(1)} %pad_maximum_fusion.here_ref), channel_id=1, source_target_pairs={{0,192},{64,0},{128,64},{192,128},{1,193},{65,1},{129,65},{193,129... | collective-permute-start | bytes 983048 | tf_op jit(solution)/shard_map/ppermute | solution.py:298
  33.3 8.5 %collective-permute-start.4 = (bf16[4,8,8,640]{3,2,1,0:T(8,128)(2,1)S(1)}, bf16[4,8,8,640]{3,2,1,0:T(8,128)(2,1)S(1)}, u32[]{:S(2)}, u32[]{:S(2)}) collective-permute-start(bf16[4,8,8,640]{3,2,1,0:T(8,128)(2,1)S(1)} %pad_maximum_fusion.here_ref), channel_id=1, source_target_pairs={{0,128},{64,192},{128,0},{192,64},{1,129},{65,193},{129,1},{193,65... | collective-permute-start | bytes 983048 | tf_op jit(solution)/shard_map/ppermute | solution.py:298
  33.9 16.8 %collective-permute-start.3 = (bf16[4,8,8,640]{3,2,1,0:T(8,128)(2,1)S(1)}, bf16[4,8,8,640]{3,2,1,0:T(8,128)(2,1)S(1)}, u32[]{:S(2)}, u32[]{:S(2)}) collective-permute-start(bf16[4,8,8,640]{3,2,1,0:T(8,128)(2,1)S(1)} %pad_maximum_fusion.here_ref), channel_id=1, source_target_pairs={{0,64},{64,128},{128,192},{192,0},{1,65},{65,129},{129,193},{193,1... | collective-permute-start | bytes 983048 | tf_op jit(solution)/shard_map/ppermute | solution.py:298
  55.4 2.9 %collective-permute-start.6 = (f32[256,512]{1,0:T(8,128)S(1)}, f32[256,512]{1,0:T(8,128)S(1)}, u32[]{:S(2)}, u32[]{:S(2)}) collective-permute-start(f32[256,512]{1,0:T(8,128)S(1)} %project.1.mine_ref), channel_id=1, source_target_pairs={{0,1},{1,0},{2,3},{3,2},{4,5},{5,4},{6,7},{7,6},{8,9},{9,8},{10,11... | collective-permute-start | bytes 1572872 | tf_op jit(solution)/shard_map/ppermute | solution.py:298
  76.3 35.6 %all-to-all-start = ((bf16[128,8,512]{2,1,0:T(8,128)(2,1)}), bf16[128,8,512]{2,1,0:T(8,128)(2,1)S(1)}, u32[]{:S(2)}, u32[]{:S(2)}) async-start(bf16[128,8,512]{2,1,0:T(8,128)(2,1)} %filter.1.tiled_ref), calls=%async_computation | async-start | bytes 2097152 | tf_op jit(solution)/shard_map/all_to_all | solution.py:306

commit v4 on v3

--- a/solution.py
+++ b/solution.py
@@ -12,6 +12,7 @@
 MAXS = 8
 ITERS = 2
 TA = ("ta_0", "ta_1", "ta_2")
+YZ = ("ta_1", "ta_2")
 TA_ROW = ("ta_0", "ta_1", "ta_2", "row")
 
 FRAMES = 8
@@ -23,7 +24,8 @@
 NEURONS = 256
 TILES = 128
 PIXELS = TH * TW
-LINE = 8
+PLANE = 32
+PLANES = 4
 MESSAGE = PIXELS + LANES
 ID_LANE = 64
 HIGHEST = lax.Precision.HIGHEST
@@ -142,32 +144,29 @@
 
 def pack_kernel(ids_ref, order_ref, footprint_ref, support_ref, start_ref, out_ref):
     footprints = footprint_ref[...] * support_ref[...].astype(jnp.bfloat16)
-    parts = jnp.concatenate(split3(start_ref[...]), axis=1)
-    source = iota((3 * LANES, LINE * LANES), 0)
-    target = iota((3 * LANES, LINE * LANES), 1)
-    part, lane = source // LANES, lax.rem(source, LANES)
-    half, z, frame = lane // 64, lax.rem(lane, 64) // FRAMES, lax.rem(lane, FRAMES)
-    exact = jnp.where(target == z * LANES + part * 16 + half * FRAMES + frame, 1.0, 0.0).astype(jnp.bfloat16)
-    pieces = dot32(parts, exact)
+    parts = [part.astype(jnp.float32) for part in split3(start_ref[...])]
     row = iota((SLOTS, LANES), 0)
-    lanes8 = iota((SLOTS, LANES), 1)
+    lane = iota((SLOTS, LANES), 1)
     owners = jnp.zeros((SLOTS, LANES), jnp.float32)
     for i in range(SLOTS):
         owner = order_ref[ids_ref[0, i]].astype(jnp.float32)
-        owners = jnp.where((row == i) & (lanes8 == ID_LANE), owner, owners)
-    for z in range(LINE):
-        out_ref[z, :, :PIXELS] = footprints
-        out_ref[z, :, PIXELS:] = (pieces[:, z * LANES : (z + 1) * LANES] + owners).astype(jnp.bfloat16)
+        owners = jnp.where((row == i) & (lane == ID_LANE), owner, owners)
+    for w in range(PLANE // 2):
+        extra = owners
+        for k, part in enumerate(parts):
+            extra = jnp.where(lane // FRAMES == k, pltpu.roll(part, (FRAMES * (k - w)) % LANES, 1), extra)
+        for to in (w, w + PLANE // 2):
+            out_ref[to, :, :PIXELS] = footprints
+            out_ref[to, :, PIXELS:] = extra.astype(jnp.bfloat16)
 
 
 def pack(ids, order, footprint, support, start):
     return pl.pallas_call(
         pack_kernel,
-        out_shape=jax.ShapeDtypeStruct((LINE, SLOTS, MESSAGE), jnp.bfloat16),
+        out_shape=jax.ShapeDtypeStruct((PLANE, SLOTS, MESSAGE), jnp.bfloat16),
         in_specs=[SMEM, SMEM, VMEM, VMEM, VMEM],
         out_specs=VMEM,
         cost_estimate=pl.CostEstimate(flops=200_000_000, bytes_accessed=200_000, transcendentals=0),
-        compiler_params=pltpu.CompilerParams(vmem_limit_bytes=4 << 20),
         name="pack",
     )(ids, order, footprint, support, start)
 
@@ -176,30 +175,25 @@
     where_ref, tiled_ref, here_ref, left_ref, far_ref, right_ref, out_ref, select_ref, terms_ref
 ):
     x, y = where_ref[0], where_ref[1]
-    rows = 2 * LINE * SLOTS
+    many = PLANE // 2
+    rows = many * SLOTS
     width = NEURONS + LANES
     same = iota((rows, 2 * rows), 0) // SLOTS == lax.rem(iota((rows, 2 * rows), 1), rows) // SLOTS
-    mine = 4 * x + y
-    own_row = iota((2 * LINE, SLOTS, LANES), 1) == mine // 2
-    back = lax.rem(LANES - FRAMES * lax.rem(mine, 2), LANES)
+    own_row = iota((many, SLOTS, LANES), 1) == 2 * x + y // 2
     contract = (((1,), (1,)), ((), ()))
     neuron = iota((rows, NEURONS), 1)
     neuron_t = iota((NEURONS, rows), 0)
     diagonal = iota((rows, rows), 0) == iota((rows, rows), 1)
     out_ref[:, width:] = jnp.zeros((NEURONS, LANES), jnp.float32)
-    for at in range(8):
-        kx, first = at // 2, 2 * (at % 2)
-        ref = (here_ref, left_ref, far_ref, right_ref)[kx]
-        tiles = [
-            pl.multiple_of(LINE * (4 * lax.rem(x + 4 - kx, 4) + lax.rem(y + 4 - ky, 4)), LINE)
-            for ky in (first, first + 1)
-        ]
-        message = ref[first : first + 2]
-        frames = [tiled_ref[pl.ds(tile, LINE)].reshape(rows // 2, PIXELS) for tile in tiles]
-        prints = message[:, :, :, :PIXELS].reshape(rows, PIXELS)
-        extra = message[:, :, :, PIXELS:].astype(jnp.float32).reshape(rows, LANES)
+    for at in range(2 * PLANES):
+        kx, first = at // 2, many * (at % 2)
+        message = (here_ref, left_ref, far_ref, right_ref)[kx][first : first + many]
+        tile = pl.multiple_of(PLANE * lax.rem(x + PLANES - kx, PLANES) + first, many)
+        frames = tiled_ref[pl.ds(tile, many)].reshape(rows, PIXELS)
+        prints = message[:, :, :PIXELS].reshape(rows, PIXELS)
+        extra = message[:, :, PIXELS:].astype(jnp.float32).reshape(rows, LANES)
         found = lax.dot_general(
-            prints, jnp.concatenate(frames + [prints], axis=0), contract, preferred_element_type=jnp.float32
+            prints, jnp.concatenate([frames, prints], axis=0), contract, preferred_element_type=jnp.float32
         )
         found = jnp.where(same, found, 0.0)
         ids = extra[:, ID_LANE : ID_LANE + 1]
@@ -211,11 +205,9 @@
         for k, (one, two) in enumerate(zip(split3(spread), split3(found[:, :rows]), strict=True)):
             terms_ref[span, k * width : k * width + NEURONS] = one
             terms_ref[span, k * width + NEURONS : (k + 1) * width] = two
-        piece = jnp.sum(jnp.where(own_row, extra.reshape(2 * LINE, SLOTS, LANES), 0.0), axis=1)
-        piece = pltpu.roll(piece, back, 1)
-        piece = piece + (pltpu.roll(piece, LANES - 16, 1) + pltpu.roll(piece, LANES - 32, 1))
-        for k in range(2):
-            out_ref[pl.ds(tiles[k], LINE), width:] = piece[k * LINE : (k + 1) * LINE]
+        piece = jnp.sum(jnp.where(own_row, extra.reshape(many, SLOTS, LANES), 0.0), axis=1)
+        piece = piece + (pltpu.roll(piece, LANES - FRAMES, 1) + pltpu.roll(piece, LANES - 2 * FRAMES, 1))
+        out_ref[pl.ds(tile, many), width:] = piece
     sums = dot32(select_ref[...], terms_ref[...])
     out_ref[:, :width] = sums[:, :width] + (sums[:, width : 2 * width] + sums[:, 2 * width :])
 
@@ -237,8 +229,9 @@
     )(where, tiled, here, left, far, right)
 
 
-def solve_kernel(where_ref, mine_ref, other_ref, out_ref, current_ref):
-    core = where_ref[2]
+def solve_kernel(where_ref, mine_ref, other_ref, *refs):
+    out_refs, current_ref, own_ref = refs[:PLANES], refs[PLANES], refs[PLANES + 1]
+    x, core = where_ref[0], where_ref[2]
     sums = mine_ref[:, : NEURONS + LANES] + other_ref[:, : NEURONS + LANES]
     coupling = sums[:, :NEURONS]
     source = iota((LANES, LANES), 0)
@@ -258,28 +251,58 @@
     current_ref[...] = current
     even = current_ref[pl.ds(0, TILES, stride=2), :]
     odd = current_ref[pl.ds(1, TILES, stride=2), :]
-    out_ref[...] = jnp.where(core == 0, even, odd)
+    own_ref[...] = jnp.where(core == 0, even, odd)
+    for k in range(PLANES):
+        at = pl.multiple_of(PLANE * lax.rem(x + k, PLANES), PLANE)
+        out_refs[k][...] = own_ref[pl.ds(at, PLANE), :]
 
 
 def solve(where, mine, other):
     return pl.pallas_call(
         solve_kernel,
-        out_shape=jax.ShapeDtypeStruct((TILES, LANES), jnp.float32),
+        out_shape=[jax.ShapeDtypeStruct((PLANE, LANES), jnp.float32)] * PLANES,
         in_specs=[SMEM, VMEM, VMEM],
-        out_specs=VMEM,
-        scratch_shapes=[pltpu.VMEM((NEURONS, LANES), jnp.float32)],
+        out_specs=[VMEM] * PLANES,
+        scratch_shapes=[pltpu.VMEM((NEURONS, LANES), jnp.float32), pltpu.VMEM((TILES, LANES), jnp.float32)],
         cost_estimate=pl.CostEstimate(flops=2_000_000_000, bytes_accessed=1_000_000, transcendentals=0),
         compiler_params=pltpu.CompilerParams(vmem_limit_bytes=8 << 20),
         name="solve",
     )(where, mine, other)
 
 
+def merge_kernel(where_ref, *refs):
+    group = lax.rem(iota((PLANE, LANES), 1) // FRAMES, PLANES)
+    merged = refs[0][...]
+    for k in range(1, PLANES):
+        merged = jnp.where(group == lax.rem(where_ref[0] + PLANES - k, PLANES), refs[k][...], merged)
+    refs[PLANES][...] = merged
+
+
+def merge(where, pieces):
+    return pl.pallas_call(
+        merge_kernel,
+        out_shape=jax.ShapeDtypeStruct((PLANE, LANES), jnp.float32),
+        in_specs=[SMEM] + [VMEM] * PLANES,
+        out_specs=VMEM,
+        cost_estimate=pl.CostEstimate(flops=100_000_000, bytes_accessed=100_000, transcendentals=0),
+        compiler_params=pltpu.CompilerParams(vmem_limit_bytes=2 << 20),
+        name="merge",
+    )(where, *pieces)
+
+
 def join_kernel(pieces_ref, out_ref):
     near = LANES // FRAMES
-    inside = iota((near, LANES), 1) // FRAMES == iota((near, LANES), 0)
+    pieces = pieces_ref[...]
+    rolled = [pieces] + [pltpu.roll(pieces, FRAMES * j, 1) for j in range(1, PLANES)]
+    group = iota((near, LANES), 1) // FRAMES
+    inside = group == iota((near, LANES), 0)
     for b in range(TILES // near):
-        piece = jnp.where(inside, pieces_ref[pl.ds(b * near, near), :], 0.0)
-        out_ref[:, b * LANES : (b + 1) * LANES] = jnp.sum(piece, axis=0, keepdims=True)
+        xs, first = b // 2, near * (b % 2)
+        total = jnp.zeros((near, LANES), jnp.float32)
+        for j in range(PLANES):
+            hit = inside & (lax.rem(group + PLANES - j, PLANES) == xs)
+            total = jnp.where(hit, rolled[j][first : first + near], total)
+        out_ref[:, b * LANES : (b + 1) * LANES] = jnp.sum(total, axis=0, keepdims=True)
 
 
 def join(pieces):
@@ -301,16 +324,17 @@
 def local(movie, shifts, footprint, support, neuron_ids, owner_order, start_traces):
     where = jnp.stack([lax.axis_index(axis) for axis in ("ta_0", "ta_1", "row")]).astype(jnp.int32)
     packed = pack(neuron_ids[0], owner_order, footprint[0, 0], support[0, 0], start_traces.reshape(8, LANES))
-    line = lax.all_to_all(packed, "ta_2", 0, 0, tiled=True)
+    here = lax.all_to_all(packed, YZ, 0, 0, tiled=True)
     tiled = filter_tiles(movie[0], shifts[0])
     tile_movie = lax.all_to_all(tiled, TA, split_axis=0, concat_axis=0, tiled=True)
-    here = jnp.stack([line] + [moved(line, "ta_1", by) for by in range(1, 4)])
-    left, far, right = [moved(here, "ta_0", by) for by in range(1, 4)]
+    left, far, right = [moved(here, "ta_0", by) for by in range(1, PLANES)]
     mine = project(where, tiled, here, left, far, right)
     other = moved(mine, "row", 1)
     pieces = solve(where, mine, other)
-    pieces = lax.all_to_all(pieces.reshape(TILES, 1, LANES), TA, 0, 0, tiled=True)
-    traces = join(pieces.reshape(TILES, LANES))
+    pieces = [pieces[0]] + [moved(pieces[k], "ta_0", k) for k in range(1, PLANES)]
+    pieces = merge(where, pieces)
+    pieces = lax.all_to_all(pieces.reshape(PLANE, 1, LANES), YZ, 0, 0, tiled=True)
+    traces = join(pieces.reshape(PLANE, LANES))
     return (tile_movie.reshape(1, 1, -1, PIXELS), traces)
 
 

time: 114 us -> 113 us (level)
  the two profiles are of different devices: /device:TPU:1 before, /device:TPU:32 now
where the time goes in v4:
time: 113 us; the launch traced here: 112 us
  waiting for transfers between devices  52 us (46%)
  starting transfers between devices  26.9 us (24%)
  Pallas kernels  16.9 us (15%)
  blocking collectives  13.7 us (12%)
  local copies, waits for them, and re-layouts  2.13 us (2%)
    all_to_all x1, waiting for transfers between devices, local(): lax.all_to_all(tiled, TA, split_axis=0, concat_axis=0, tiled=True)  28 us
    all_to_all x1, blocking collectives, local(): lax.all_to_all(pieces.reshape(PLANE, 1, LANES), YZ, 0, 0, tiled=True)  13.7 us
    all_to_all x1, waiting for transfers between devices, local(): here = lax.all_to_all(packed, YZ, 0, 0, tiled=True)  13.4 us
    all_to_all x1, starting transfers between devices, local(): here = lax.all_to_all(packed, YZ, 0, 0, tiled=True)  11.5 us
    ppermute x7, waiting for transfers between devices, moved(): lax.ppermute(array, axis, [(i, (i + by) % count) for i in range(count)])  10.6 us
    ppermute x7, starting transfers between devices, moved(): lax.ppermute(array, axis, [(i, (i + by) % count) for i in range(count)])  8.04 us
    pallas_call x1, Pallas kernels, filter_tiles(): pl.pallas_call(filter_kernel, out_shape=jax.ShapeDtypeStruct((TILES, FRAM...  7.41 us
    all_to_all x1, starting transfers between devices, local(): lax.all_to_all(tiled, TA, split_axis=0, concat_axis=0, tiled=True)  7.37 us
  transfers between devices with their start and end apart: 9, of which 8 were waited for; matrix products, arithmetic and copies ran while one was open for 0% of the time, Pallas kernels for 7%

profile of v4, /device:TPU:32, one launch (start us, length us, event | category | flops | bytes accessed | tf_op | source)
XLA Modules:
  0.0 112.4 jit_solution(12750263844292426274)
XLA Ops:
  0.6 1.7 %pack.1 = bf16[32,8,640]{2,1,0:T(8,128)(2,1)} custom-call(s32[1,8]{1,0:T(1,128)} %bitcast.22, s32[256]{0:T(256)} %order_ref.1, bf16[8,512]{1,0:T(8,128)(2,1)} %bitcast.20, s32[8,512]{1,0:T(8,128)} %bitcast.19, f32[8,128]{1,0:T(8,128)} %bitcast.21), custom_call_target="tpu_custom_call" | custom-call | flops 200000000 | bytes 200000 | tf_op jit(solution)/shard_map/pack/pallas_call | solution.py:164
  2.3 11.5 %all-to-all-start.1 = ((bf16[32,8,640]{2,1,0:T(8,128)(2,1)}), bf16[32,8,640]{2,1,0:T(8,128)(2,1)S(1)}, u32[]{:S(2)}, u32[]{:S(2)}) async-start(bf16[32,8,640]{2,1,0:T(8,128)(2,1)} %pack.1), calls=%async_computation.1 | async-start | bytes 655360 | tf_op jit(solution)/shard_map/all_to_all | solution.py:327
  14.0 13.4 %all-to-all-done.1.here_ref = bf16[32,8,640]{2,1,0:T(8,128)(2,1)S(1)} async-done(((bf16[32,8,640]{2,1,0:T(8,128)(2,1)}), bf16[32,8,640]{2,1,0:T(8,128)(2,1)S(1)}, u32[]{:S(2)}, u32[]{:S(2)}) %all-to-all-start.1) | async-done | bytes 327712 | tf_op jit(solution)/shard_map/all_to_all | solution.py:327
  27.4 2.8 %collective-permute-start.2 = (bf16[32,8,640]{2,1,0:T(8,128)(2,1)S(1)}, bf16[32,8,640]{2,1,0:T(8,128)(2,1)S(1)}, u32[]{:S(2)}, u32[]{:S(2)}) collective-permute-start(bf16[32,8,640]{2,1,0:T(8,128)(2,1)S(1)} %all-to-all-done.1.here_ref), channel_id=1, source_target_pairs={{0,192},{64,0},{128,64},{192,128},{1,193},{65,1},{129,65},{193,129... | collective-permute-start | bytes 983048 | tf_op jit(solution)/shard_map/ppermute | solution.py:321
  30.1 0.8 collective-permute-start.1
  30.9 0.9 collective-permute-start
  31.8 1.0 copy-done.1
  32.9 7.4 %filter.1.tiled_ref = bf16[128,8,512]{2,1,0:T(8,128)(2,1)} custom-call(s32[8,4,2]{2,1,0:T(4,128)S(1)} %copy.14.shifts_ref, bf16[8,128,512]{2,1,0:T(8,128)(2,1)S(1)} %bitcast.16, bf16[512,512]{1,0:T(8,128)(2,1)S(1)} %copy-done.1, bf16[128,128]{1,0:T(8,128)(2,1)S(1)} %copy-done.2), custom_call_target="tpu_custom_call" | custom-call | flops 4000000000 | bytes 3000000 | tf_op jit(solution)/shard_map/filter/pallas_call | solution.py:129
  40.3 2.4 %collective-permute-done.2.right_ref = bf16[32,8,640]{2,1,0:T(8,128)(2,1)S(1)} collective-permute-done((bf16[32,8,640]{2,1,0:T(8,128)(2,1)S(1)}, bf16[32,8,640]{2,1,0:T(8,128)(2,1)S(1)}, u32[]{:S(2)}, u32[]{:S(2)}) %collective-permute-start.2) | collective-permute-done | bytes 327712 | tf_op jit(solution)/shard_map/ppermute | solution.py:321
  42.7 3.7 %collective-permute-done.left_ref = bf16[32,8,640]{2,1,0:T(8,128)(2,1)S(1)} collective-permute-done((bf16[32,8,640]{2,1,0:T(8,128)(2,1)S(1)}, bf16[32,8,640]{2,1,0:T(8,128)(2,1)S(1)}, u32[]{:S(2)}, u32[]{:S(2)}) %collective-permute-start) | collective-permute-done | bytes 327712 | tf_op jit(solution)/shard_map/ppermute | solution.py:321
  46.4 4.7 %project.1.mine_ref = f32[256,512]{1,0:T(8,128)S(1)} custom-call(s32[3]{0:T(128)S(1)} %pad_add_fusion.where_ref, bf16[128,8,512]{2,1,0:T(8,128)(2,1)} %filter.1.tiled_ref, bf16[32,8,640]{2,1,0:T(8,128)(2,1)S(1)} %all-to-all-done.1.here_ref, bf16[32,8,640]{2,1,0:T(8,128)(2,1)S(1)} %collective-permute-done.left_ref, ...), custom_call_target="tpu_custom_call" | custom-call | flops 2000000000 | bytes 3000000 | tf_op jit(solution)/shard_map/project/pallas_call | solution.py:217
  51.2 1.9 %collective-permute-done.3.other_ref = f32[256,512]{1,0:T(8,128)S(1)} collective-permute-done((f32[256,512]{1,0:T(8,128)S(1)}, f32[256,512]{1,0:T(8,128)S(1)}, u32[]{:S(2)}, u32[]{:S(2)}) %collective-permute-start.3) | collective-permute-done | bytes 524320 | tf_op jit(solution)/shard_map/ppermute | solution.py:321
  53.1 1.9 %solve.1 = (f32[32,128]{1,0:T(8,128)S(1)}, f32[32,128]{1,0:T(8,128)S(1)}, f32[32,128]{1,0:T(8,128)S(1)}, f32[32,128]{1,0:T(8,128)S(1)}) custom-call(s32[3]{0:T(128)S(1)} %pad_add_fusion.where_ref, f32[256,512]{1,0:T(8,128)S(1)} %project.1.mine_ref, f32[256,512]{1,0:T(8,128)S(1)} %collective-permute-done.3.other_ref), custom_call_target="tpu_custom_call" | custom-call | flops 2000000000 | bytes 1000000 | tf_op jit(solution)/shard_map/solve/pallas_call | solution.py:261
  55.1 2.0 %collective-permute-start.5 = (f32[32,128]{1,0:T(8,128)S(1)}, f32[32,128]{1,0:T(8,128)S(1)}, u32[]{:S(2)}, u32[]{:S(2)}) collective-permute-start(f32[32,128]{1,0:T(8,128)S(1)} %get-tuple-element.8), channel_id=1, source_target_pairs={{0,128},{64,192},{128,0},{192,64},{1,129},{65,193},{129,1},{193,65... | collective-permute-start | bytes 49160 | tf_op jit(solution)/shard_map/ppermute | solution.py:321
  57.1 1.4 %collective-permute-start.6 = (f32[32,128]{1,0:T(8,128)S(1)}, f32[32,128]{1,0:T(8,128)S(1)}, u32[]{:S(2)}, u32[]{:S(2)}) collective-permute-start(f32[32,128]{1,0:T(8,128)S(1)} %get-tuple-element.9), channel_id=1, source_target_pairs={{0,192},{64,0},{128,64},{192,128},{1,193},{65,1},{129,65},{193,129... | collective-permute-start | bytes 49160 | tf_op jit(solution)/shard_map/ppermute | solution.py:321
  58.5 1.5 %collective-permute-done.4.refs_1_ = f32[32,128]{1,0:T(8,128)S(1)} collective-permute-done((f32[32,128]{1,0:T(8,128)S(1)}, f32[32,128]{1,0:T(8,128)S(1)}, u32[]{:S(2)}, u32[]{:S(2)}) %collective-permute-start.4) | collective-permute-done | bytes 16416 | tf_op jit(solution)/shard_map/ppermute | solution.py:321
  60.0 0.4 collective-permute-done.5.refs_2_
  60.4 0.6 collective-permute-done.6.refs_3_
  61.1 0.6 merge.1
  61.6 13.7 %all_to_all.15 = f32[32,1,128]{2,1,0:T(1,128)S(1)} all-to-all(f32[32,1,128]{2,1,0:T(1,128)S(1)} %bitcast.15), channel_id=1, replica_groups=mesh['ta_0'=4,'ta_1'=4,'ta_2'=8,'row'=2] {'ta_1','ta_2'}, dimensions={0} | all-to-all | bytes 32768 | tf_op jit(solution)/shard_map/all_to_all | solution.py:336
  75.3 7.4 %all-to-all-start = ((bf16[128,8,512]{2,1,0:T(8,128)(2,1)}), bf16[128,8,512]{2,1,0:T(8,128)(2,1)S(1)}, u32[]{:S(2)}, u32[]{:S(2)}) async-start(bf16[128,8,512]{2,1,0:T(8,128)(2,1)} %filter.1.tiled_ref), calls=%async_computation | async-start | bytes 2097152 | tf_op jit(solution)/shard_map/all_to_all | solution.py:329
  82.7 0.7 join.1
  83.4 28.0 %all-to-all-done = bf16[128,8,512]{2,1,0:T(8,128)(2,1)S(1)} async-done(((bf16[128,8,512]{2,1,0:T(8,128)(2,1)}), bf16[128,8,512]{2,1,0:T(8,128)(2,1)S(1)}, u32[]{:S(2)}, u32[]{:S(2)}) %all-to-all-start) | async-done | bytes 1048608 | tf_op jit(solution)/shard_map/all_to_all | solution.py:329
  111.5 1.0 copy.19
  (12 shorter events, 0.4 us)
Async XLA Ops:
  0.6 31.2 %copy-start = (bf16[1,8,128,512]{3,2,1,0:T(8,128)(2,1)S(1)}, bf16[1,8,128,512]{3,2,1,0:T(8,128)(2,1)}, u32[]{:S(2)}) copy-start(bf16[1,8,128,512]{3,2,1,0:T(8,128)(2,1)} %param.9) | copy-start | bytes 3145732
  2.3 11.5 %copy-start.3 = (s32[1,8,4,2]{1,3,2,0:T(2,128)S(1)}, s32[1,8,4,2]{1,3,2,0:T(2,128)}, u32[]{:S(2)}) copy-start(s32[1,8,4,2]{1,3,2,0:T(2,128)} %param.10) | copy-start | bytes 772
  2.3 25.1 %all-to-all-start.1 = ((bf16[32,8,640]{2,1,0:T(8,128)(2,1)}), bf16[32,8,640]{2,1,0:T(8,128)(2,1)S(1)}, u32[]{:S(2)}, u32[]{:S(2)}) async-start(bf16[32,8,640]{2,1,0:T(8,128)(2,1)} %pack.1), calls=%async_computation.1 | async-start | bytes 655360 | tf_op jit(solution)/shard_map/all_to_all | solution.py:327
  13.8 18.0 %copy-start.2 = (bf16[128,128]{1,0:T(8,128)(2,1)S(1)}, bf16[128,128]{1,0:T(8,128)(2,1)}, u32[]{:S(2)}) copy-start(bf16[128,128]{1,0:T(8,128)(2,1)} %constant.19.clone.tall_ref) | copy-start | bytes 98308
  27.4 15.3 %collective-permute-start.2 = (bf16[32,8,640]{2,1,0:T(8,128)(2,1)S(1)}, bf16[32,8,640]{2,1,0:T(8,128)(2,1)S(1)}, u32[]{:S(2)}, u32[]{:S(2)}) collective-permute-start(bf16[32,8,640]{2,1,0:T(8,128)(2,1)S(1)} %all-to-all-done.1.here_ref), channel_id=1, source_target_pairs={{0,192},{64,0},{128,64},{192,128},{1,193},{65,1},{129,65},{193,129... | collective-permute-start | bytes 983048 | tf_op jit(solution)/shard_map/ppermute | solution.py:321
  30.1 12.6 %collective-permute-start.1 = (bf16[32,8,640]{2,1,0:T(8,128)(2,1)S(1)}, bf16[32,8,640]{2,1,0:T(8,128)(2,1)S(1)}, u32[]{:S(2)}, u32[]{:S(2)}) collective-permute-start(bf16[32,8,640]{2,1,0:T(8,128)(2,1)S(1)} %all-to-all-done.1.here_ref), channel_id=1, source_target_pairs={{0,128},{64,192},{128,0},{192,64},{1,129},{65,193},{129,1},{193,65... | collective-permute-start | bytes 983048 | tf_op jit(solution)/shard_map/ppermute | solution.py:321
  30.9 15.5 %collective-permute-start = (bf16[32,8,640]{2,1,0:T(8,128)(2,1)S(1)}, bf16[32,8,640]{2,1,0:T(8,128)(2,1)S(1)}, u32[]{:S(2)}, u32[]{:S(2)}) collective-permute-start(bf16[32,8,640]{2,1,0:T(8,128)(2,1)S(1)} %all-to-all-done.1.here_ref), channel_id=1, source_target_pairs={{0,64},{64,128},{128,192},{192,0},{1,65},{65,129},{129,193},{193,1... | collective-permute-start | bytes 983048 | tf_op jit(solution)/shard_map/ppermute | solution.py:321
  31.8 1.0 copy-start.1
  51.1 2.0 %collective-permute-start.3 = (f32[256,512]{1,0:T(8,128)S(1)}, f32[256,512]{1,0:T(8,128)S(1)}, u32[]{:S(2)}, u32[]{:S(2)}) collective-permute-start(f32[256,512]{1,0:T(8,128)S(1)} %project.1.mine_ref), channel_id=1, source_target_pairs={{0,1},{1,0},{2,3},{3,2},{4,5},{5,4},{6,7},{7,6},{8,9},{9,8},{10,11... | collective-permute-start | bytes 1572872 | tf_op jit(solution)/shard_map/ppermute | solution.py:321
  55.0 5.0 %collective-permute-start.4 = (f32[32,128]{1,0:T(8,128)S(1)}, f32[32,128]{1,0:T(8,128)S(1)}, u32[]{:S(2)}, u32[]{:S(2)}) collective-permute-start(f32[32,128]{1,0:T(8,128)S(1)} %get-tuple-element.7), channel_id=1, source_target_pairs={{0,64},{64,128},{128,192},{192,0},{1,65},{65,129},{129,193},{193,1... | collective-permute-start | bytes 49160 | tf_op jit(solution)/shard_map/ppermute | solution.py:321
  55.1 5.3 %collective-permute-start.5 = (f32[32,128]{1,0:T(8,128)S(1)}, f32[32,128]{1,0:T(8,128)S(1)}, u32[]{:S(2)}, u32[]{:S(2)}) collective-permute-start(f32[32,128]{1,0:T(8,128)S(1)} %get-tuple-element.8), channel_id=1, source_target_pairs={{0,128},{64,192},{128,0},{192,64},{1,129},{65,193},{129,1},{193,65... | collective-permute-start | bytes 49160 | tf_op jit(solution)/shard_map/ppermute | solution.py:321
  57.1 3.9 %collective-permute-start.6 = (f32[32,128]{1,0:T(8,128)S(1)}, f32[32,128]{1,0:T(8,128)S(1)}, u32[]{:S(2)}, u32[]{:S(2)}) collective-permute-start(f32[32,128]{1,0:T(8,128)S(1)} %get-tuple-element.9), channel_id=1, source_target_pairs={{0,192},{64,0},{128,64},{192,128},{1,193},{65,1},{129,65},{193,129... | collective-permute-start | bytes 49160 | tf_op jit(solution)/shard_map/ppermute | solution.py:321
  75.3 36.1 %all-to-all-start = ((bf16[128,8,512]{2,1,0:T(8,128)(2,1)}), bf16[128,8,512]{2,1,0:T(8,128)(2,1)S(1)}, u32[]{:S(2)}, u32[]{:S(2)}) async-start(bf16[128,8,512]{2,1,0:T(8,128)(2,1)} %filter.1.tiled_ref), calls=%async_computation | async-start | bytes 2097152 | tf_op jit(solution)/shard_map/all_to_all | solution.py:329

commit v5 on v4

--- a/solution.py
+++ b/solution.py
@@ -61,42 +61,69 @@
     return dot32(high, exact) + (dot32(mid, exact) + dot32(low, exact))
 
 
-def filter_kernel(
-    shifts_ref, movie_ref, wide_ref, tall_ref, out_ref, padded_ref, registered_ref, filtered_ref,
-):
+def register_kernel(shifts_ref, movie_ref, out_ref, padded_ref):
     lane = iota((H, LANES), 1)
-    padded_ref[:, pl.ds(0, MAXS), :] = jnp.zeros((BLOCKS, MAXS, LANES), jnp.float32)
-    padded_ref[:, pl.ds(MAXS + H, MAXS), :] = jnp.zeros((BLOCKS, MAXS, LANES), jnp.float32)
+    for s in range(2 * BLOCKS):
+        padded_ref[s, pl.ds(0, MAXS), :] = jnp.zeros((MAXS, LANES), jnp.float32)
+        padded_ref[s, pl.ds(MAXS + H, MAXS), :] = jnp.zeros((MAXS, LANES), jnp.float32)
 
     def block(f, p):
         if p < 0 or p >= BLOCKS:
             return None
         return movie_ref[f, :, p * LANES : (p + 1) * LANES].astype(jnp.float32)
 
-    def frame(f, carry):
-        for p in range(BLOCKS):
-            dy = shifts_ref[f, p, 0]
-            dx = shifts_ref[f, p, 1]
-            amount = jnp.where(dx > 0, LANES - dx, -dx)
-            source = lane + dx
-
-            def rolled(value):
-                if value is None:
-                    return jnp.zeros((H, LANES), jnp.float32)
-                return pltpu.roll(value, amount, 1)
-
-            inner = jnp.where(source >= LANES, rolled(block(f, p + 1)), rolled(block(f, p)))
-            moved = jnp.where(source < 0, rolled(block(f, p - 1)), inner)
-            padded_ref[p, pl.ds(MAXS, H), :] = moved
-            registered_ref[:, p * LANES : (p + 1) * LANES] = padded_ref[p, pl.ds(MAXS + dy, H), :]
-        registered = registered_ref[...]
-        wide = dot32(registered.astype(jnp.bfloat16), wide_ref[...]).astype(jnp.bfloat16)
-        filtered = registered - dot32(tall_ref[...], wide)
-        for p in range(BLOCKS):
-            filtered_ref[p, pl.ds(f, H, stride=FRAMES), :] = filtered[:, p * LANES : (p + 1) * LANES]
+    def shift(f, p, s):
+        dy = shifts_ref[f, p, 0]
+        dx = shifts_ref[f, p, 1]
+        amount = jnp.where(dx > 0, LANES - dx, -dx)
+        source = lane + dx
+
+        def rolled(value):
+            if value is None:
+                return jnp.zeros((H, LANES), jnp.float32)
+            return pltpu.roll(value, amount, 1)
+
+        inner = jnp.where(source >= LANES, rolled(block(f, p + 1)), rolled(block(f, p)))
+        padded_ref[s, pl.ds(MAXS, H), :] = jnp.where(source < 0, rolled(block(f, p - 1)), inner)
+        out_ref[f, :, p * LANES : (p + 1) * LANES] = padded_ref[s, pl.ds(MAXS + dy, H), :].astype(jnp.bfloat16)
+
+    def frames(g, carry):
+        for h in range(2):
+            for p in range(BLOCKS):
+                shift(2 * g + h, p, h * BLOCKS + p)
         return carry
 
-    lax.fori_loop(0, FRAMES, frame, 0)
+    lax.fori_loop(0, FRAMES // 2, frames, 0)
+
+
+def register(movie, shifts):
+    return pl.pallas_call(
+        register_kernel,
+        out_shape=jax.ShapeDtypeStruct((FRAMES, H, W), jnp.bfloat16),
+        in_specs=[SMEM, VMEM],
+        out_specs=VMEM,
+        scratch_shapes=[pltpu.VMEM((2 * BLOCKS, H + 2 * MAXS, LANES), jnp.float32)],
+        cost_estimate=pl.CostEstimate(flops=2_000_000_000, bytes_accessed=2_000_000, transcendentals=0),
+        compiler_params=pltpu.CompilerParams(vmem_limit_bytes=8 << 20),
+        name="register",
+    )(shifts, movie)
+
+
+def smooth_kernel(registered_ref, wide_ref, tall_ref, out_ref, filtered_ref, soft_ref):
+    step = 2
+
+    def chunk(c, carry):
+        registered = registered_ref[pl.ds(c * step, step)].reshape(step * H, W)
+        soft_ref[...] = dot32(registered, wide_ref[...]).astype(jnp.bfloat16)
+        for k in range(step):
+            low = dot32(tall_ref[...], soft_ref[k * H : (k + 1) * H, :])
+            filtered = registered[k * H : (k + 1) * H].astype(jnp.float32) - low
+            for p in range(BLOCKS):
+                span = pl.ds(c * step + k, H, stride=FRAMES)
+                filtered_ref[p, span, :] = filtered[:, p * LANES : (p + 1) * LANES]
+        return carry
+
+    lax.fori_loop(0, FRAMES // step, chunk, 0)
     lanes8 = iota((FRAMES, LANES), 1)
     near = lanes8 < 2 * TW
     even = lax.rem(lanes8 // TW, 2) == 0
@@ -123,23 +150,23 @@
         return carry
 
     lax.fori_loop(0, H // TH, tile_row, 0)
-
-
-def filter_tiles(movie, shifts):
-    return pl.pallas_call(
-        filter_kernel,
-        out_shape=jax.ShapeDtypeStruct((TILES, FRAMES, PIXELS), jnp.bfloat16),
-        in_specs=[SMEM, VMEM, VMEM, VMEM],
+    out_ref[:, :, PIXELS:] = jnp.zeros((TILES, FRAMES, LANES), jnp.bfloat16)
+
+
+def smooth(registered):
+    return pl.pallas_call(
+        smooth_kernel,
+        out_shape=jax.ShapeDtypeStruct((TILES, FRAMES, MESSAGE), jnp.bfloat16),
+        in_specs=[VMEM] * 3,
         out_specs=VMEM,
         scratch_shapes=[
-            pltpu.VMEM((BLOCKS, H + 2 * MAXS, LANES), jnp.float32),
-            pltpu.VMEM((H, W), jnp.float32),
             pltpu.VMEM((BLOCKS, H * FRAMES, LANES), jnp.float32),
+            pltpu.VMEM((2 * H, W), jnp.bfloat16),
         ],
         cost_estimate=pl.CostEstimate(flops=4_000_000_000, bytes_accessed=3_000_000, transcendentals=0),
         compiler_params=pltpu.CompilerParams(vmem_limit_bytes=16 << 20),
-        name="filter",
-    )(shifts, movie, smoothing_table(W), smoothing_table(H).T)
+        name="smooth",
+    )(registered, smoothing_table(W), smoothing_table(H).T)
 
 
 def pack_kernel(ids_ref, order_ref, footprint_ref, support_ref, start_ref, out_ref):
@@ -189,7 +216,7 @@
         kx, first = at // 2, many * (at % 2)
         message = (here_ref, left_ref, far_ref, right_ref)[kx][first : first + many]
         tile = pl.multiple_of(PLANE * lax.rem(x + PLANES - kx, PLANES) + first, many)
-        frames = tiled_ref[pl.ds(tile, many)].reshape(rows, PIXELS)
+        frames = tiled_ref[pl.ds(tile, many), :, :PIXELS].reshape(rows, PIXELS)
         prints = message[:, :, :PIXELS].reshape(rows, PIXELS)
         extra = message[:, :, PIXELS:].astype(jnp.float32).reshape(rows, LANES)
         found = lax.dot_general(
@@ -229,9 +256,8 @@
     )(where, tiled, here, left, far, right)
 
 
-def solve_kernel(where_ref, mine_ref, other_ref, *refs):
-    out_refs, current_ref, own_ref = refs[:PLANES], refs[PLANES], refs[PLANES + 1]
-    x, core = where_ref[0], where_ref[2]
+def solve_kernel(where_ref, mine_ref, other_ref, tiled_ref, out_ref, current_ref, parts_ref, sem):
+    core = where_ref[2]
     sums = mine_ref[:, : NEURONS + LANES] + other_ref[:, : NEURONS + LANES]
     coupling = sums[:, :NEURONS]
     source = iota((LANES, LANES), 0)
@@ -251,69 +277,57 @@
     current_ref[...] = current
     even = current_ref[pl.ds(0, TILES, stride=2), :]
     odd = current_ref[pl.ds(1, TILES, stride=2), :]
-    own_ref[...] = jnp.where(core == 0, even, odd)
-    for k in range(PLANES):
-        at = pl.multiple_of(PLANE * lax.rem(x + k, PLANES), PLANE)
-        out_refs[k][...] = own_ref[pl.ds(at, PLANE), :]
-
-
-def solve(where, mine, other):
+    high, mid, low = [part.astype(jnp.float32) for part in split3(jnp.where(core == 0, even, odd))]
+    row = iota((SLOTS, LANES), 0)
+    for t in range(TILES):
+        lower = jnp.where(row == 1, mid[t : t + 1], jnp.where(row == 2, low[t : t + 1], 0.0))
+        parts_ref[t] = jnp.where(row == 0, high[t : t + 1], lower).astype(jnp.bfloat16)
+    store = pltpu.make_async_copy(parts_ref, out_ref.at[:, :, pl.ds(PIXELS, LANES)], sem)
+    store.start()
+    store.wait()
+
+
+def solve(where, mine, other, tiled):
     return pl.pallas_call(
         solve_kernel,
-        out_shape=[jax.ShapeDtypeStruct((PLANE, LANES), jnp.float32)] * PLANES,
-        in_specs=[SMEM, VMEM, VMEM],
-        out_specs=[VMEM] * PLANES,
-        scratch_shapes=[pltpu.VMEM((NEURONS, LANES), jnp.float32), pltpu.VMEM((TILES, LANES), jnp.float32)],
+        out_shape=jax.ShapeDtypeStruct(tiled.shape, tiled.dtype),
+        in_specs=[SMEM, VMEM, VMEM, pl.BlockSpec(memory_space=pl.ANY)],
+        out_specs=pl.BlockSpec(memory_space=pl.ANY),
+        scratch_shapes=[
+            pltpu.VMEM((NEURONS, LANES), jnp.float32),
+            pltpu.VMEM((TILES, SLOTS, LANES), jnp.bfloat16),
+            pltpu.SemaphoreType.DMA,
+        ],
+        input_output_aliases={3: 0},
         cost_estimate=pl.CostEstimate(flops=2_000_000_000, bytes_accessed=1_000_000, transcendentals=0),
         compiler_params=pltpu.CompilerParams(vmem_limit_bytes=8 << 20),
         name="solve",
-    )(where, mine, other)
-
-
-def merge_kernel(where_ref, *refs):
-    group = lax.rem(iota((PLANE, LANES), 1) // FRAMES, PLANES)
-    merged = refs[0][...]
-    for k in range(1, PLANES):
-        merged = jnp.where(group == lax.rem(where_ref[0] + PLANES - k, PLANES), refs[k][...], merged)
-    refs[PLANES][...] = merged
-
-
-def merge(where, pieces):
-    return pl.pallas_call(
-        merge_kernel,
-        out_shape=jax.ShapeDtypeStruct((PLANE, LANES), jnp.float32),
-        in_specs=[SMEM] + [VMEM] * PLANES,
-        out_specs=VMEM,
-        cost_estimate=pl.CostEstimate(flops=100_000_000, bytes_accessed=100_000, transcendentals=0),
-        compiler_params=pltpu.CompilerParams(vmem_limit_bytes=2 << 20),
-        name="merge",
-    )(where, *pieces)
-
-
-def join_kernel(pieces_ref, out_ref):
+    )(where, mine, other, tiled)
+
+
+def unpack_kernel(arrived_ref, movie_ref, traces_ref):
+    movie_ref[...] = arrived_ref[:, :, :PIXELS].reshape(TILES * FRAMES, PIXELS)
     near = LANES // FRAMES
-    pieces = pieces_ref[...]
-    rolled = [pieces] + [pltpu.roll(pieces, FRAMES * j, 1) for j in range(1, PLANES)]
-    group = iota((near, LANES), 1) // FRAMES
-    inside = group == iota((near, LANES), 0)
+    group = iota((SLOTS, LANES), 1) // FRAMES
     for b in range(TILES // near):
-        xs, first = b // 2, near * (b % 2)
-        total = jnp.zeros((near, LANES), jnp.float32)
-        for j in range(PLANES):
-            hit = inside & (lax.rem(group + PLANES - j, PLANES) == xs)
-            total = jnp.where(hit, rolled[j][first : first + near], total)
-        out_ref[:, b * LANES : (b + 1) * LANES] = jnp.sum(total, axis=0, keepdims=True)
-
-
-def join(pieces):
-    return pl.pallas_call(
-        join_kernel,
-        out_shape=jax.ShapeDtypeStruct((1, TILES * FRAMES), jnp.float32),
+        total = jnp.zeros((SLOTS, LANES), jnp.float32)
+        for t in range(near):
+            total = jnp.where(group == t, arrived_ref[b * near + t, :, PIXELS:].astype(jnp.float32), total)
+        traces_ref[:, b * LANES : (b + 1) * LANES] = jnp.sum(total, axis=0, keepdims=True)
+
+
+def unpack(arrived):
+    return pl.pallas_call(
+        unpack_kernel,
+        out_shape=(
+            jax.ShapeDtypeStruct((TILES * FRAMES, PIXELS), jnp.bfloat16),
+            jax.ShapeDtypeStruct((1, TILES * FRAMES), jnp.float32),
+        ),
         in_specs=[VMEM],
-        out_specs=VMEM,
-        compiler_params=pltpu.CompilerParams(vmem_limit_bytes=2 << 20),
-        name="join",
-    )(pieces)
+        out_specs=(VMEM, VMEM),
+        compiler_params=pltpu.CompilerParams(vmem_limit_bytes=8 << 20),
+        name="unpack",
+    )(arrived)
 
 
 def moved(array, axis, by):
@@ -325,16 +339,14 @@
     where = jnp.stack([lax.axis_index(axis) for axis in ("ta_0", "ta_1", "row")]).astype(jnp.int32)
     packed = pack(neuron_ids[0], owner_order, footprint[0, 0], support[0, 0], start_traces.reshape(8, LANES))
     here = lax.all_to_all(packed, YZ, 0, 0, tiled=True)
-    tiled = filter_tiles(movie[0], shifts[0])
-    tile_movie = lax.all_to_all(tiled, TA, split_axis=0, concat_axis=0, tiled=True)
+    registered = register(movie[0], shifts[0])
     left, far, right = [moved(here, "ta_0", by) for by in range(1, PLANES)]
+    tiled = smooth(registered)
     mine = project(where, tiled, here, left, far, right)
     other = moved(mine, "row", 1)
-    pieces = solve(where, mine, other)
-    pieces = [pieces[0]] + [moved(pieces[k], "ta_0", k) for k in range(1, PLANES)]
-    pieces = merge(where, pieces)
-    pieces = lax.all_to_all(pieces.reshape(PLANE, 1, LANES), YZ, 0, 0, tiled=True)
-    traces = join(pieces.reshape(PLANE, LANES))
+    tiled = solve(where, mine, other, tiled)
+    arrived = lax.all_to_all(tiled, TA, split_axis=0, concat_axis=0, tiled=True)
+    tile_movie, traces = unpack(arrived)
     return (tile_movie.reshape(1, 1, -1, PIXELS), traces)
 
 

time: 113 us -> 100 us (0.88)
  the two profiles are of different devices: /device:TPU:32 before, /device:TPU:1 now
where the time goes in v5:
time: 100 us; the launch traced here: 99.9 us
  blocking collectives  45.5 us (46%)
  waiting for transfers between devices  21.5 us (22%)
  starting transfers between devices  17.9 us (18%)
  Pallas kernels  14.1 us (14%)
    all_to_all x1, blocking collectives, local(): arrived = lax.all_to_all(tiled, TA, split_axis=0, concat_axis=0, tiled=True)  45.5 us
    ppermute x4, waiting for transfers between devices, moved(): lax.ppermute(array, axis, [(i, (i + by) % count) for i in range(count)])  13.3 us
    all_to_all x1, starting transfers between devices, local(): here = lax.all_to_all(packed, YZ, 0, 0, tiled=True)  12 us
    all_to_all x1, waiting for transfers between devices, local(): here = lax.all_to_all(packed, YZ, 0, 0, tiled=True)  8.18 us
    ppermute x4, starting transfers between devices, moved(): lax.ppermute(array, axis, [(i, (i + by) % count) for i in range(count)])  5.85 us
    pallas_call x1, Pallas kernels, project(): pl.pallas_call(project_kernel, out_shape=jax.ShapeDtypeStruct((NEURONS, N...  3.99 us
    pallas_call x1, Pallas kernels, smooth(): pl.pallas_call(smooth_kernel, out_shape=jax.ShapeDtypeStruct((TILES, FRAM...  3.59 us
    pallas_call x1, Pallas kernels, solve(): pl.pallas_call(solve_kernel, out_shape=jax.ShapeDtypeStruct(tiled.shape,...  2.04 us
  transfers between devices with their start and end apart: 5, of which 5 were waited for; matrix products, arithmetic and copies ran while one was open for 0% of the time, Pallas kernels for 5%

profile of v5, /device:TPU:1, one launch (start us, length us, event | category | flops | bytes accessed | tf_op | source)
XLA Modules:
  0.0 99.9 jit_solution(11759620412216395623)
XLA Ops:
  0.6 0.0 copy-start.3
  0.6 0.0 copy-start
  0.7 1.7 %pack.1 = bf16[32,8,640]{2,1,0:T(8,128)(2,1)} custom-call(s32[1,8]{1,0:T(1,128)} %bitcast.16, s32[256]{0:T(256)} %order_ref.1, bf16[8,512]{1,0:T(8,128)(2,1)} %bitcast.14, s32[8,512]{1,0:T(8,128)} %bitcast.13, f32[8,128]{1,0:T(8,128)} %bitcast.15), custom_call_target="tpu_custom_call" | custom-call | flops 200000000 | bytes 200000 | tf_op jit(solution)/shard_map/pack/pallas_call | solution.py:191
  2.3 12.0 %all-to-all-start = ((bf16[32,8,640]{2,1,0:T(8,128)(2,1)}), bf16[32,8,640]{2,1,0:T(8,128)(2,1)S(1)}, u32[]{:S(2)}, u32[]{:S(2)}) async-start(bf16[32,8,640]{2,1,0:T(8,128)(2,1)} %pack.1), calls=%async_computation | async-start | bytes 655360 | tf_op jit(solution)/shard_map/all_to_all | solution.py:341
  14.4 0.0 copy-done.3
  14.4 0.1 copy.13.shifts_ref
  14.5 0.1 pad_add_fusion.where_ref
  14.5 0.0 copy-done
  14.6 1.8 %register.1.registered_ref = bf16[8,128,512]{2,1,0:T(8,128)(2,1)S(1)} custom-call(s32[8,4,2]{2,1,0:T(4,128)S(1)} %copy.13.shifts_ref, bf16[8,128,512]{2,1,0:T(8,128)(2,1)S(1)} %bitcast.10), custom_call_target="tpu_custom_call" | custom-call | flops 2000000000 | bytes 2000000 | tf_op jit(solution)/shard_map/register/pallas_call | solution.py:100
  16.4 8.2 %all-to-all-done.here_ref = bf16[32,8,640]{2,1,0:T(8,128)(2,1)S(1)} async-done(((bf16[32,8,640]{2,1,0:T(8,128)(2,1)}), bf16[32,8,640]{2,1,0:T(8,128)(2,1)S(1)}, u32[]{:S(2)}, u32[]{:S(2)}) %all-to-all-start) | async-done | bytes 327712 | tf_op jit(solution)/shard_map/all_to_all | solution.py:341
  24.6 2.5 %collective-permute-start.2 = (bf16[32,8,640]{2,1,0:T(8,128)(2,1)S(1)}, bf16[32,8,640]{2,1,0:T(8,128)(2,1)S(1)}, u32[]{:S(2)}, u32[]{:S(2)}) collective-permute-start(bf16[32,8,640]{2,1,0:T(8,128)(2,1)S(1)} %all-to-all-done.here_ref), channel_id=1, source_target_pairs={{0,192},{64,0},{128,64},{192,128},{1,193},{65,1},{129,65},{193,129... | collective-permute-start | bytes 983048 | tf_op jit(solution)/shard_map/ppermute | solution.py:335
  27.0 0.5 collective-permute-start.1
  27.6 0.6 collective-permute-start
  28.2 0.0 copy-done.1
  28.2 3.6 %smooth.1.tiled_ref = bf16[128,8,640]{2,1,0:T(8,128)(2,1)S(1)} custom-call(bf16[8,128,512]{2,1,0:T(8,128)(2,1)S(1)} %register.1.registered_ref, bf16[512,512]{1,0:T(8,128)(2,1)S(1)} %copy-done.1, bf16[128,128]{1,0:T(8,128)(2,1)S(1)} %copy-done.2), custom_call_target="tpu_custom_call" | custom-call | flops 4000000000 | bytes 3000000 | tf_op jit(solution)/shard_map/smooth/pallas_call | solution.py:157
  31.8 2.4 %collective-permute-done.2.right_ref = bf16[32,8,640]{2,1,0:T(8,128)(2,1)S(1)} collective-permute-done((bf16[32,8,640]{2,1,0:T(8,128)(2,1)S(1)}, bf16[32,8,640]{2,1,0:T(8,128)(2,1)S(1)}, u32[]{:S(2)}, u32[]{:S(2)}) %collective-permute-start.2) | collective-permute-done | bytes 327712 | tf_op jit(solution)/shard_map/ppermute | solution.py:335
  34.2 0.4 collective-permute-done.1.far_ref
  34.6 9.0 %collective-permute-done.left_ref = bf16[32,8,640]{2,1,0:T(8,128)(2,1)S(1)} collective-permute-done((bf16[32,8,640]{2,1,0:T(8,128)(2,1)S(1)}, bf16[32,8,640]{2,1,0:T(8,128)(2,1)S(1)}, u32[]{:S(2)}, u32[]{:S(2)}) %collective-permute-start) | collective-permute-done | bytes 327712 | tf_op jit(solution)/shard_map/ppermute | solution.py:335
  43.5 4.0 %project.1.mine_ref = f32[256,512]{1,0:T(8,128)S(1)} custom-call(s32[3]{0:T(128)S(1)} %pad_add_fusion.where_ref, bf16[128,8,640]{2,1,0:T(8,128)(2,1)S(1)} %smooth.1.tiled_ref, bf16[32,8,640]{2,1,0:T(8,128)(2,1)S(1)} %all-to-all-done.here_ref, bf16[32,8,640]{2,1,0:T(8,128)(2,1)S(1)} %collective-permute-done.left_ref, ...), custom_call_target="tpu_custom_call" | custom-call | flops 2000000000 | bytes 3000000 | tf_op jit(solution)/shard_map/project/pallas_call | solution.py:244
  47.5 2.3 %collective-permute-start.3 = (f32[256,512]{1,0:T(8,128)S(1)}, f32[256,512]{1,0:T(8,128)S(1)}, u32[]{:S(2)}, u32[]{:S(2)}) collective-permute-start(f32[256,512]{1,0:T(8,128)S(1)} %project.1.mine_ref), channel_id=1, source_target_pairs={{0,1},{1,0},{2,3},{3,2},{4,5},{5,4},{6,7},{7,6},{8,9},{9,8},{10,11... | collective-permute-start | bytes 1572872 | tf_op jit(solution)/shard_map/ppermute | solution.py:335
  49.8 1.5 %collective-permute-done.3.other_ref = f32[256,512]{1,0:T(8,128)S(1)} collective-permute-done((f32[256,512]{1,0:T(8,128)S(1)}, f32[256,512]{1,0:T(8,128)S(1)}, u32[]{:S(2)}, u32[]{:S(2)}) %collective-permute-start.3) | collective-permute-done | bytes 524320 | tf_op jit(solution)/shard_map/ppermute | solution.py:335
  51.3 2.0 %solve.1 = bf16[128,8,640]{2,1,0:T(8,128)(2,1)S(1)} custom-call(s32[3]{0:T(128)S(1)} %pad_add_fusion.where_ref, f32[256,512]{1,0:T(8,128)S(1)} %project.1.mine_ref, f32[256,512]{1,0:T(8,128)S(1)} %collective-permute-done.3.other_ref, bf16[128,8,640]{2,1,0:T(8,128)(2,1)S(1)} %smooth.1.tiled_ref), custom_call_target="tpu_custom_call", output_to_operand_aliasing={{}: (3, {})} | custom-call | flops 2000000000 | bytes 1000000 | tf_op jit(solution)/shard_map/solve/pallas_call | solution.py:291
  53.4 45.5 %all_to_all.10.arrived_ref = bf16[128,8,640]{2,1,0:T(8,128)(2,1)S(1)} all-to-all(bf16[128,8,640]{2,1,0:T(8,128)(2,1)S(1)} %solve.1), channel_id=1, replica_groups=mesh['ta_0'=4,'ta_1'=4,'ta_2'=8,'row'=2] {'ta_0','ta_1','ta_2'}, dimensions={0} | all-to-all | bytes 2621440 | tf_op jit(solution)/shard_map/all_to_all | solution.py:348
  98.9 1.0 %unpack.1 = (bf16[1024,512]{1,0:T(8,128)(2,1)}, f32[1,1024]{1,0:T(1,128)}) custom-call(bf16[128,8,640]{2,1,0:T(8,128)(2,1)S(1)} %all_to_all.10.arrived_ref), custom_call_target="tpu_custom_call" | custom-call | tf_op jit(solution)/shard_map/unpack/pallas_call | solution.py:320
  (3 shorter events, 0.0 us)
Async XLA Ops:
  0.6 13.7 %copy-start.3 = (s32[1,8,4,2]{1,3,2,0:T(2,128)S(1)}, s32[1,8,4,2]{1,3,2,0:T(2,128)}, u32[]{:S(2)}) copy-start(s32[1,8,4,2]{1,3,2,0:T(2,128)} %param.10) | copy-start | bytes 772
  0.6 13.9 %copy-start = (bf16[1,8,128,512]{3,2,1,0:T(8,128)(2,1)S(1)}, bf16[1,8,128,512]{3,2,1,0:T(8,128)(2,1)}, u32[]{:S(2)}) copy-start(bf16[1,8,128,512]{3,2,1,0:T(8,128)(2,1)} %param.9) | copy-start | bytes 3145732
  2.3 22.2 %all-to-all-start = ((bf16[32,8,640]{2,1,0:T(8,128)(2,1)}), bf16[32,8,640]{2,1,0:T(8,128)(2,1)S(1)}, u32[]{:S(2)}, u32[]{:S(2)}) async-start(bf16[32,8,640]{2,1,0:T(8,128)(2,1)} %pack.1), calls=%async_computation | async-start | bytes 655360 | tf_op jit(solution)/shard_map/all_to_all | solution.py:341
  14.5 13.6 %copy-start.1 = (bf16[512,512]{1,0:T(8,128)(2,1)S(1)}, bf16[512,512]{1,0:T(8,128)(2,1)}, u32[]{:S(2)}) copy-start(bf16[512,512]{1,0:T(8,128)(2,1)} %constant.18.clone.wide_ref) | copy-start | bytes 1572868
  14.5 13.6 %copy-start.2 = (bf16[128,128]{1,0:T(8,128)(2,1)S(1)}, bf16[128,128]{1,0:T(8,128)(2,1)}, u32[]{:S(2)}) copy-start(bf16[128,128]{1,0:T(8,128)(2,1)} %constant.19.clone.tall_ref) | copy-start | bytes 98308
  24.6 9.6 %collective-permute-start.2 = (bf16[32,8,640]{2,1,0:T(8,128)(2,1)S(1)}, bf16[32,8,640]{2,1,0:T(8,128)(2,1)S(1)}, u32[]{:S(2)}, u32[]{:S(2)}) collective-permute-start(bf16[32,8,640]{2,1,0:T(8,128)(2,1)S(1)} %all-to-all-done.here_ref), channel_id=1, source_target_pairs={{0,192},{64,0},{128,64},{192,128},{1,193},{65,1},{129,65},{193,129... | collective-permute-start | bytes 983048 | tf_op jit(solution)/shard_map/ppermute | solution.py:335
  27.0 7.5 %collective-permute-start.1 = (bf16[32,8,640]{2,1,0:T(8,128)(2,1)S(1)}, bf16[32,8,640]{2,1,0:T(8,128)(2,1)S(1)}, u32[]{:S(2)}, u32[]{:S(2)}) collective-permute-start(bf16[32,8,640]{2,1,0:T(8,128)(2,1)S(1)} %all-to-all-done.here_ref), channel_id=1, source_target_pairs={{0,128},{64,192},{128,0},{192,64},{1,129},{65,193},{129,1},{193,65... | collective-permute-start | bytes 983048 | tf_op jit(solution)/shard_map/ppermute | solution.py:335
  27.6 16.0 %collective-permute-start = (bf16[32,8,640]{2,1,0:T(8,128)(2,1)S(1)}, bf16[32,8,640]{2,1,0:T(8,128)(2,1)S(1)}, u32[]{:S(2)}, u32[]{:S(2)}) collective-permute-start(bf16[32,8,640]{2,1,0:T(8,128)(2,1)S(1)} %all-to-all-done.here_ref), channel_id=1, source_target_pairs={{0,64},{64,128},{128,192},{192,0},{1,65},{65,129},{129,193},{193,1... | collective-permute-start | bytes 983048 | tf_op jit(solution)/shard_map/ppermute | solution.py:335
  47.5 3.8 %collective-permute-start.3 = (f32[256,512]{1,0:T(8,128)S(1)}, f32[256,512]{1,0:T(8,128)S(1)}, u32[]{:S(2)}, u32[]{:S(2)}) collective-permute-start(f32[256,512]{1,0:T(8,128)S(1)} %project.1.mine_ref), channel_id=1, source_target_pairs={{0,1},{1,0},{2,3},{3,2},{4,5},{5,4},{6,7},{7,6},{8,9},{9,8},{10,11... | collective-permute-start | bytes 1572872 | tf_op jit(solution)/shard_map/ppermute | solution.py:335

commit v6 on v4

--- a/solution.py
+++ b/solution.py
@@ -13,6 +13,7 @@
 ITERS = 2
 TA = ("ta_0", "ta_1", "ta_2")
 YZ = ("ta_1", "ta_2")
+ZYX = ("ta_2", "ta_1", "ta_0")
 TA_ROW = ("ta_0", "ta_1", "ta_2", "row")
 
 FRAMES = 8
@@ -61,42 +62,69 @@
     return dot32(high, exact) + (dot32(mid, exact) + dot32(low, exact))
 
 
-def filter_kernel(
-    shifts_ref, movie_ref, wide_ref, tall_ref, out_ref, padded_ref, registered_ref, filtered_ref,
-):
+def register_kernel(shifts_ref, movie_ref, out_ref, padded_ref):
     lane = iota((H, LANES), 1)
-    padded_ref[:, pl.ds(0, MAXS), :] = jnp.zeros((BLOCKS, MAXS, LANES), jnp.float32)
-    padded_ref[:, pl.ds(MAXS + H, MAXS), :] = jnp.zeros((BLOCKS, MAXS, LANES), jnp.float32)
+    for s in range(2 * BLOCKS):
+        padded_ref[s, pl.ds(0, MAXS), :] = jnp.zeros((MAXS, LANES), jnp.float32)
+        padded_ref[s, pl.ds(MAXS + H, MAXS), :] = jnp.zeros((MAXS, LANES), jnp.float32)
 
     def block(f, p):
         if p < 0 or p >= BLOCKS:
             return None
         return movie_ref[f, :, p * LANES : (p + 1) * LANES].astype(jnp.float32)
 
-    def frame(f, carry):
-        for p in range(BLOCKS):
-            dy = shifts_ref[f, p, 0]
-            dx = shifts_ref[f, p, 1]
-            amount = jnp.where(dx > 0, LANES - dx, -dx)
-            source = lane + dx
-
-            def rolled(value):
-                if value is None:
-                    return jnp.zeros((H, LANES), jnp.float32)
-                return pltpu.roll(value, amount, 1)
-
-            inner = jnp.where(source >= LANES, rolled(block(f, p + 1)), rolled(block(f, p)))
-            moved = jnp.where(source < 0, rolled(block(f, p - 1)), inner)
-            padded_ref[p, pl.ds(MAXS, H), :] = moved
-            registered_ref[:, p * LANES : (p + 1) * LANES] = padded_ref[p, pl.ds(MAXS + dy, H), :]
-        registered = registered_ref[...]
-        wide = dot32(registered.astype(jnp.bfloat16), wide_ref[...]).astype(jnp.bfloat16)
-        filtered = registered - dot32(tall_ref[...], wide)
-        for p in range(BLOCKS):
-            filtered_ref[p, pl.ds(f, H, stride=FRAMES), :] = filtered[:, p * LANES : (p + 1) * LANES]
+    def shift(f, p, s):
+        dy = shifts_ref[f, p, 0]
+        dx = shifts_ref[f, p, 1]
+        amount = jnp.where(dx > 0, LANES - dx, -dx)
+        source = lane + dx
+
+        def rolled(value):
+            if value is None:
+                return jnp.zeros((H, LANES), jnp.float32)
+            return pltpu.roll(value, amount, 1)
+
+        inner = jnp.where(source >= LANES, rolled(block(f, p + 1)), rolled(block(f, p)))
+        padded_ref[s, pl.ds(MAXS, H), :] = jnp.where(source < 0, rolled(block(f, p - 1)), inner)
+        out_ref[f, :, p * LANES : (p + 1) * LANES] = padded_ref[s, pl.ds(MAXS + dy, H), :].astype(jnp.bfloat16)
+
+    def frames(g, carry):
+        for h in range(2):
+            for p in range(BLOCKS):
+                shift(2 * g + h, p, h * BLOCKS + p)
         return carry
 
-    lax.fori_loop(0, FRAMES, frame, 0)
+    lax.fori_loop(0, FRAMES // 2, frames, 0)
+
+
+def register(movie, shifts):
+    return pl.pallas_call(
+        register_kernel,
+        out_shape=jax.ShapeDtypeStruct((FRAMES, H, W), jnp.bfloat16),
+        in_specs=[SMEM, VMEM],
+        out_specs=VMEM,
+        scratch_shapes=[pltpu.VMEM((2 * BLOCKS, H + 2 * MAXS, LANES), jnp.float32)],
+        cost_estimate=pl.CostEstimate(flops=2_000_000_000, bytes_accessed=2_000_000, transcendentals=0),
+        compiler_params=pltpu.CompilerParams(vmem_limit_bytes=8 << 20),
+        name="register",
+    )(shifts, movie)
+
+
+def smooth_kernel(registered_ref, wide_ref, tall_ref, out_ref, filtered_ref, soft_ref):
+    step = 2
+
+    def chunk(c, carry):
+        registered = registered_ref[pl.ds(c * step, step)].reshape(step * H, W)
+        soft_ref[...] = dot32(registered, wide_ref[...]).astype(jnp.bfloat16)
+        for k in range(step):
+            low = dot32(tall_ref[...], soft_ref[k * H : (k + 1) * H, :])
+            filtered = registered[k * H : (k + 1) * H].astype(jnp.float32) - low
+            for p in range(BLOCKS):
+                span = pl.ds(c * step + k, H, stride=FRAMES)
+                filtered_ref[p, span, :] = filtered[:, p * LANES : (p + 1) * LANES]
+        return carry
+
+    lax.fori_loop(0, FRAMES // step, chunk, 0)
     lanes8 = iota((FRAMES, LANES), 1)
     near = lanes8 < 2 * TW
     even = lax.rem(lanes8 // TW, 2) == 0
@@ -119,27 +147,28 @@
                     jnp.where(even, pltpu.roll(a2, 96, 1), a3),
                 )
                 for m in range(4):
-                    out_ref[ty * 16 + 4 * p + m, :, q * LANES : (q + 1) * LANES] = tiles[m].astype(jnp.bfloat16)
+                    column = 4 * p + m
+                    at = (column % 8) * 16 + (2 * lax.rem(ty, 2) + column // 8) * 4 + ty // 2
+                    out_ref[at, :, q * LANES : (q + 1) * LANES] = tiles[m].astype(jnp.bfloat16)
         return carry
 
     lax.fori_loop(0, H // TH, tile_row, 0)
 
 
-def filter_tiles(movie, shifts):
-    return pl.pallas_call(
-        filter_kernel,
+def smooth(registered):
+    return pl.pallas_call(
+        smooth_kernel,
         out_shape=jax.ShapeDtypeStruct((TILES, FRAMES, PIXELS), jnp.bfloat16),
-        in_specs=[SMEM, VMEM, VMEM, VMEM],
+        in_specs=[VMEM] * 3,
         out_specs=VMEM,
         scratch_shapes=[
-            pltpu.VMEM((BLOCKS, H + 2 * MAXS, LANES), jnp.float32),
-            pltpu.VMEM((H, W), jnp.float32),
             pltpu.VMEM((BLOCKS, H * FRAMES, LANES), jnp.float32),
+            pltpu.VMEM((2 * H, W), jnp.bfloat16),
         ],
         cost_estimate=pl.CostEstimate(flops=4_000_000_000, bytes_accessed=3_000_000, transcendentals=0),
         compiler_params=pltpu.CompilerParams(vmem_limit_bytes=16 << 20),
-        name="filter",
-    )(shifts, movie, smoothing_table(W), smoothing_table(H).T)
+        name="smooth",
+    )(registered, smoothing_table(W), smoothing_table(H).T)
 
 
 def pack_kernel(ids_ref, order_ref, footprint_ref, support_ref, start_ref, out_ref):
@@ -188,12 +217,13 @@
     for at in range(2 * PLANES):
         kx, first = at // 2, many * (at % 2)
         message = (here_ref, left_ref, far_ref, right_ref)[kx][first : first + many]
-        tile = pl.multiple_of(PLANE * lax.rem(x + PLANES - kx, PLANES) + first, many)
-        frames = tiled_ref[pl.ds(tile, many)].reshape(rows, PIXELS)
+        source = lax.rem(x + PLANES - kx, PLANES)
+        tile = pl.multiple_of(PLANE * source + first, many)
+        frames = [tiled_ref[(k % 8) * 16 + (first // 8 + k // 8) * 4 + source] for k in range(many)]
         prints = message[:, :, :PIXELS].reshape(rows, PIXELS)
         extra = message[:, :, PIXELS:].astype(jnp.float32).reshape(rows, LANES)
         found = lax.dot_general(
-            prints, jnp.concatenate([frames, prints], axis=0), contract, preferred_element_type=jnp.float32
+            prints, jnp.concatenate(frames + [prints], axis=0), contract, preferred_element_type=jnp.float32
         )
         found = jnp.where(same, found, 0.0)
         ids = extra[:, ID_LANE : ID_LANE + 1]
@@ -316,6 +346,30 @@
     )(pieces)
 
 
+def store_kernel(arrived_ref, out_ref, sems):
+    copies = []
+    for x in range(4):
+        for y in range(4):
+            copies.append(pltpu.make_async_copy(arrived_ref.at[:, y, x], out_ref.at[x, y], sems.at[4 * x + y]))
+    for copy in copies:
+        copy.start()
+    for copy in copies:
+        copy.wait()
+
+
+def store(arrived):
+    return pl.pallas_call(
+        store_kernel,
+        out_shape=jax.ShapeDtypeStruct((4, 4, 8, FRAMES, PIXELS), jnp.bfloat16),
+        in_specs=[VMEM],
+        out_specs=pl.BlockSpec(memory_space=pl.ANY),
+        scratch_shapes=[pltpu.SemaphoreType.DMA((16,))],
+        cost_estimate=pl.CostEstimate(flops=500_000_000, bytes_accessed=2_000_000, transcendentals=0),
+        compiler_params=pltpu.CompilerParams(vmem_limit_bytes=4 << 20),
+        name="store",
+    )(arrived.reshape(8, 4, 4, FRAMES, PIXELS))
+
+
 def moved(array, axis, by):
     count = lax.axis_size(axis)
     return lax.ppermute(array, axis, [(i, (i + by) % count) for i in range(count)])
@@ -325,8 +379,9 @@
     where = jnp.stack([lax.axis_index(axis) for axis in ("ta_0", "ta_1", "row")]).astype(jnp.int32)
     packed = pack(neuron_ids[0], owner_order, footprint[0, 0], support[0, 0], start_traces.reshape(8, LANES))
     here = lax.all_to_all(packed, YZ, 0, 0, tiled=True)
-    tiled = filter_tiles(movie[0], shifts[0])
-    tile_movie = lax.all_to_all(tiled, TA, split_axis=0, concat_axis=0, tiled=True)
+    registered = register(movie[0], shifts[0])
+    tiled = smooth(registered)
+    arrived = lax.all_to_all(tiled, ZYX, split_axis=0, concat_axis=0, tiled=True)
     left, far, right = [moved(here, "ta_0", by) for by in range(1, PLANES)]
     mine = project(where, tiled, here, left, far, right)
     other = moved(mine, "row", 1)
@@ -334,6 +389,7 @@
     pieces = [pieces[0]] + [moved(pieces[k], "ta_0", k) for k in range(1, PLANES)]
     pieces = merge(where, pieces)
     pieces = lax.all_to_all(pieces.reshape(PLANE, 1, LANES), YZ, 0, 0, tiled=True)
+    tile_movie = store(arrived)
     traces = join(pieces.reshape(PLANE, LANES))
     return (tile_movie.reshape(1, 1, -1, PIXELS), traces)
 

time: 113 us -> 113 us (level)
  waiting for transfers between devices: 52 us -> 53.4 us
  local copies, waits for them, and re-layouts: 2.13 us -> 0.8 us
    ppermute x7, waiting for transfers between devices: 10.6 us -> 14.5 us  [moved(): lax.ppermute(array, axis, [(i, (i + by) % count) for i in range(count)])]
    all_to_all x1, waiting for transfers between devices: 13.4 us -> 10.9 us  [local(): here = lax.all_to_all(packed, YZ, 0, 0, tiled=True)]
    unnamed x9 -> x8, local copies, waits for them, and re-layouts: 2.03 us -> 0.69 us
    pallas_call x1 -> x3, Pallas kernels: 7.41 us -> 7.44 us  [the longest x1 4.54 us: smooth(): pl.pallas_call(smooth_kernel, out_shape=jax.ShapeDtypeStruct((TILES, FRAM...]
  transfers between devices with their start and end apart: 9 -> 9, of which waited for: 8 -> 8; matrix products, arithmetic and copies ran while one was open for 0% -> 0% of each run, Pallas kernels for 7% -> 6%
where the time goes in v6:
time: 113 us; the launch traced here: 112 us
  waiting for transfers between devices  53.4 us (47%)
  starting transfers between devices  26.8 us (24%)
  Pallas kernels  16.9 us (15%)
  blocking collectives  13.7 us (12%)
    all_to_all x1, waiting for transfers between devices, local(): lax.all_to_all(tiled, ZYX, split_axis=0, concat_axis=0, tiled=True)  28 us
    ppermute x7, waiting for transfers between devices, moved(): lax.ppermute(array, axis, [(i, (i + by) % count) for i in range(count)])  14.5 us
    all_to_all x1, blocking collectives, local(): lax.all_to_all(pieces.reshape(PLANE, 1, LANES), YZ, 0, 0, tiled=True)  13.7 us
    all_to_all x1, starting transfers between devices, local(): here = lax.all_to_all(packed, YZ, 0, 0, tiled=True)  11.4 us
    all_to_all x1, waiting for transfers between devices, local(): here = lax.all_to_all(packed, YZ, 0, 0, tiled=True)  10.9 us
    ppermute x7, starting transfers between devices, moved(): lax.ppermute(array, axis, [(i, (i + by) % count) for i in range(count)])  8.05 us
    all_to_all x1, starting transfers between devices, local(): lax.all_to_all(tiled, ZYX, split_axis=0, concat_axis=0, tiled=True)  7.38 us
    pallas_call x1, Pallas kernels, project(): pl.pallas_call(project_kernel, out_shape=jax.ShapeDtypeStruct((NEURONS, N...  4.7 us
  transfers between devices with their start and end apart: 9, of which 8 were waited for; matrix products, arithmetic and copies ran while one was open for 0% of the time, Pallas kernels for 6%

profile of v6, /device:TPU:32, one launch (start us, length us, event | category | flops | bytes accessed | tf_op | source)
XLA Modules:
  0.0 112.4 jit_solution(11828232780317540540)
XLA Ops:
  0.6 1.7 %pack.1 = bf16[32,8,640]{2,1,0:T(8,128)(2,1)} custom-call(s32[1,8]{1,0:T(1,128)} %bitcast.24, s32[256]{0:T(256)} %order_ref.1, bf16[8,512]{1,0:T(8,128)(2,1)} %bitcast.22, s32[8,512]{1,0:T(8,128)} %bitcast.21, f32[8,128]{1,0:T(8,128)} %bitcast.23), custom_call_target="tpu_custom_call" | custom-call | flops 200000000 | bytes 200000 | tf_op jit(solution)/shard_map/pack/pallas_call | solution.py:193
  2.3 11.4 %all-to-all-start.1 = ((bf16[32,8,640]{2,1,0:T(8,128)(2,1)}), bf16[32,8,640]{2,1,0:T(8,128)(2,1)S(1)}, u32[]{:S(2)}, u32[]{:S(2)}) async-start(bf16[32,8,640]{2,1,0:T(8,128)(2,1)} %pack.1), calls=%async_computation.1 | async-start | bytes 655360 | tf_op jit(solution)/shard_map/all_to_all | solution.py:381
  13.7 0.7 copy-done.3
  14.6 1.8 %register.1.registered_ref = bf16[8,128,512]{2,1,0:T(8,128)(2,1)S(1)} custom-call(s32[8,4,2]{2,1,0:T(4,128)S(1)} %copy.14.shifts_ref, bf16[8,128,512]{2,1,0:T(8,128)(2,1)S(1)} %bitcast.18), custom_call_target="tpu_custom_call" | custom-call | flops 2000000000 | bytes 2000000 | tf_op jit(solution)/shard_map/register/pallas_call | solution.py:101
  16.4 10.9 %all-to-all-done.1.here_ref = bf16[32,8,640]{2,1,0:T(8,128)(2,1)S(1)} async-done(((bf16[32,8,640]{2,1,0:T(8,128)(2,1)}), bf16[32,8,640]{2,1,0:T(8,128)(2,1)S(1)}, u32[]{:S(2)}, u32[]{:S(2)}) %all-to-all-start.1) | async-done | bytes 327712 | tf_op jit(solution)/shard_map/all_to_all | solution.py:381
  27.3 2.8 %collective-permute-start.2 = (bf16[32,8,640]{2,1,0:T(8,128)(2,1)S(1)}, bf16[32,8,640]{2,1,0:T(8,128)(2,1)S(1)}, u32[]{:S(2)}, u32[]{:S(2)}) collective-permute-start(bf16[32,8,640]{2,1,0:T(8,128)(2,1)S(1)} %all-to-all-done.1.here_ref), channel_id=1, source_target_pairs={{0,192},{64,0},{128,64},{192,128},{1,193},{65,1},{129,65},{193,129... | collective-permute-start | bytes 983048 | tf_op jit(solution)/shard_map/ppermute | solution.py:375
  30.0 0.8 collective-permute-start.1
  30.8 0.9 collective-permute-start
  31.7 4.5 %smooth.1.tiled_ref = bf16[128,8,512]{2,1,0:T(8,128)(2,1)} custom-call(bf16[8,128,512]{2,1,0:T(8,128)(2,1)S(1)} %register.1.registered_ref, bf16[512,512]{1,0:T(8,128)(2,1)S(1)} %copy-done.1, bf16[128,128]{1,0:T(8,128)(2,1)S(1)} %copy-done.2), custom_call_target="tpu_custom_call" | custom-call | flops 4000000000 | bytes 3000000 | tf_op jit(solution)/shard_map/smooth/pallas_call | solution.py:159
  36.2 6.4 %collective-permute-done.2.right_ref = bf16[32,8,640]{2,1,0:T(8,128)(2,1)S(1)} collective-permute-done((bf16[32,8,640]{2,1,0:T(8,128)(2,1)S(1)}, bf16[32,8,640]{2,1,0:T(8,128)(2,1)S(1)}, u32[]{:S(2)}, u32[]{:S(2)}) %collective-permute-start.2) | collective-permute-done | bytes 327712 | tf_op jit(solution)/shard_map/ppermute | solution.py:375
  42.6 3.7 %collective-permute-done.left_ref = bf16[32,8,640]{2,1,0:T(8,128)(2,1)S(1)} collective-permute-done((bf16[32,8,640]{2,1,0:T(8,128)(2,1)S(1)}, bf16[32,8,640]{2,1,0:T(8,128)(2,1)S(1)}, u32[]{:S(2)}, u32[]{:S(2)}) %collective-permute-start) | collective-permute-done | bytes 327712 | tf_op jit(solution)/shard_map/ppermute | solution.py:375
  46.3 4.7 %project.1.mine_ref = f32[256,512]{1,0:T(8,128)S(1)} custom-call(s32[3]{0:T(128)S(1)} %pad_add_fusion.where_ref, bf16[128,8,512]{2,1,0:T(8,128)(2,1)} %smooth.1.tiled_ref, bf16[32,8,640]{2,1,0:T(8,128)(2,1)S(1)} %all-to-all-done.1.here_ref, bf16[32,8,640]{2,1,0:T(8,128)(2,1)S(1)} %collective-permute-done.left_ref, ...), custom_call_target="tpu_custom_call" | custom-call | flops 2000000000 | bytes 3000000 | tf_op jit(solution)/shard_map/project/pallas_call | solution.py:247
  51.1 1.9 %collective-permute-done.3.other_ref = f32[256,512]{1,0:T(8,128)S(1)} collective-permute-done((f32[256,512]{1,0:T(8,128)S(1)}, f32[256,512]{1,0:T(8,128)S(1)}, u32[]{:S(2)}, u32[]{:S(2)}) %collective-permute-start.3) | collective-permute-done | bytes 524320 | tf_op jit(solution)/shard_map/ppermute | solution.py:375
  53.0 1.9 %solve.1 = (f32[32,128]{1,0:T(8,128)S(1)}, f32[32,128]{1,0:T(8,128)S(1)}, f32[32,128]{1,0:T(8,128)S(1)}, f32[32,128]{1,0:T(8,128)S(1)}) custom-call(s32[3]{0:T(128)S(1)} %pad_add_fusion.where_ref, f32[256,512]{1,0:T(8,128)S(1)} %project.1.mine_ref, f32[256,512]{1,0:T(8,128)S(1)} %collective-permute-done.3.other_ref), custom_call_target="tpu_custom_call" | custom-call | flops 2000000000 | bytes 1000000 | tf_op jit(solution)/shard_map/solve/pallas_call | solution.py:291
  55.0 2.1 %collective-permute-start.5 = (f32[32,128]{1,0:T(8,128)S(1)}, f32[32,128]{1,0:T(8,128)S(1)}, u32[]{:S(2)}, u32[]{:S(2)}) collective-permute-start(f32[32,128]{1,0:T(8,128)S(1)} %get-tuple-element.8), channel_id=1, source_target_pairs={{0,128},{64,192},{128,0},{192,64},{1,129},{65,193},{129,1},{193,65... | collective-permute-start | bytes 49160 | tf_op jit(solution)/shard_map/ppermute | solution.py:375
  57.0 1.4 %collective-permute-start.6 = (f32[32,128]{1,0:T(8,128)S(1)}, f32[32,128]{1,0:T(8,128)S(1)}, u32[]{:S(2)}, u32[]{:S(2)}) collective-permute-start(f32[32,128]{1,0:T(8,128)S(1)} %get-tuple-element.9), channel_id=1, source_target_pairs={{0,192},{64,0},{128,64},{192,128},{1,193},{65,1},{129,65},{193,129... | collective-permute-start | bytes 49160 | tf_op jit(solution)/shard_map/ppermute | solution.py:375
  58.4 1.5 %collective-permute-done.4.refs_1_ = f32[32,128]{1,0:T(8,128)S(1)} collective-permute-done((f32[32,128]{1,0:T(8,128)S(1)}, f32[32,128]{1,0:T(8,128)S(1)}, u32[]{:S(2)}, u32[]{:S(2)}) %collective-permute-start.4) | collective-permute-done | bytes 16416 | tf_op jit(solution)/shard_map/ppermute | solution.py:375
  60.3 0.6 collective-permute-done.6.refs_3_
  60.9 0.6 merge.1
  61.5 13.7 %all_to_all.15 = f32[32,1,128]{2,1,0:T(1,128)S(1)} all-to-all(f32[32,1,128]{2,1,0:T(1,128)S(1)} %bitcast.17), channel_id=1, replica_groups=mesh['ta_0'=4,'ta_1'=4,'ta_2'=8,'row'=2] {'ta_1','ta_2'}, dimensions={0} | all-to-all | bytes 32768 | tf_op jit(solution)/shard_map/all_to_all | solution.py:391
  75.2 7.4 %all-to-all-start = ((bf16[128,8,512]{2,1,0:T(8,128)(2,1)}), bf16[128,8,512]{2,1,0:T(8,128)(2,1)S(1)}, u32[]{:S(2)}, u32[]{:S(2)}) async-start(bf16[128,8,512]{2,1,0:T(8,128)(2,1)} %smooth.1.tiled_ref), calls=%async_computation | async-start | bytes 2097152 | tf_op jit(solution)/shard_map/all_to_all | solution.py:384
  82.6 0.7 join.1
  83.3 28.0 %all-to-all-done = bf16[128,8,512]{2,1,0:T(8,128)(2,1)S(1)} async-done(((bf16[128,8,512]{2,1,0:T(8,128)(2,1)}), bf16[128,8,512]{2,1,0:T(8,128)(2,1)S(1)}, u32[]{:S(2)}, u32[]{:S(2)}) %all-to-all-start) | async-done | bytes 1048608 | tf_op jit(solution)/shard_map/all_to_all | solution.py:384
  111.3 1.1 store.1
  (13 shorter events, 0.8 us)
Async XLA Ops:
  0.6 13.9 %copy-start = (bf16[1,8,128,512]{3,2,1,0:T(8,128)(2,1)S(1)}, bf16[1,8,128,512]{3,2,1,0:T(8,128)(2,1)}, u32[]{:S(2)}) copy-start(bf16[1,8,128,512]{3,2,1,0:T(8,128)(2,1)} %param.9) | copy-start | bytes 3145732
  2.3 24.9 %all-to-all-start.1 = ((bf16[32,8,640]{2,1,0:T(8,128)(2,1)}), bf16[32,8,640]{2,1,0:T(8,128)(2,1)S(1)}, u32[]{:S(2)}, u32[]{:S(2)}) async-start(bf16[32,8,640]{2,1,0:T(8,128)(2,1)} %pack.1), calls=%async_computation.1 | async-start | bytes 655360 | tf_op jit(solution)/shard_map/all_to_all | solution.py:381
  13.7 0.7 copy-start.3
  14.5 17.2 %copy-start.1 = (bf16[512,512]{1,0:T(8,128)(2,1)S(1)}, bf16[512,512]{1,0:T(8,128)(2,1)}, u32[]{:S(2)}) copy-start(bf16[512,512]{1,0:T(8,128)(2,1)} %constant.18.clone.wide_ref) | copy-start | bytes 1572868
  14.5 17.2 %copy-start.2 = (bf16[128,128]{1,0:T(8,128)(2,1)S(1)}, bf16[128,128]{1,0:T(8,128)(2,1)}, u32[]{:S(2)}) copy-start(bf16[128,128]{1,0:T(8,128)(2,1)} %constant.19.clone.tall_ref) | copy-start | bytes 98308
  27.3 15.3 %collective-permute-start.2 = (bf16[32,8,640]{2,1,0:T(8,128)(2,1)S(1)}, bf16[32,8,640]{2,1,0:T(8,128)(2,1)S(1)}, u32[]{:S(2)}, u32[]{:S(2)}) collective-permute-start(bf16[32,8,640]{2,1,0:T(8,128)(2,1)S(1)} %all-to-all-done.1.here_ref), channel_id=1, source_target_pairs={{0,192},{64,0},{128,64},{192,128},{1,193},{65,1},{129,65},{193,129... | collective-permute-start | bytes 983048 | tf_op jit(solution)/shard_map/ppermute | solution.py:375
  30.0 12.6 %collective-permute-start.1 = (bf16[32,8,640]{2,1,0:T(8,128)(2,1)S(1)}, bf16[32,8,640]{2,1,0:T(8,128)(2,1)S(1)}, u32[]{:S(2)}, u32[]{:S(2)}) collective-permute-start(bf16[32,8,640]{2,1,0:T(8,128)(2,1)S(1)} %all-to-all-done.1.here_ref), channel_id=1, source_target_pairs={{0,128},{64,192},{128,0},{192,64},{1,129},{65,193},{129,1},{193,65... | collective-permute-start | bytes 983048 | tf_op jit(solution)/shard_map/ppermute | solution.py:375
  30.8 15.5 %collective-permute-start = (bf16[32,8,640]{2,1,0:T(8,128)(2,1)S(1)}, bf16[32,8,640]{2,1,0:T(8,128)(2,1)S(1)}, u32[]{:S(2)}, u32[]{:S(2)}) collective-permute-start(bf16[32,8,640]{2,1,0:T(8,128)(2,1)S(1)} %all-to-all-done.1.here_ref), channel_id=1, source_target_pairs={{0,64},{64,128},{128,192},{192,0},{1,65},{65,129},{129,193},{193,1... | collective-permute-start | bytes 983048 | tf_op jit(solution)/shard_map/ppermute | solution.py:375
  51.0 2.0 %collective-permute-start.3 = (f32[256,512]{1,0:T(8,128)S(1)}, f32[256,512]{1,0:T(8,128)S(1)}, u32[]{:S(2)}, u32[]{:S(2)}) collective-permute-start(f32[256,512]{1,0:T(8,128)S(1)} %project.1.mine_ref), channel_id=1, source_target_pairs={{0,1},{1,0},{2,3},{3,2},{4,5},{5,4},{6,7},{7,6},{8,9},{9,8},{10,11... | collective-permute-start | bytes 1572872 | tf_op jit(solution)/shard_map/ppermute | solution.py:375
  54.9 5.0 %collective-permute-start.4 = (f32[32,128]{1,0:T(8,128)S(1)}, f32[32,128]{1,0:T(8,128)S(1)}, u32[]{:S(2)}, u32[]{:S(2)}) collective-permute-start(f32[32,128]{1,0:T(8,128)S(1)} %get-tuple-element.7), channel_id=1, source_target_pairs={{0,64},{64,128},{128,192},{192,0},{1,65},{65,129},{129,193},{193,1... | collective-permute-start | bytes 49160 | tf_op jit(solution)/shard_map/ppermute | solution.py:375
  55.0 5.3 %collective-permute-start.5 = (f32[32,128]{1,0:T(8,128)S(1)}, f32[32,128]{1,0:T(8,128)S(1)}, u32[]{:S(2)}, u32[]{:S(2)}) collective-permute-start(f32[32,128]{1,0:T(8,128)S(1)} %get-tuple-element.8), channel_id=1, source_target_pairs={{0,128},{64,192},{128,0},{192,64},{1,129},{65,193},{129,1},{193,65... | collective-permute-start | bytes 49160 | tf_op jit(solution)/shard_map/ppermute | solution.py:375
  57.0 3.9 %collective-permute-start.6 = (f32[32,128]{1,0:T(8,128)S(1)}, f32[32,128]{1,0:T(8,128)S(1)}, u32[]{:S(2)}, u32[]{:S(2)}) collective-permute-start(f32[32,128]{1,0:T(8,128)S(1)} %get-tuple-element.9), channel_id=1, source_target_pairs={{0,192},{64,0},{128,64},{192,128},{1,193},{65,1},{129,65},{193,129... | collective-permute-start | bytes 49160 | tf_op jit(solution)/shard_map/ppermute | solution.py:375
  75.2 36.1 %all-to-all-start = ((bf16[128,8,512]{2,1,0:T(8,128)(2,1)}), bf16[128,8,512]{2,1,0:T(8,128)(2,1)S(1)}, u32[]{:S(2)}, u32[]{:S(2)}) async-start(bf16[128,8,512]{2,1,0:T(8,128)(2,1)} %smooth.1.tiled_ref), calls=%async_computation | async-start | bytes 2097152 | tf_op jit(solution)/shard_map/all_to_all | solution.py:384

commit v7 on v6

--- a/solution.py
+++ b/solution.py
@@ -13,7 +13,7 @@
 ITERS = 2
 TA = ("ta_0", "ta_1", "ta_2")
 YZ = ("ta_1", "ta_2")
-ZYX = ("ta_2", "ta_1", "ta_0")
+YZX = ("ta_1", "ta_2", "ta_0")
 TA_ROW = ("ta_0", "ta_1", "ta_2", "row")
 
 FRAMES = 8
@@ -148,7 +148,7 @@
                 )
                 for m in range(4):
                     column = 4 * p + m
-                    at = (column % 8) * 16 + (2 * lax.rem(ty, 2) + column // 8) * 4 + ty // 2
+                    at = (16 * lax.rem(ty, 2) + column) * 4 + ty // 2
                     out_ref[at, :, q * LANES : (q + 1) * LANES] = tiles[m].astype(jnp.bfloat16)
         return carry
 
@@ -219,7 +219,7 @@
         message = (here_ref, left_ref, far_ref, right_ref)[kx][first : first + many]
         source = lax.rem(x + PLANES - kx, PLANES)
         tile = pl.multiple_of(PLANE * source + first, many)
-        frames = [tiled_ref[(k % 8) * 16 + (first // 8 + k // 8) * 4 + source] for k in range(many)]
+        frames = [tiled_ref[PLANES * (first + k) + source] for k in range(many)]
         prints = message[:, :, :PIXELS].reshape(rows, PIXELS)
         extra = message[:, :, PIXELS:].astype(jnp.float32).reshape(rows, LANES)
         found = lax.dot_general(
@@ -347,10 +347,7 @@
 
 
 def store_kernel(arrived_ref, out_ref, sems):
-    copies = []
-    for x in range(4):
-        for y in range(4):
-            copies.append(pltpu.make_async_copy(arrived_ref.at[:, y, x], out_ref.at[x, y], sems.at[4 * x + y]))
+    copies = [pltpu.make_async_copy(arrived_ref.at[:, x], out_ref.at[x], sems.at[x]) for x in range(PLANES)]
     for copy in copies:
         copy.start()
     for copy in copies:
@@ -360,14 +357,14 @@
 def store(arrived):
     return pl.pallas_call(
         store_kernel,
-        out_shape=jax.ShapeDtypeStruct((4, 4, 8, FRAMES, PIXELS), jnp.bfloat16),
+        out_shape=jax.ShapeDtypeStruct((PLANES, PLANE, FRAMES, PIXELS), jnp.bfloat16),
         in_specs=[VMEM],
         out_specs=pl.BlockSpec(memory_space=pl.ANY),
-        scratch_shapes=[pltpu.SemaphoreType.DMA((16,))],
+        scratch_shapes=[pltpu.SemaphoreType.DMA((PLANES,))],
         cost_estimate=pl.CostEstimate(flops=500_000_000, bytes_accessed=2_000_000, transcendentals=0),
         compiler_params=pltpu.CompilerParams(vmem_limit_bytes=4 << 20),
         name="store",
-    )(arrived.reshape(8, 4, 4, FRAMES, PIXELS))
+    )(arrived.reshape(PLANE, PLANES, FRAMES, PIXELS))
 
 
 def moved(array, axis, by):
@@ -381,7 +378,7 @@
     here = lax.all_to_all(packed, YZ, 0, 0, tiled=True)
     registered = register(movie[0], shifts[0])
     tiled = smooth(registered)
-    arrived = lax.all_to_all(tiled, ZYX, split_axis=0, concat_axis=0, tiled=True)
+    arrived = lax.all_to_all(tiled, YZX, split_axis=0, concat_axis=0, tiled=True)
     left, far, right = [moved(here, "ta_0", by) for by in range(1, PLANES)]
     mine = project(where, tiled, here, left, far, right)
     other = moved(mine, "row", 1)

time: 113 us -> 112 us (level)
  the two profiles are of different devices: /device:TPU:32 before, /device:TPU:8 now
where the time goes in v7:
time: 112 us; the launch traced here: 111 us
  waiting for transfers between devices  48.6 us (43%)
  starting transfers between devices  27.2 us (24%)
  blocking collectives  16.9 us (15%)
  Pallas kernels  16.8 us (15%)
    all_to_all x1, waiting for transfers between devices, local(): lax.all_to_all(tiled, YZX, split_axis=0, concat_axis=0, tiled=True)  26.5 us
    all_to_all x1, blocking collectives, local(): lax.all_to_all(pieces.reshape(PLANE, 1, LANES), YZ, 0, 0, tiled=True)  16.9 us
    ppermute x7, waiting for transfers between devices, moved(): lax.ppermute(array, axis, [(i, (i + by) % count) for i in range(count)])  12.5 us
    all_to_all x1, starting transfers between devices, local(): here = lax.all_to_all(packed, YZ, 0, 0, tiled=True)  11.7 us
    all_to_all x1, waiting for transfers between devices, local(): here = lax.all_to_all(packed, YZ, 0, 0, tiled=True)  9.64 us
    ppermute x7, starting transfers between devices, moved(): lax.ppermute(array, axis, [(i, (i + by) % count) for i in range(count)])  8.04 us
    all_to_all x1, starting transfers between devices, local(): lax.all_to_all(tiled, YZX, split_axis=0, concat_axis=0, tiled=True)  7.47 us
    pallas_call x1, Pallas kernels, project(): pl.pallas_call(project_kernel, out_shape=jax.ShapeDtypeStruct((NEURONS, N...  4.7 us
  transfers between devices with their start and end apart: 9, of which 9 were waited for; matrix products, arithmetic and copies ran while one was open for 0% of the time, Pallas kernels for 6%

profile of v7, /device:TPU:8, one launch (start us, length us, event | category | flops | bytes accessed | tf_op | source)
XLA Modules:
  0.0 111.2 jit_solution(83378256500103048)
XLA Ops:
  0.6 1.7 %pack.1 = bf16[32,8,640]{2,1,0:T(8,128)(2,1)} custom-call(s32[1,8]{1,0:T(1,128)} %bitcast.24, s32[256]{0:T(256)} %order_ref.1, bf16[8,512]{1,0:T(8,128)(2,1)} %bitcast.22, s32[8,512]{1,0:T(8,128)} %bitcast.21, f32[8,128]{1,0:T(8,128)} %bitcast.23), custom_call_target="tpu_custom_call" | custom-call | flops 200000000 | bytes 200000 | tf_op jit(solution)/shard_map/pack/pallas_call | solution.py:193
  2.3 11.7 %all-to-all-start.1 = ((bf16[32,8,640]{2,1,0:T(8,128)(2,1)}), bf16[32,8,640]{2,1,0:T(8,128)(2,1)S(1)}, u32[]{:S(2)}, u32[]{:S(2)}) async-start(bf16[32,8,640]{2,1,0:T(8,128)(2,1)} %pack.1), calls=%async_computation.1 | async-start | bytes 655360 | tf_op jit(solution)/shard_map/all_to_all | solution.py:378
  14.0 0.7 copy-done.3
  14.9 1.8 %register.1.registered_ref = bf16[8,128,512]{2,1,0:T(8,128)(2,1)S(1)} custom-call(s32[8,4,2]{2,1,0:T(4,128)S(1)} %copy.14.shifts_ref, bf16[8,128,512]{2,1,0:T(8,128)(2,1)S(1)} %bitcast.18), custom_call_target="tpu_custom_call" | custom-call | flops 2000000000 | bytes 2000000 | tf_op jit(solution)/shard_map/register/pallas_call | solution.py:101
  16.7 9.6 %all-to-all-done.1.here_ref = bf16[32,8,640]{2,1,0:T(8,128)(2,1)S(1)} async-done(((bf16[32,8,640]{2,1,0:T(8,128)(2,1)}), bf16[32,8,640]{2,1,0:T(8,128)(2,1)S(1)}, u32[]{:S(2)}, u32[]{:S(2)}) %all-to-all-start.1) | async-done | bytes 327712 | tf_op jit(solution)/shard_map/all_to_all | solution.py:378
  26.4 2.8 %collective-permute-start.2 = (bf16[32,8,640]{2,1,0:T(8,128)(2,1)S(1)}, bf16[32,8,640]{2,1,0:T(8,128)(2,1)S(1)}, u32[]{:S(2)}, u32[]{:S(2)}) collective-permute-start(bf16[32,8,640]{2,1,0:T(8,128)(2,1)S(1)} %all-to-all-done.1.here_ref), channel_id=1, source_target_pairs={{0,192},{64,0},{128,64},{192,128},{1,193},{65,1},{129,65},{193,129... | collective-permute-start | bytes 983048 | tf_op jit(solution)/shard_map/ppermute | solution.py:372
  29.1 0.8 collective-permute-start.1
  29.9 0.9 collective-permute-start
  30.8 4.5 %smooth.1.tiled_ref = bf16[128,8,512]{2,1,0:T(8,128)(2,1)} custom-call(bf16[8,128,512]{2,1,0:T(8,128)(2,1)S(1)} %register.1.registered_ref, bf16[512,512]{1,0:T(8,128)(2,1)S(1)} %copy-done.1, bf16[128,128]{1,0:T(8,128)(2,1)S(1)} %copy-done.2), custom_call_target="tpu_custom_call" | custom-call | flops 4000000000 | bytes 3000000 | tf_op jit(solution)/shard_map/smooth/pallas_call | solution.py:159
  35.3 4.4 %collective-permute-done.2.right_ref = bf16[32,8,640]{2,1,0:T(8,128)(2,1)S(1)} collective-permute-done((bf16[32,8,640]{2,1,0:T(8,128)(2,1)S(1)}, bf16[32,8,640]{2,1,0:T(8,128)(2,1)S(1)}, u32[]{:S(2)}, u32[]{:S(2)}) %collective-permute-start.2) | collective-permute-done | bytes 327712 | tf_op jit(solution)/shard_map/ppermute | solution.py:372
  40.0 3.4 %collective-permute-done.left_ref = bf16[32,8,640]{2,1,0:T(8,128)(2,1)S(1)} collective-permute-done((bf16[32,8,640]{2,1,0:T(8,128)(2,1)S(1)}, bf16[32,8,640]{2,1,0:T(8,128)(2,1)S(1)}, u32[]{:S(2)}, u32[]{:S(2)}) %collective-permute-start) | collective-permute-done | bytes 327712 | tf_op jit(solution)/shard_map/ppermute | solution.py:372
  43.4 4.7 %project.1.mine_ref = f32[256,512]{1,0:T(8,128)S(1)} custom-call(s32[3]{0:T(128)S(1)} %pad_add_fusion.where_ref, bf16[128,8,512]{2,1,0:T(8,128)(2,1)} %smooth.1.tiled_ref, bf16[32,8,640]{2,1,0:T(8,128)(2,1)S(1)} %all-to-all-done.1.here_ref, bf16[32,8,640]{2,1,0:T(8,128)(2,1)S(1)} %collective-permute-done.left_ref, ...), custom_call_target="tpu_custom_call" | custom-call | flops 2000000000 | bytes 3000000 | tf_op jit(solution)/shard_map/project/pallas_call | solution.py:247
  48.2 1.9 %collective-permute-done.3.other_ref = f32[256,512]{1,0:T(8,128)S(1)} collective-permute-done((f32[256,512]{1,0:T(8,128)S(1)}, f32[256,512]{1,0:T(8,128)S(1)}, u32[]{:S(2)}, u32[]{:S(2)}) %collective-permute-start.3) | collective-permute-done | bytes 524320 | tf_op jit(solution)/shard_map/ppermute | solution.py:372
  50.1 1.9 %solve.1 = (f32[32,128]{1,0:T(8,128)S(1)}, f32[32,128]{1,0:T(8,128)S(1)}, f32[32,128]{1,0:T(8,128)S(1)}, f32[32,128]{1,0:T(8,128)S(1)}) custom-call(s32[3]{0:T(128)S(1)} %pad_add_fusion.where_ref, f32[256,512]{1,0:T(8,128)S(1)} %project.1.mine_ref, f32[256,512]{1,0:T(8,128)S(1)} %collective-permute-done.3.other_ref), custom_call_target="tpu_custom_call" | custom-call | flops 2000000000 | bytes 1000000 | tf_op jit(solution)/shard_map/solve/pallas_call | solution.py:291
  52.1 2.1 %collective-permute-start.5 = (f32[32,128]{1,0:T(8,128)S(1)}, f32[32,128]{1,0:T(8,128)S(1)}, u32[]{:S(2)}, u32[]{:S(2)}) collective-permute-start(f32[32,128]{1,0:T(8,128)S(1)} %get-tuple-element.8), channel_id=1, source_target_pairs={{0,128},{64,192},{128,0},{192,64},{1,129},{65,193},{129,1},{193,65... | collective-permute-start | bytes 49160 | tf_op jit(solution)/shard_map/ppermute | solution.py:372
  54.2 1.3 %collective-permute-start.6 = (f32[32,128]{1,0:T(8,128)S(1)}, f32[32,128]{1,0:T(8,128)S(1)}, u32[]{:S(2)}, u32[]{:S(2)}) collective-permute-start(f32[32,128]{1,0:T(8,128)S(1)} %get-tuple-element.9), channel_id=1, source_target_pairs={{0,192},{64,0},{128,64},{192,128},{1,193},{65,1},{129,65},{193,129... | collective-permute-start | bytes 49160 | tf_op jit(solution)/shard_map/ppermute | solution.py:372
  55.5 1.5 %collective-permute-done.4.refs_1_ = f32[32,128]{1,0:T(8,128)S(1)} collective-permute-done((f32[32,128]{1,0:T(8,128)S(1)}, f32[32,128]{1,0:T(8,128)S(1)}, u32[]{:S(2)}, u32[]{:S(2)}) %collective-permute-start.4) | collective-permute-done | bytes 16416 | tf_op jit(solution)/shard_map/ppermute | solution.py:372
  57.4 0.6 collective-permute-done.6.refs_3_
  58.1 0.6 merge.1
  58.6 16.9 %all_to_all.15 = f32[32,1,128]{2,1,0:T(1,128)S(1)} all-to-all(f32[32,1,128]{2,1,0:T(1,128)S(1)} %bitcast.17), channel_id=1, replica_groups=mesh['ta_0'=4,'ta_1'=4,'ta_2'=8,'row'=2] {'ta_1','ta_2'}, dimensions={0} | all-to-all | bytes 32768 | tf_op jit(solution)/shard_map/all_to_all | solution.py:388
  75.6 7.5 %all-to-all-start = ((bf16[128,8,512]{2,1,0:T(8,128)(2,1)}), bf16[128,8,512]{2,1,0:T(8,128)(2,1)S(1)}, u32[]{:S(2)}, u32[]{:S(2)}) async-start(bf16[128,8,512]{2,1,0:T(8,128)(2,1)} %smooth.1.tiled_ref), calls=%async_computation | async-start | bytes 2097152 | tf_op jit(solution)/shard_map/all_to_all | solution.py:381
  83.0 0.7 join.1
  83.7 26.5 %all-to-all-done = bf16[128,8,512]{2,1,0:T(8,128)(2,1)S(1)} async-done(((bf16[128,8,512]{2,1,0:T(8,128)(2,1)}), bf16[128,8,512]{2,1,0:T(8,128)(2,1)S(1)}, u32[]{:S(2)}, u32[]{:S(2)}) %all-to-all-start) | async-done | bytes 1048608 | tf_op jit(solution)/shard_map/all_to_all | solution.py:381
  110.2 1.0 store.1
  (13 shorter events, 1.1 us)
Async XLA Ops:
  0.6 14.3 %copy-start = (bf16[1,8,128,512]{3,2,1,0:T(8,128)(2,1)S(1)}, bf16[1,8,128,512]{3,2,1,0:T(8,128)(2,1)}, u32[]{:S(2)}) copy-start(bf16[1,8,128,512]{3,2,1,0:T(8,128)(2,1)} %param.9) | copy-start | bytes 3145732
  2.3 24.1 %all-to-all-start.1 = ((bf16[32,8,640]{2,1,0:T(8,128)(2,1)}), bf16[32,8,640]{2,1,0:T(8,128)(2,1)S(1)}, u32[]{:S(2)}, u32[]{:S(2)}) async-start(bf16[32,8,640]{2,1,0:T(8,128)(2,1)} %pack.1), calls=%async_computation.1 | async-start | bytes 655360 | tf_op jit(solution)/shard_map/all_to_all | solution.py:378
  14.0 0.7 copy-start.3
  14.9 15.9 %copy-start.1 = (bf16[512,512]{1,0:T(8,128)(2,1)S(1)}, bf16[512,512]{1,0:T(8,128)(2,1)}, u32[]{:S(2)}) copy-start(bf16[512,512]{1,0:T(8,128)(2,1)} %constant.18.clone.wide_ref) | copy-start | bytes 1572868
  14.9 15.9 %copy-start.2 = (bf16[128,128]{1,0:T(8,128)(2,1)S(1)}, bf16[128,128]{1,0:T(8,128)(2,1)}, u32[]{:S(2)}) copy-start(bf16[128,128]{1,0:T(8,128)(2,1)} %constant.19.clone.tall_ref) | copy-start | bytes 98308
  26.4 13.4 %collective-permute-start.2 = (bf16[32,8,640]{2,1,0:T(8,128)(2,1)S(1)}, bf16[32,8,640]{2,1,0:T(8,128)(2,1)S(1)}, u32[]{:S(2)}, u32[]{:S(2)}) collective-permute-start(bf16[32,8,640]{2,1,0:T(8,128)(2,1)S(1)} %all-to-all-done.1.here_ref), channel_id=1, source_target_pairs={{0,192},{64,0},{128,64},{192,128},{1,193},{65,1},{129,65},{193,129... | collective-permute-start | bytes 983048 | tf_op jit(solution)/shard_map/ppermute | solution.py:372
  29.1 10.9 %collective-permute-start.1 = (bf16[32,8,640]{2,1,0:T(8,128)(2,1)S(1)}, bf16[32,8,640]{2,1,0:T(8,128)(2,1)S(1)}, u32[]{:S(2)}, u32[]{:S(2)}) collective-permute-start(bf16[32,8,640]{2,1,0:T(8,128)(2,1)S(1)} %all-to-all-done.1.here_ref), channel_id=1, source_target_pairs={{0,128},{64,192},{128,0},{192,64},{1,129},{65,193},{129,1},{193,65... | collective-permute-start | bytes 983048 | tf_op jit(solution)/shard_map/ppermute | solution.py:372
  29.9 13.5 %collective-permute-start = (bf16[32,8,640]{2,1,0:T(8,128)(2,1)S(1)}, bf16[32,8,640]{2,1,0:T(8,128)(2,1)S(1)}, u32[]{:S(2)}, u32[]{:S(2)}) collective-permute-start(bf16[32,8,640]{2,1,0:T(8,128)(2,1)S(1)} %all-to-all-done.1.here_ref), channel_id=1, source_target_pairs={{0,64},{64,128},{128,192},{192,0},{1,65},{65,129},{129,193},{193,1... | collective-permute-start | bytes 983048 | tf_op jit(solution)/shard_map/ppermute | solution.py:372
  48.1 2.0 %collective-permute-start.3 = (f32[256,512]{1,0:T(8,128)S(1)}, f32[256,512]{1,0:T(8,128)S(1)}, u32[]{:S(2)}, u32[]{:S(2)}) collective-permute-start(f32[256,512]{1,0:T(8,128)S(1)} %project.1.mine_ref), channel_id=1, source_target_pairs={{0,1},{1,0},{2,3},{3,2},{4,5},{5,4},{6,7},{7,6},{8,9},{9,8},{10,11... | collective-permute-start | bytes 1572872 | tf_op jit(solution)/shard_map/ppermute | solution.py:372
  52.0 5.0 %collective-permute-start.4 = (f32[32,128]{1,0:T(8,128)S(1)}, f32[32,128]{1,0:T(8,128)S(1)}, u32[]{:S(2)}, u32[]{:S(2)}) collective-permute-start(f32[32,128]{1,0:T(8,128)S(1)} %get-tuple-element.7), channel_id=1, source_target_pairs={{0,64},{64,128},{128,192},{192,0},{1,65},{65,129},{129,193},{193,1... | collective-permute-start | bytes 49160 | tf_op jit(solution)/shard_map/ppermute | solution.py:372
  52.1 5.3 %collective-permute-start.5 = (f32[32,128]{1,0:T(8,128)S(1)}, f32[32,128]{1,0:T(8,128)S(1)}, u32[]{:S(2)}, u32[]{:S(2)}) collective-permute-start(f32[32,128]{1,0:T(8,128)S(1)} %get-tuple-element.8), channel_id=1, source_target_pairs={{0,128},{64,192},{128,0},{192,64},{1,129},{65,193},{129,1},{193,65... | collective-permute-start | bytes 49160 | tf_op jit(solution)/shard_map/ppermute | solution.py:372
  54.2 3.9 %collective-permute-start.6 = (f32[32,128]{1,0:T(8,128)S(1)}, f32[32,128]{1,0:T(8,128)S(1)}, u32[]{:S(2)}, u32[]{:S(2)}) collective-permute-start(f32[32,128]{1,0:T(8,128)S(1)} %get-tuple-element.9), channel_id=1, source_target_pairs={{0,192},{64,0},{128,64},{192,128},{1,193},{65,1},{129,65},{193,129... | collective-permute-start | bytes 49160 | tf_op jit(solution)/shard_map/ppermute | solution.py:372
  75.6 34.6 %all-to-all-start = ((bf16[128,8,512]{2,1,0:T(8,128)(2,1)}), bf16[128,8,512]{2,1,0:T(8,128)(2,1)S(1)}, u32[]{:S(2)}, u32[]{:S(2)}) async-start(bf16[128,8,512]{2,1,0:T(8,128)(2,1)} %smooth.1.tiled_ref), calls=%async_computation | async-start | bytes 2097152 | tf_op jit(solution)/shard_map/all_to_all | solution.py:381

commit v8 on v7

--- a/solution.py
+++ b/solution.py
@@ -12,7 +12,7 @@
 MAXS = 8
 ITERS = 2
 TA = ("ta_0", "ta_1", "ta_2")
-YZ = ("ta_1", "ta_2")
+XZ = ("ta_0", "ta_2")
 YZX = ("ta_1", "ta_2", "ta_0")
 TA_ROW = ("ta_0", "ta_1", "ta_2", "row")
 
@@ -27,6 +27,7 @@
 PIXELS = TH * TW
 PLANE = 32
 PLANES = 4
+LINE = 8
 MESSAGE = PIXELS + LANES
 ID_LANE = 64
 HIGHEST = lax.Precision.HIGHEST
@@ -180,11 +181,14 @@
     for i in range(SLOTS):
         owner = order_ref[ids_ref[0, i]].astype(jnp.float32)
         owners = jnp.where((row == i) & (lane == ID_LANE), owner, owners)
-    for w in range(PLANE // 2):
+    for w in range(LINE):
         extra = owners
-        for k, part in enumerate(parts):
-            extra = jnp.where(lane // FRAMES == k, pltpu.roll(part, (FRAMES * (k - w)) % LANES, 1), extra)
-        for to in (w, w + PLANE // 2):
+        for half in range(2):
+            for k, part in enumerate(parts):
+                group = 3 * half + k
+                turned = pltpu.roll(part, (FRAMES * (group - w - LINE * half)) % LANES, 1)
+                extra = jnp.where(lane // FRAMES == group, turned, extra)
+        for to in range(w, PLANE, LINE):
             out_ref[to, :, :PIXELS] = footprints
             out_ref[to, :, PIXELS:] = extra.astype(jnp.bfloat16)
 
@@ -209,17 +213,19 @@
     width = NEURONS + LANES
     same = iota((rows, 2 * rows), 0) // SLOTS == lax.rem(iota((rows, 2 * rows), 1), rows) // SLOTS
     own_row = iota((many, SLOTS, LANES), 1) == 2 * x + y // 2
+    back = lax.rem(LANES - 3 * FRAMES * lax.rem(y, 2), LANES)
     contract = (((1,), (1,)), ((), ()))
     neuron = iota((rows, NEURONS), 1)
     neuron_t = iota((NEURONS, rows), 0)
     diagonal = iota((rows, rows), 0) == iota((rows, rows), 1)
     out_ref[:, width:] = jnp.zeros((NEURONS, LANES), jnp.float32)
     for at in range(2 * PLANES):
-        kx, first = at // 2, many * (at % 2)
-        message = (here_ref, left_ref, far_ref, right_ref)[kx][first : first + many]
-        source = lax.rem(x + PLANES - kx, PLANES)
-        tile = pl.multiple_of(PLANE * source + first, many)
-        frames = [tiled_ref[PLANES * (first + k) + source] for k in range(many)]
+        ky, first = at // 2, many * (at % 2)
+        message = (here_ref, left_ref, far_ref, right_ref)[ky][first : first + many]
+        source = lax.rem(y + PLANES - ky, PLANES)
+        frames = [
+            tiled_ref[PLANES * (LINE * source + k % LINE) + (first + k) // LINE] for k in range(many)
+        ]
         prints = message[:, :, :PIXELS].reshape(rows, PIXELS)
         extra = message[:, :, PIXELS:].astype(jnp.float32).reshape(rows, LANES)
         found = lax.dot_general(
@@ -236,8 +242,11 @@
             terms_ref[span, k * width : k * width + NEURONS] = one
             terms_ref[span, k * width + NEURONS : (k + 1) * width] = two
         piece = jnp.sum(jnp.where(own_row, extra.reshape(many, SLOTS, LANES), 0.0), axis=1)
+        piece = pltpu.roll(piece, back, 1)
         piece = piece + (pltpu.roll(piece, LANES - FRAMES, 1) + pltpu.roll(piece, LANES - 2 * FRAMES, 1))
-        out_ref[pl.ds(tile, many), width:] = piece
+        for k in range(many // LINE):
+            tile = pl.multiple_of(PLANE * (first // LINE + k) + LINE * source, LINE)
+            out_ref[pl.ds(tile, LINE), width:] = piece[k * LINE : (k + 1) * LINE]
     sums = dot32(select_ref[...], terms_ref[...])
     out_ref[:, :width] = sums[:, :width] + (sums[:, width : 2 * width] + sums[:, 2 * width :])
 
@@ -261,7 +270,7 @@
 
 def solve_kernel(where_ref, mine_ref, other_ref, *refs):
     out_refs, current_ref, own_ref = refs[:PLANES], refs[PLANES], refs[PLANES + 1]
-    x, core = where_ref[0], where_ref[2]
+    y, core = where_ref[1], where_ref[2]
     sums = mine_ref[:, : NEURONS + LANES] + other_ref[:, : NEURONS + LANES]
     coupling = sums[:, :NEURONS]
     source = iota((LANES, LANES), 0)
@@ -283,8 +292,9 @@
     odd = current_ref[pl.ds(1, TILES, stride=2), :]
     own_ref[...] = jnp.where(core == 0, even, odd)
     for k in range(PLANES):
-        at = pl.multiple_of(PLANE * lax.rem(x + k, PLANES), PLANE)
-        out_refs[k][...] = own_ref[pl.ds(at, PLANE), :]
+        for x in range(PLANE // LINE):
+            at = pl.multiple_of(PLANE * x + LINE * lax.rem(y + k, PLANES), LINE)
+            out_refs[k][x * LINE : (x + 1) * LINE, :] = own_ref[pl.ds(at, LINE), :]
 
 
 def solve(where, mine, other):
@@ -304,7 +314,7 @@
     group = lax.rem(iota((PLANE, LANES), 1) // FRAMES, PLANES)
     merged = refs[0][...]
     for k in range(1, PLANES):
-        merged = jnp.where(group == lax.rem(where_ref[0] + PLANES - k, PLANES), refs[k][...], merged)
+        merged = jnp.where(group == lax.rem(where_ref[1] + PLANES - k, PLANES), refs[k][...], merged)
     refs[PLANES][...] = merged
 
 
@@ -321,17 +331,16 @@
 
 
 def join_kernel(pieces_ref, out_ref):
-    near = LANES // FRAMES
     pieces = pieces_ref[...]
     rolled = [pieces] + [pltpu.roll(pieces, FRAMES * j, 1) for j in range(1, PLANES)]
-    group = iota((near, LANES), 1) // FRAMES
-    inside = group == iota((near, LANES), 0)
-    for b in range(TILES // near):
-        xs, first = b // 2, near * (b % 2)
-        total = jnp.zeros((near, LANES), jnp.float32)
+    group = iota((LINE, LANES), 1) // FRAMES
+    inside = lax.rem(group, LINE) == iota((LINE, LANES), 0)
+    for b in range(TILES * FRAMES // LANES):
+        first = LINE * (b // 2)
+        total = jnp.zeros((LINE, LANES), jnp.float32)
         for j in range(PLANES):
-            hit = inside & (lax.rem(group + PLANES - j, PLANES) == xs)
-            total = jnp.where(hit, rolled[j][first : first + near], total)
+            hit = inside & (lax.rem(group + PLANES - j, PLANES) == 2 * (b % 2) + group // LINE)
+            total = jnp.where(hit, rolled[j][first : first + LINE], total)
         out_ref[:, b * LANES : (b + 1) * LANES] = jnp.sum(total, axis=0, keepdims=True)
 
 
@@ -375,17 +384,17 @@
 def local(movie, shifts, footprint, support, neuron_ids, owner_order, start_traces):
     where = jnp.stack([lax.axis_index(axis) for axis in ("ta_0", "ta_1", "row")]).astype(jnp.int32)
     packed = pack(neuron_ids[0], owner_order, footprint[0, 0], support[0, 0], start_traces.reshape(8, LANES))
-    here = lax.all_to_all(packed, YZ, 0, 0, tiled=True)
+    here = lax.all_to_all(packed, XZ, 0, 0, tiled=True)
     registered = register(movie[0], shifts[0])
     tiled = smooth(registered)
     arrived = lax.all_to_all(tiled, YZX, split_axis=0, concat_axis=0, tiled=True)
-    left, far, right = [moved(here, "ta_0", by) for by in range(1, PLANES)]
+    left, far, right = [moved(here, "ta_1", by) for by in range(1, PLANES)]
     mine = project(where, tiled, here, left, far, right)
     other = moved(mine, "row", 1)
     pieces = solve(where, mine, other)
-    pieces = [pieces[0]] + [moved(pieces[k], "ta_0", k) for k in range(1, PLANES)]
+    pieces = [pieces[0]] + [moved(pieces[k], "ta_1", k) for k in range(1, PLANES)]
     pieces = merge(where, pieces)
-    pieces = lax.all_to_all(pieces.reshape(PLANE, 1, LANES), YZ, 0, 0, tiled=True)
+    pieces = lax.all_to_all(pieces.reshape(PLANE, 1, LANES), XZ, 0, 0, tiled=True)
     tile_movie = store(arrived)
     traces = join(pieces.reshape(PLANE, LANES))
     return (tile_movie.reshape(1, 1, -1, PIXELS), traces)

time: 112 us -> 112 us (level)
    ppermute x7, starting transfers between devices: 8.04 us -> 10 us  [moved(): lax.ppermute(array, axis, [(i, (i + by) % count) for i in range(count)])]
    ppermute x7, waiting for transfers between devices: 12.5 us -> 10.9 us  [moved(): lax.ppermute(array, axis, [(i, (i + by) % count) for i in range(count)])]
    all_to_all x1, starting transfers between devices: 7.47 us -> 6.17 us  [local(): lax.all_to_all(tiled, YZX, split_axis=0, concat_axis=0, tiled=True)]
    all_to_all x1, waiting for transfers between devices: 9.64 us -> 10.8 us  [local(): here = lax.all_to_all(packed, XZ, 0, 0, tiled=True)]
  transfers between devices with their start and end apart: 9 -> 9, of which waited for: 9 -> 8; matrix products, arithmetic and copies ran while one was open for 0% -> 0% of each run, Pallas kernels for 6% -> 6%
where the time goes in v8:
time: 112 us; the launch traced here: 111 us
  waiting for transfers between devices  48.3 us (43%)
  starting transfers between devices  27.5 us (25%)
  blocking collectives  17.1 us (15%)
  Pallas kernels  16.8 us (15%)
    all_to_all x1, waiting for transfers between devices, local(): lax.all_to_all(tiled, YZX, split_axis=0, concat_axis=0, tiled=True)  26.6 us
    all_to_all x1, blocking collectives, local(): lax.all_to_all(pieces.reshape(PLANE, 1, LANES), XZ, 0, 0, tiled=True)  17.1 us
    all_to_all x1, starting transfers between devices, local(): here = lax.all_to_all(packed, XZ, 0, 0, tiled=True)  11.3 us
    ppermute x7, waiting for transfers between devices, moved(): lax.ppermute(array, axis, [(i, (i + by) % count) for i in range(count)])  10.9 us
    all_to_all x1, waiting for transfers between devices, local(): here = lax.all_to_all(packed, XZ, 0, 0, tiled=True)  10.8 us
    ppermute x7, starting transfers between devices, moved(): lax.ppermute(array, axis, [(i, (i + by) % count) for i in range(count)])  10 us
    all_to_all x1, starting transfers between devices, local(): lax.all_to_all(tiled, YZX, split_axis=0, concat_axis=0, tiled=True)  6.17 us
    pallas_call x1, Pallas kernels, project(): pl.pallas_call(project_kernel, out_shape=jax.ShapeDtypeStruct((NEURONS, N...  4.7 us
  transfers between devices with their start and end apart: 9, of which 8 were waited for; matrix products, arithmetic and copies ran while one was open for 0% of the time, Pallas kernels for 6%

profile of v8, /device:TPU:8, one launch (start us, length us, event | category | flops | bytes accessed | tf_op | source)
XLA Modules:
  0.0 111.3 jit_solution(2629322091600786825)
XLA Ops:
  0.6 1.7 %pack.1 = bf16[32,8,640]{2,1,0:T(8,128)(2,1)} custom-call(s32[1,8]{1,0:T(1,128)} %bitcast.24, s32[256]{0:T(256)} %order_ref.1, bf16[8,512]{1,0:T(8,128)(2,1)} %bitcast.22, s32[8,512]{1,0:T(8,128)} %bitcast.21, f32[8,128]{1,0:T(8,128)} %bitcast.23), custom_call_target="tpu_custom_call" | custom-call | flops 200000000 | bytes 200000 | tf_op jit(solution)/shard_map/pack/pallas_call | solution.py:197
  2.3 11.3 %all-to-all-start.1 = ((bf16[32,8,640]{2,1,0:T(8,128)(2,1)}), bf16[32,8,640]{2,1,0:T(8,128)(2,1)S(1)}, u32[]{:S(2)}, u32[]{:S(2)}) async-start(bf16[32,8,640]{2,1,0:T(8,128)(2,1)} %pack.1), calls=%async_computation.1 | async-start | bytes 655360 | tf_op jit(solution)/shard_map/all_to_all | solution.py:387
  13.6 0.7 copy-done.3
  14.5 1.8 %register.1.registered_ref = bf16[8,128,512]{2,1,0:T(8,128)(2,1)S(1)} custom-call(s32[8,4,2]{2,1,0:T(4,128)S(1)} %copy.14.shifts_ref, bf16[8,128,512]{2,1,0:T(8,128)(2,1)S(1)} %bitcast.18), custom_call_target="tpu_custom_call" | custom-call | flops 2000000000 | bytes 2000000 | tf_op jit(solution)/shard_map/register/pallas_call | solution.py:102
  16.3 10.8 %all-to-all-done.1.here_ref = bf16[32,8,640]{2,1,0:T(8,128)(2,1)S(1)} async-done(((bf16[32,8,640]{2,1,0:T(8,128)(2,1)}), bf16[32,8,640]{2,1,0:T(8,128)(2,1)S(1)}, u32[]{:S(2)}, u32[]{:S(2)}) %all-to-all-start.1) | async-done | bytes 327712 | tf_op jit(solution)/shard_map/all_to_all | solution.py:387
  27.6 2.6 %collective-permute-start.1 = (bf16[32,8,640]{2,1,0:T(8,128)(2,1)S(1)}, bf16[32,8,640]{2,1,0:T(8,128)(2,1)S(1)}, u32[]{:S(2)}, u32[]{:S(2)}) collective-permute-start(bf16[32,8,640]{2,1,0:T(8,128)(2,1)S(1)} %all-to-all-done.1.here_ref), channel_id=1, source_target_pairs={{0,32},{16,48},{32,0},{48,16},{1,33},{17,49},{33,1},{49,17},{2,34}... | collective-permute-start | bytes 983048 | tf_op jit(solution)/shard_map/ppermute | solution.py:381
  30.2 1.9 %collective-permute-start = (bf16[32,8,640]{2,1,0:T(8,128)(2,1)S(1)}, bf16[32,8,640]{2,1,0:T(8,128)(2,1)S(1)}, u32[]{:S(2)}, u32[]{:S(2)}) collective-permute-start(bf16[32,8,640]{2,1,0:T(8,128)(2,1)S(1)} %all-to-all-done.1.here_ref), channel_id=1, source_target_pairs={{0,16},{16,32},{32,48},{48,0},{1,17},{17,33},{33,49},{49,1},{2,18}... | collective-permute-start | bytes 983048 | tf_op jit(solution)/shard_map/ppermute | solution.py:381
  32.1 4.5 %smooth.1.tiled_ref = bf16[128,8,512]{2,1,0:T(8,128)(2,1)} custom-call(bf16[8,128,512]{2,1,0:T(8,128)(2,1)S(1)} %register.1.registered_ref, bf16[512,512]{1,0:T(8,128)(2,1)S(1)} %copy-done.1, bf16[128,128]{1,0:T(8,128)(2,1)S(1)} %copy-done.2), custom_call_target="tpu_custom_call" | custom-call | flops 4000000000 | bytes 3000000 | tf_op jit(solution)/shard_map/smooth/pallas_call | solution.py:160
  36.6 0.9 collective-permute-done.2.right_ref
  37.5 3.5 %collective-permute-done.1.far_ref = bf16[32,8,640]{2,1,0:T(8,128)(2,1)S(1)} collective-permute-done((bf16[32,8,640]{2,1,0:T(8,128)(2,1)S(1)}, bf16[32,8,640]{2,1,0:T(8,128)(2,1)S(1)}, u32[]{:S(2)}, u32[]{:S(2)}) %collective-permute-start.1) | collective-permute-done | bytes 327712 | tf_op jit(solution)/shard_map/ppermute | solution.py:381
  41.0 0.9 collective-permute-done.left_ref
  41.9 4.7 %project.1.mine_ref = f32[256,512]{1,0:T(8,128)S(1)} custom-call(s32[3]{0:T(128)S(1)} %pad_add_fusion.where_ref, bf16[128,8,512]{2,1,0:T(8,128)(2,1)} %smooth.1.tiled_ref, bf16[32,8,640]{2,1,0:T(8,128)(2,1)S(1)} %all-to-all-done.1.here_ref, bf16[32,8,640]{2,1,0:T(8,128)(2,1)S(1)} %collective-permute-done.left_ref, ...), custom_call_target="tpu_custom_call" | custom-call | flops 2000000000 | bytes 3000000 | tf_op jit(solution)/shard_map/project/pallas_call | solution.py:256
  46.7 1.9 %collective-permute-done.3.other_ref = f32[256,512]{1,0:T(8,128)S(1)} collective-permute-done((f32[256,512]{1,0:T(8,128)S(1)}, f32[256,512]{1,0:T(8,128)S(1)}, u32[]{:S(2)}, u32[]{:S(2)}) %collective-permute-start.3) | collective-permute-done | bytes 524320 | tf_op jit(solution)/shard_map/ppermute | solution.py:381
  48.6 1.9 %solve.1 = (f32[32,128]{1,0:T(8,128)S(1)}, f32[32,128]{1,0:T(8,128)S(1)}, f32[32,128]{1,0:T(8,128)S(1)}, f32[32,128]{1,0:T(8,128)S(1)}) custom-call(s32[3]{0:T(128)S(1)} %pad_add_fusion.where_ref, f32[256,512]{1,0:T(8,128)S(1)} %project.1.mine_ref, f32[256,512]{1,0:T(8,128)S(1)} %collective-permute-done.3.other_ref), custom_call_target="tpu_custom_call" | custom-call | flops 2000000000 | bytes 1000000 | tf_op jit(solution)/shard_map/solve/pallas_call | solution.py:301
  50.5 1.5 %collective-permute-start.4 = (f32[32,128]{1,0:T(8,128)S(1)}, f32[32,128]{1,0:T(8,128)S(1)}, u32[]{:S(2)}, u32[]{:S(2)}) collective-permute-start(f32[32,128]{1,0:T(8,128)S(1)} %get-tuple-element.7), channel_id=1, source_target_pairs={{0,16},{16,32},{32,48},{48,0},{1,17},{17,33},{33,49},{49,1},{2,18}... | collective-permute-start | bytes 49160 | tf_op jit(solution)/shard_map/ppermute | solution.py:381
  51.9 3.5 %collective-permute-start.5 = (f32[32,128]{1,0:T(8,128)S(1)}, f32[32,128]{1,0:T(8,128)S(1)}, u32[]{:S(2)}, u32[]{:S(2)}) collective-permute-start(f32[32,128]{1,0:T(8,128)S(1)} %get-tuple-element.8), channel_id=1, source_target_pairs={{0,32},{16,48},{32,0},{48,16},{1,33},{17,49},{33,1},{49,17},{2,34}... | collective-permute-start | bytes 49160 | tf_op jit(solution)/shard_map/ppermute | solution.py:381
  55.5 1.7 %collective-permute-done.5.refs_2_ = f32[32,128]{1,0:T(8,128)S(1)} collective-permute-done((f32[32,128]{1,0:T(8,128)S(1)}, f32[32,128]{1,0:T(8,128)S(1)}, u32[]{:S(2)}, u32[]{:S(2)}) %collective-permute-start.5) | collective-permute-done | bytes 16416 | tf_op jit(solution)/shard_map/ppermute | solution.py:381
  57.2 2.0 %collective-permute-done.6.refs_3_ = f32[32,128]{1,0:T(8,128)S(1)} collective-permute-done((f32[32,128]{1,0:T(8,128)S(1)}, f32[32,128]{1,0:T(8,128)S(1)}, u32[]{:S(2)}, u32[]{:S(2)}) %collective-permute-start.6) | collective-permute-done | bytes 16416 | tf_op jit(solution)/shard_map/ppermute | solution.py:381
  59.2 0.6 merge.1
  59.8 17.1 %all_to_all.15 = f32[32,1,128]{2,1,0:T(1,128)S(1)} all-to-all(f32[32,1,128]{2,1,0:T(1,128)S(1)} %bitcast.17), channel_id=1, replica_groups=mesh['ta_0'=4,'ta_1'=4,'ta_2'=8,'row'=2] {'ta_0','ta_2'}, dimensions={0} | all-to-all | bytes 32768 | tf_op jit(solution)/shard_map/all_to_all | solution.py:397
  76.9 6.2 %all-to-all-start = ((bf16[128,8,512]{2,1,0:T(8,128)(2,1)}), bf16[128,8,512]{2,1,0:T(8,128)(2,1)S(1)}, u32[]{:S(2)}, u32[]{:S(2)}) async-start(bf16[128,8,512]{2,1,0:T(8,128)(2,1)} %smooth.1.tiled_ref), calls=%async_computation | async-start | bytes 2097152 | tf_op jit(solution)/shard_map/all_to_all | solution.py:390
  83.0 0.7 join.1
  83.7 26.6 %all-to-all-done = bf16[128,8,512]{2,1,0:T(8,128)(2,1)S(1)} async-done(((bf16[128,8,512]{2,1,0:T(8,128)(2,1)}), bf16[128,8,512]{2,1,0:T(8,128)(2,1)S(1)}, u32[]{:S(2)}, u32[]{:S(2)}) %all-to-all-start) | async-done | bytes 1048608 | tf_op jit(solution)/shard_map/all_to_all | solution.py:390
  110.3 1.0 store.1
  (13 shorter events, 0.8 us)
Async XLA Ops:
  0.6 13.9 %copy-start = (bf16[1,8,128,512]{3,2,1,0:T(8,128)(2,1)S(1)}, bf16[1,8,128,512]{3,2,1,0:T(8,128)(2,1)}, u32[]{:S(2)}) copy-start(bf16[1,8,128,512]{3,2,1,0:T(8,128)(2,1)} %param.9) | copy-start | bytes 3145732
  2.3 24.9 %all-to-all-start.1 = ((bf16[32,8,640]{2,1,0:T(8,128)(2,1)}), bf16[32,8,640]{2,1,0:T(8,128)(2,1)S(1)}, u32[]{:S(2)}, u32[]{:S(2)}) async-start(bf16[32,8,640]{2,1,0:T(8,128)(2,1)} %pack.1), calls=%async_computation.1 | async-start | bytes 655360 | tf_op jit(solution)/shard_map/all_to_all | solution.py:387
  13.6 0.7 copy-start.3
  14.5 17.6 %copy-start.1 = (bf16[512,512]{1,0:T(8,128)(2,1)S(1)}, bf16[512,512]{1,0:T(8,128)(2,1)}, u32[]{:S(2)}) copy-start(bf16[512,512]{1,0:T(8,128)(2,1)} %constant.18.clone.wide_ref) | copy-start | bytes 1572868
  14.5 17.6 %copy-start.2 = (bf16[128,128]{1,0:T(8,128)(2,1)S(1)}, bf16[128,128]{1,0:T(8,128)(2,1)}, u32[]{:S(2)}) copy-start(bf16[128,128]{1,0:T(8,128)(2,1)} %constant.19.clone.tall_ref) | copy-start | bytes 98308
  27.2 10.4 %collective-permute-start.2 = (bf16[32,8,640]{2,1,0:T(8,128)(2,1)S(1)}, bf16[32,8,640]{2,1,0:T(8,128)(2,1)S(1)}, u32[]{:S(2)}, u32[]{:S(2)}) collective-permute-start(bf16[32,8,640]{2,1,0:T(8,128)(2,1)S(1)} %all-to-all-done.1.here_ref), channel_id=1, source_target_pairs={{0,48},{16,0},{32,16},{48,32},{1,49},{17,1},{33,17},{49,33},{2,50}... | collective-permute-start | bytes 983048 | tf_op jit(solution)/shard_map/ppermute | solution.py:381
  27.6 13.4 %collective-permute-start.1 = (bf16[32,8,640]{2,1,0:T(8,128)(2,1)S(1)}, bf16[32,8,640]{2,1,0:T(8,128)(2,1)S(1)}, u32[]{:S(2)}, u32[]{:S(2)}) collective-permute-start(bf16[32,8,640]{2,1,0:T(8,128)(2,1)S(1)} %all-to-all-done.1.here_ref), channel_id=1, source_target_pairs={{0,32},{16,48},{32,0},{48,16},{1,33},{17,49},{33,1},{49,17},{2,34}... | collective-permute-start | bytes 983048 | tf_op jit(solution)/shard_map/ppermute | solution.py:381
  30.2 11.7 %collective-permute-start = (bf16[32,8,640]{2,1,0:T(8,128)(2,1)S(1)}, bf16[32,8,640]{2,1,0:T(8,128)(2,1)S(1)}, u32[]{:S(2)}, u32[]{:S(2)}) collective-permute-start(bf16[32,8,640]{2,1,0:T(8,128)(2,1)S(1)} %all-to-all-done.1.here_ref), channel_id=1, source_target_pairs={{0,16},{16,32},{32,48},{48,0},{1,17},{17,33},{33,49},{49,1},{2,18}... | collective-permute-start | bytes 983048 | tf_op jit(solution)/shard_map/ppermute | solution.py:381
  46.6 2.0 %collective-permute-start.3 = (f32[256,512]{1,0:T(8,128)S(1)}, f32[256,512]{1,0:T(8,128)S(1)}, u32[]{:S(2)}, u32[]{:S(2)}) collective-permute-start(f32[256,512]{1,0:T(8,128)S(1)} %project.1.mine_ref), channel_id=1, source_target_pairs={{0,1},{1,0},{2,3},{3,2},{4,5},{5,4},{6,7},{7,6},{8,9},{9,8},{10,11... | collective-permute-start | bytes 1572872 | tf_op jit(solution)/shard_map/ppermute | solution.py:381
  50.5 5.0 %collective-permute-start.4 = (f32[32,128]{1,0:T(8,128)S(1)}, f32[32,128]{1,0:T(8,128)S(1)}, u32[]{:S(2)}, u32[]{:S(2)}) collective-permute-start(f32[32,128]{1,0:T(8,128)S(1)} %get-tuple-element.7), channel_id=1, source_target_pairs={{0,16},{16,32},{32,48},{48,0},{1,17},{17,33},{33,49},{49,1},{2,18}... | collective-permute-start | bytes 49160 | tf_op jit(solution)/shard_map/ppermute | solution.py:381
  51.9 5.2 %collective-permute-start.5 = (f32[32,128]{1,0:T(8,128)S(1)}, f32[32,128]{1,0:T(8,128)S(1)}, u32[]{:S(2)}, u32[]{:S(2)}) collective-permute-start(f32[32,128]{1,0:T(8,128)S(1)} %get-tuple-element.8), channel_id=1, source_target_pairs={{0,32},{16,48},{32,0},{48,16},{1,33},{17,49},{33,1},{49,17},{2,34}... | collective-permute-start | bytes 49160 | tf_op jit(solution)/shard_map/ppermute | solution.py:381
  55.5 3.7 %collective-permute-start.6 = (f32[32,128]{1,0:T(8,128)S(1)}, f32[32,128]{1,0:T(8,128)S(1)}, u32[]{:S(2)}, u32[]{:S(2)}) collective-permute-start(f32[32,128]{1,0:T(8,128)S(1)} %get-tuple-element.9), channel_id=1, source_target_pairs={{0,48},{16,0},{32,16},{48,32},{1,49},{17,1},{33,17},{49,33},{2,50}... | collective-permute-start | bytes 49160 | tf_op jit(solution)/shard_map/ppermute | solution.py:381
  76.9 33.4 %all-to-all-start = ((bf16[128,8,512]{2,1,0:T(8,128)(2,1)}), bf16[128,8,512]{2,1,0:T(8,128)(2,1)S(1)}, u32[]{:S(2)}, u32[]{:S(2)}) async-start(bf16[128,8,512]{2,1,0:T(8,128)(2,1)} %smooth.1.tiled_ref), calls=%async_computation | async-start | bytes 2097152 | tf_op jit(solution)/shard_map/all_to_all | solution.py:390

commit v9 on v7

--- a/solution.py
+++ b/solution.py
@@ -27,6 +27,7 @@
 PIXELS = TH * TW
 PLANE = 32
 PLANES = 4
+LINE = 8
 MESSAGE = PIXELS + LANES
 ID_LANE = 64
 HIGHEST = lax.Precision.HIGHEST
@@ -301,37 +302,62 @@
 
 
 def merge_kernel(where_ref, *refs):
+    out_refs, merged_ref = refs[PLANES : 2 * PLANES], refs[2 * PLANES]
     group = lax.rem(iota((PLANE, LANES), 1) // FRAMES, PLANES)
     merged = refs[0][...]
     for k in range(1, PLANES):
         merged = jnp.where(group == lax.rem(where_ref[0] + PLANES - k, PLANES), refs[k][...], merged)
-    refs[PLANES][...] = merged
+    merged_ref[...] = merged
+    for k in range(PLANES):
+        at = pl.multiple_of(LINE * lax.rem(where_ref[1] + k, PLANES), LINE)
+        out_refs[k][...] = merged_ref[pl.ds(at, LINE), :]
 
 
 def merge(where, pieces):
     return pl.pallas_call(
         merge_kernel,
-        out_shape=jax.ShapeDtypeStruct((PLANE, LANES), jnp.float32),
+        out_shape=[jax.ShapeDtypeStruct((LINE, LANES), jnp.float32)] * PLANES,
         in_specs=[SMEM] + [VMEM] * PLANES,
-        out_specs=VMEM,
+        out_specs=[VMEM] * PLANES,
+        scratch_shapes=[pltpu.VMEM((PLANE, LANES), jnp.float32)],
         cost_estimate=pl.CostEstimate(flops=100_000_000, bytes_accessed=100_000, transcendentals=0),
         compiler_params=pltpu.CompilerParams(vmem_limit_bytes=2 << 20),
         name="merge",
     )(where, *pieces)
 
 
+def gather_kernel(where_ref, *refs):
+    group = iota((LINE, LANES), 1) // FRAMES // PLANES
+    merged = refs[0][...]
+    for k in range(1, PLANES):
+        merged = jnp.where(group == lax.rem(where_ref[1] + PLANES - k, PLANES), refs[k][...], merged)
+    refs[PLANES][...] = merged
+
+
+def gather(where, pieces):
+    return pl.pallas_call(
+        gather_kernel,
+        out_shape=jax.ShapeDtypeStruct((LINE, LANES), jnp.float32),
+        in_specs=[SMEM] + [VMEM] * PLANES,
+        out_specs=VMEM,
+        cost_estimate=pl.CostEstimate(flops=100_000_000, bytes_accessed=100_000, transcendentals=0),
+        compiler_params=pltpu.CompilerParams(vmem_limit_bytes=2 << 20),
+        name="gather",
+    )(where, *pieces)
+
+
 def join_kernel(pieces_ref, out_ref):
-    near = LANES // FRAMES
     pieces = pieces_ref[...]
-    rolled = [pieces] + [pltpu.roll(pieces, FRAMES * j, 1) for j in range(1, PLANES)]
-    group = iota((near, LANES), 1) // FRAMES
-    inside = group == iota((near, LANES), 0)
-    for b in range(TILES // near):
-        xs, first = b // 2, near * (b % 2)
-        total = jnp.zeros((near, LANES), jnp.float32)
-        for j in range(PLANES):
-            hit = inside & (lax.rem(group + PLANES - j, PLANES) == xs)
-            total = jnp.where(hit, rolled[j][first : first + near], total)
+    places = LANES // FRAMES
+    rolled = [pieces] + [pltpu.roll(pieces, FRAMES * j, 1) for j in range(1, places)]
+    group = iota((LINE, LANES), 1) // FRAMES
+    inside = lax.rem(group, LINE) == iota((LINE, LANES), 0)
+    for b in range(TILES * FRAMES // LANES):
+        wanted = PLANES * (2 * (b % 2) + group // LINE) + b // 2
+        shift = lax.rem(group - wanted + places, places)
+        total = jnp.zeros((LINE, LANES), jnp.float32)
+        for j in range(places):
+            total = jnp.where(inside & (shift == j), rolled[j], total)
         out_ref[:, b * LANES : (b + 1) * LANES] = jnp.sum(total, axis=0, keepdims=True)
 
 
@@ -385,9 +411,11 @@
     pieces = solve(where, mine, other)
     pieces = [pieces[0]] + [moved(pieces[k], "ta_0", k) for k in range(1, PLANES)]
     pieces = merge(where, pieces)
-    pieces = lax.all_to_all(pieces.reshape(PLANE, 1, LANES), YZ, 0, 0, tiled=True)
+    pieces = [pieces[0]] + [moved(pieces[k], "ta_1", k) for k in range(1, PLANES)]
+    pieces = gather(where, pieces)
+    pieces = lax.all_to_all(pieces.reshape(LINE, 1, LANES), "ta_2", 0, 0, tiled=True)
     tile_movie = store(arrived)
-    traces = join(pieces.reshape(PLANE, LANES))
+    traces = join(pieces.reshape(LINE, LANES))
     return (tile_movie.reshape(1, 1, -1, PIXELS), traces)
 
 

time: 112 us -> 115 us (1.027)
  the two profiles are of different devices: /device:TPU:8 before, /device:TPU:32 now
where the time goes in v9:
time: 115 us; the launch traced here: 114 us
  waiting for transfers between devices  52.2 us (45%)
  starting transfers between devices  32.7 us (28%)
  Pallas kernels  17.4 us (15%)
  blocking collectives  10.4 us (9%)
    all_to_all x1, waiting for transfers between devices, local(): lax.all_to_all(tiled, YZX, split_axis=0, concat_axis=0, tiled=True)  25.1 us
    ppermute x10, waiting for transfers between devices, moved(): lax.ppermute(array, axis, [(i, (i + by) % count) for i in range(count)])  16.2 us
    ppermute x10, starting transfers between devices, moved(): lax.ppermute(array, axis, [(i, (i + by) % count) for i in range(count)])  12.7 us
    all_to_all x1, starting transfers between devices, local(): here = lax.all_to_all(packed, YZ, 0, 0, tiled=True)  11.4 us
    all_to_all x1, waiting for transfers between devices, local(): here = lax.all_to_all(packed, YZ, 0, 0, tiled=True)  10.9 us
    all_to_all x1, blocking collectives, local(): lax.all_to_all(pieces.reshape(LINE, 1, LANES), 'ta_2', 0, 0, tiled=True)  10.4 us
    all_to_all x1, starting transfers between devices, local(): lax.all_to_all(tiled, YZX, split_axis=0, concat_axis=0, tiled=True)  8.6 us
    pallas_call x1, Pallas kernels, project(): pl.pallas_call(project_kernel, out_shape=jax.ShapeDtypeStruct((NEURONS, N...  4.7 us
  transfers between devices with their start and end apart: 12, of which 11 were waited for; matrix products, arithmetic and copies ran while one was open for 0% of the time, Pallas kernels for 6%

profile of v9, /device:TPU:32, one launch (start us, length us, event | category | flops | bytes accessed | tf_op | source)
XLA Modules:
  0.0 114.3 jit_solution(13999811552751641380)
XLA Ops:
  0.6 1.7 %pack.1 = bf16[32,8,640]{2,1,0:T(8,128)(2,1)} custom-call(s32[1,8]{1,0:T(1,128)} %bitcast.24, s32[256]{0:T(256)} %order_ref.1, bf16[8,512]{1,0:T(8,128)(2,1)} %bitcast.22, s32[8,512]{1,0:T(8,128)} %bitcast.21, f32[8,128]{1,0:T(8,128)} %bitcast.23), custom_call_target="tpu_custom_call" | custom-call | flops 200000000 | bytes 200000 | tf_op jit(solution)/shard_map/pack/pallas_call | solution.py:194
  2.3 11.4 %all-to-all-start.1 = ((bf16[32,8,640]{2,1,0:T(8,128)(2,1)}), bf16[32,8,640]{2,1,0:T(8,128)(2,1)S(1)}, u32[]{:S(2)}, u32[]{:S(2)}) async-start(bf16[32,8,640]{2,1,0:T(8,128)(2,1)} %pack.1), calls=%async_computation.1 | async-start | bytes 655360 | tf_op jit(solution)/shard_map/all_to_all | solution.py:404
  14.6 1.8 %register.1.registered_ref = bf16[8,128,512]{2,1,0:T(8,128)(2,1)S(1)} custom-call(s32[8,4,2]{2,1,0:T(4,128)S(1)} %copy.14.shifts_ref, bf16[8,128,512]{2,1,0:T(8,128)(2,1)S(1)} %bitcast.18), custom_call_target="tpu_custom_call" | custom-call | flops 2000000000 | bytes 2000000 | tf_op jit(solution)/shard_map/register/pallas_call | solution.py:102
  16.4 10.9 %all-to-all-done.1.here_ref = bf16[32,8,640]{2,1,0:T(8,128)(2,1)S(1)} async-done(((bf16[32,8,640]{2,1,0:T(8,128)(2,1)}), bf16[32,8,640]{2,1,0:T(8,128)(2,1)S(1)}, u32[]{:S(2)}, u32[]{:S(2)}) %all-to-all-start.1) | async-done | bytes 327712 | tf_op jit(solution)/shard_map/all_to_all | solution.py:404
  27.3 2.8 %collective-permute-start.2 = (bf16[32,8,640]{2,1,0:T(8,128)(2,1)S(1)}, bf16[32,8,640]{2,1,0:T(8,128)(2,1)S(1)}, u32[]{:S(2)}, u32[]{:S(2)}) collective-permute-start(bf16[32,8,640]{2,1,0:T(8,128)(2,1)S(1)} %all-to-all-done.1.here_ref), channel_id=1, source_target_pairs={{0,192},{64,0},{128,64},{192,128},{1,193},{65,1},{129,65},{193,129... | collective-permute-start | bytes 983048 | tf_op jit(solution)/shard_map/ppermute | solution.py:398
  30.0 0.8 collective-permute-start.1
  30.8 0.9 collective-permute-start
  31.7 4.5 %smooth.1.tiled_ref = bf16[128,8,512]{2,1,0:T(8,128)(2,1)} custom-call(bf16[8,128,512]{2,1,0:T(8,128)(2,1)S(1)} %register.1.registered_ref, bf16[512,512]{1,0:T(8,128)(2,1)S(1)} %copy-done.1, bf16[128,128]{1,0:T(8,128)(2,1)S(1)} %copy-done.2), custom_call_target="tpu_custom_call" | custom-call | flops 4000000000 | bytes 3000000 | tf_op jit(solution)/shard_map/smooth/pallas_call | solution.py:160
  36.2 6.4 %collective-permute-done.2.right_ref = bf16[32,8,640]{2,1,0:T(8,128)(2,1)S(1)} collective-permute-done((bf16[32,8,640]{2,1,0:T(8,128)(2,1)S(1)}, bf16[32,8,640]{2,1,0:T(8,128)(2,1)S(1)}, u32[]{:S(2)}, u32[]{:S(2)}) %collective-permute-start.2) | collective-permute-done | bytes 327712 | tf_op jit(solution)/shard_map/ppermute | solution.py:398
  42.6 3.7 %collective-permute-done.left_ref = bf16[32,8,640]{2,1,0:T(8,128)(2,1)S(1)} collective-permute-done((bf16[32,8,640]{2,1,0:T(8,128)(2,1)S(1)}, bf16[32,8,640]{2,1,0:T(8,128)(2,1)S(1)}, u32[]{:S(2)}, u32[]{:S(2)}) %collective-permute-start) | collective-permute-done | bytes 327712 | tf_op jit(solution)/shard_map/ppermute | solution.py:398
  46.3 4.7 %project.1.mine_ref = f32[256,512]{1,0:T(8,128)S(1)} custom-call(s32[3]{0:T(128)S(1)} %pad_add_fusion.where_ref, bf16[128,8,512]{2,1,0:T(8,128)(2,1)} %smooth.1.tiled_ref, bf16[32,8,640]{2,1,0:T(8,128)(2,1)S(1)} %all-to-all-done.1.here_ref, bf16[32,8,640]{2,1,0:T(8,128)(2,1)S(1)} %collective-permute-done.left_ref, ...), custom_call_target="tpu_custom_call" | custom-call | flops 2000000000 | bytes 3000000 | tf_op jit(solution)/shard_map/project/pallas_call | solution.py:248
  51.1 1.9 %collective-permute-done.3.other_ref = f32[256,512]{1,0:T(8,128)S(1)} collective-permute-done((f32[256,512]{1,0:T(8,128)S(1)}, f32[256,512]{1,0:T(8,128)S(1)}, u32[]{:S(2)}, u32[]{:S(2)}) %collective-permute-start.3) | collective-permute-done | bytes 524320 | tf_op jit(solution)/shard_map/ppermute | solution.py:398
  53.0 1.9 %solve.1 = (f32[32,128]{1,0:T(8,128)S(1)}, f32[32,128]{1,0:T(8,128)S(1)}, f32[32,128]{1,0:T(8,128)S(1)}, f32[32,128]{1,0:T(8,128)S(1)}) custom-call(s32[3]{0:T(128)S(1)} %pad_add_fusion.where_ref, f32[256,512]{1,0:T(8,128)S(1)} %project.1.mine_ref, f32[256,512]{1,0:T(8,128)S(1)} %collective-permute-done.3.other_ref), custom_call_target="tpu_custom_call" | custom-call | flops 2000000000 | bytes 1000000 | tf_op jit(solution)/shard_map/solve/pallas_call | solution.py:292
  55.0 2.1 %collective-permute-start.5 = (f32[32,128]{1,0:T(8,128)S(1)}, f32[32,128]{1,0:T(8,128)S(1)}, u32[]{:S(2)}, u32[]{:S(2)}) collective-permute-start(f32[32,128]{1,0:T(8,128)S(1)} %get-tuple-element.12), channel_id=1, source_target_pairs={{0,128},{64,192},{128,0},{192,64},{1,129},{65,193},{129,1},{193,65... | collective-permute-start | bytes 49160 | tf_op jit(solution)/shard_map/ppermute | solution.py:398
  57.0 1.4 %collective-permute-start.6 = (f32[32,128]{1,0:T(8,128)S(1)}, f32[32,128]{1,0:T(8,128)S(1)}, u32[]{:S(2)}, u32[]{:S(2)}) collective-permute-start(f32[32,128]{1,0:T(8,128)S(1)} %get-tuple-element.13), channel_id=1, source_target_pairs={{0,192},{64,0},{128,64},{192,128},{1,193},{65,1},{129,65},{193,129... | collective-permute-start | bytes 49160 | tf_op jit(solution)/shard_map/ppermute | solution.py:398
  58.4 1.5 %collective-permute-done.4.refs_1_ = f32[32,128]{1,0:T(8,128)S(1)} collective-permute-done((f32[32,128]{1,0:T(8,128)S(1)}, f32[32,128]{1,0:T(8,128)S(1)}, u32[]{:S(2)}, u32[]{:S(2)}) %collective-permute-start.4) | collective-permute-done | bytes 16416 | tf_op jit(solution)/shard_map/ppermute | solution.py:398
  62.2 2.1 %collective-permute-start.8 = (f32[8,128]{1,0:T(8,128)S(1)}, f32[8,128]{1,0:T(8,128)S(1)}, u32[]{:S(2)}, u32[]{:S(2)}) collective-permute-start(f32[8,128]{1,0:T(8,128)S(1)} %get-tuple-element.16), channel_id=1, source_target_pairs={{0,32},{16,48},{32,0},{48,16},{1,33},{17,49},{33,1},{49,17},{2,34}... | collective-permute-start | bytes 12296 | tf_op jit(solution)/shard_map/ppermute | solution.py:398
  64.3 1.9 %collective-permute-start.9 = (f32[8,128]{1,0:T(8,128)S(1)}, f32[8,128]{1,0:T(8,128)S(1)}, u32[]{:S(2)}, u32[]{:S(2)}) collective-permute-start(f32[8,128]{1,0:T(8,128)S(1)} %get-tuple-element.17), channel_id=1, source_target_pairs={{0,48},{16,0},{32,16},{48,32},{1,49},{17,1},{33,17},{49,33},{2,50}... | collective-permute-start | bytes 12296 | tf_op jit(solution)/shard_map/ppermute | solution.py:398
  66.4 0.9 collective-permute-done.8.refs_2_
  68.4 10.4 %all_to_all.15 = f32[8,1,128]{2,1,0:T(1,128)S(1)} all-to-all(f32[8,1,128]{2,1,0:T(1,128)S(1)} %bitcast.17), channel_id=1, replica_groups=mesh['ta_0'=4,'ta_1'=4,'ta_2'=8,'row'=2] {'ta_2'}, dimensions={0} | all-to-all | bytes 8192 | tf_op jit(solution)/shard_map/all_to_all | solution.py:416
  78.8 8.6 %all-to-all-start = ((bf16[128,8,512]{2,1,0:T(8,128)(2,1)}), bf16[128,8,512]{2,1,0:T(8,128)(2,1)S(1)}, u32[]{:S(2)}, u32[]{:S(2)}) async-start(bf16[128,8,512]{2,1,0:T(8,128)(2,1)} %smooth.1.tiled_ref), calls=%async_computation | async-start | bytes 2097152 | tf_op jit(solution)/shard_map/all_to_all | solution.py:407
  87.4 0.7 join.1
  88.1 25.1 %all-to-all-done = bf16[128,8,512]{2,1,0:T(8,128)(2,1)S(1)} async-done(((bf16[128,8,512]{2,1,0:T(8,128)(2,1)}), bf16[128,8,512]{2,1,0:T(8,128)(2,1)S(1)}, u32[]{:S(2)}, u32[]{:S(2)}) %all-to-all-start) | async-done | bytes 1048608 | tf_op jit(solution)/shard_map/all_to_all | solution.py:407
  113.3 1.0 store.1
  (20 shorter events, 4.7 us)
Async XLA Ops:
  0.6 13.9 %copy-start = (bf16[1,8,128,512]{3,2,1,0:T(8,128)(2,1)S(1)}, bf16[1,8,128,512]{3,2,1,0:T(8,128)(2,1)}, u32[]{:S(2)}) copy-start(bf16[1,8,128,512]{3,2,1,0:T(8,128)(2,1)} %param.9) | copy-start | bytes 3145732
  2.3 24.9 %all-to-all-start.1 = ((bf16[32,8,640]{2,1,0:T(8,128)(2,1)}), bf16[32,8,640]{2,1,0:T(8,128)(2,1)S(1)}, u32[]{:S(2)}, u32[]{:S(2)}) async-start(bf16[32,8,640]{2,1,0:T(8,128)(2,1)} %pack.1), calls=%async_computation.1 | async-start | bytes 655360 | tf_op jit(solution)/shard_map/all_to_all | solution.py:404
  13.7 0.7 copy-start.3
  14.5 17.2 %copy-start.1 = (bf16[512,512]{1,0:T(8,128)(2,1)S(1)}, bf16[512,512]{1,0:T(8,128)(2,1)}, u32[]{:S(2)}) copy-start(bf16[512,512]{1,0:T(8,128)(2,1)} %constant.18.clone.wide_ref) | copy-start | bytes 1572868
  14.5 17.2 %copy-start.2 = (bf16[128,128]{1,0:T(8,128)(2,1)S(1)}, bf16[128,128]{1,0:T(8,128)(2,1)}, u32[]{:S(2)}) copy-start(bf16[128,128]{1,0:T(8,128)(2,1)} %constant.19.clone.tall_ref) | copy-start | bytes 98308
  27.3 15.3 %collective-permute-start.2 = (bf16[32,8,640]{2,1,0:T(8,128)(2,1)S(1)}, bf16[32,8,640]{2,1,0:T(8,128)(2,1)S(1)}, u32[]{:S(2)}, u32[]{:S(2)}) collective-permute-start(bf16[32,8,640]{2,1,0:T(8,128)(2,1)S(1)} %all-to-all-done.1.here_ref), channel_id=1, source_target_pairs={{0,192},{64,0},{128,64},{192,128},{1,193},{65,1},{129,65},{193,129... | collective-permute-start | bytes 983048 | tf_op jit(solution)/shard_map/ppermute | solution.py:398
  30.0 12.6 %collective-permute-start.1 = (bf16[32,8,640]{2,1,0:T(8,128)(2,1)S(1)}, bf16[32,8,640]{2,1,0:T(8,128)(2,1)S(1)}, u32[]{:S(2)}, u32[]{:S(2)}) collective-permute-start(bf16[32,8,640]{2,1,0:T(8,128)(2,1)S(1)} %all-to-all-done.1.here_ref), channel_id=1, source_target_pairs={{0,128},{64,192},{128,0},{192,64},{1,129},{65,193},{129,1},{193,65... | collective-permute-start | bytes 983048 | tf_op jit(solution)/shard_map/ppermute | solution.py:398
  30.8 15.5 %collective-permute-start = (bf16[32,8,640]{2,1,0:T(8,128)(2,1)S(1)}, bf16[32,8,640]{2,1,0:T(8,128)(2,1)S(1)}, u32[]{:S(2)}, u32[]{:S(2)}) collective-permute-start(bf16[32,8,640]{2,1,0:T(8,128)(2,1)S(1)} %all-to-all-done.1.here_ref), channel_id=1, source_target_pairs={{0,64},{64,128},{128,192},{192,0},{1,65},{65,129},{129,193},{193,1... | collective-permute-start | bytes 983048 | tf_op jit(solution)/shard_map/ppermute | solution.py:398
  51.0 2.0 %collective-permute-start.3 = (f32[256,512]{1,0:T(8,128)S(1)}, f32[256,512]{1,0:T(8,128)S(1)}, u32[]{:S(2)}, u32[]{:S(2)}) collective-permute-start(f32[256,512]{1,0:T(8,128)S(1)} %project.1.mine_ref), channel_id=1, source_target_pairs={{0,1},{1,0},{2,3},{3,2},{4,5},{5,4},{6,7},{7,6},{8,9},{9,8},{10,11... | collective-permute-start | bytes 1572872 | tf_op jit(solution)/shard_map/ppermute | solution.py:398
  54.9 5.0 %collective-permute-start.4 = (f32[32,128]{1,0:T(8,128)S(1)}, f32[32,128]{1,0:T(8,128)S(1)}, u32[]{:S(2)}, u32[]{:S(2)}) collective-permute-start(f32[32,128]{1,0:T(8,128)S(1)} %get-tuple-element.11), channel_id=1, source_target_pairs={{0,64},{64,128},{128,192},{192,0},{1,65},{65,129},{129,193},{193,1... | collective-permute-start | bytes 49160 | tf_op jit(solution)/shard_map/ppermute | solution.py:398
  55.0 5.3 %collective-permute-start.5 = (f32[32,128]{1,0:T(8,128)S(1)}, f32[32,128]{1,0:T(8,128)S(1)}, u32[]{:S(2)}, u32[]{:S(2)}) collective-permute-start(f32[32,128]{1,0:T(8,128)S(1)} %get-tuple-element.12), channel_id=1, source_target_pairs={{0,128},{64,192},{128,0},{192,64},{1,129},{65,193},{129,1},{193,65... | collective-permute-start | bytes 49160 | tf_op jit(solution)/shard_map/ppermute | solution.py:398
  57.0 3.9 %collective-permute-start.6 = (f32[32,128]{1,0:T(8,128)S(1)}, f32[32,128]{1,0:T(8,128)S(1)}, u32[]{:S(2)}, u32[]{:S(2)}) collective-permute-start(f32[32,128]{1,0:T(8,128)S(1)} %get-tuple-element.13), channel_id=1, source_target_pairs={{0,192},{64,0},{128,64},{192,128},{1,193},{65,1},{129,65},{193,129... | collective-permute-start | bytes 49160 | tf_op jit(solution)/shard_map/ppermute | solution.py:398
  61.5 4.9 %collective-permute-start.7 = (f32[8,128]{1,0:T(8,128)S(1)}, f32[8,128]{1,0:T(8,128)S(1)}, u32[]{:S(2)}, u32[]{:S(2)}) collective-permute-start(f32[8,128]{1,0:T(8,128)S(1)} %get-tuple-element.15), channel_id=1, source_target_pairs={{0,16},{16,32},{32,48},{48,0},{1,17},{17,33},{33,49},{49,1},{2,18}... | collective-permute-start | bytes 12296 | tf_op jit(solution)/shard_map/ppermute | solution.py:398
  62.2 5.1 %collective-permute-start.8 = (f32[8,128]{1,0:T(8,128)S(1)}, f32[8,128]{1,0:T(8,128)S(1)}, u32[]{:S(2)}, u32[]{:S(2)}) collective-permute-start(f32[8,128]{1,0:T(8,128)S(1)} %get-tuple-element.16), channel_id=1, source_target_pairs={{0,32},{16,48},{32,0},{48,16},{1,33},{17,49},{33,1},{49,17},{2,34}... | collective-permute-start | bytes 12296 | tf_op jit(solution)/shard_map/ppermute | solution.py:398
  64.3 3.6 %collective-permute-start.9 = (f32[8,128]{1,0:T(8,128)S(1)}, f32[8,128]{1,0:T(8,128)S(1)}, u32[]{:S(2)}, u32[]{:S(2)}) collective-permute-start(f32[8,128]{1,0:T(8,128)S(1)} %get-tuple-element.17), channel_id=1, source_target_pairs={{0,48},{16,0},{32,16},{48,32},{1,49},{17,1},{33,17},{49,33},{2,50}... | collective-permute-start | bytes 12296 | tf_op jit(solution)/shard_map/ppermute | solution.py:398
  78.8 34.5 %all-to-all-start = ((bf16[128,8,512]{2,1,0:T(8,128)(2,1)}), bf16[128,8,512]{2,1,0:T(8,128)(2,1)S(1)}, u32[]{:S(2)}, u32[]{:S(2)}) async-start(bf16[128,8,512]{2,1,0:T(8,128)(2,1)} %smooth.1.tiled_ref), calls=%async_computation | async-start | bytes 2097152 | tf_op jit(solution)/shard_map/all_to_all | solution.py:407

commit v10 on v7

--- a/solution.py
+++ b/solution.py
@@ -4,17 +4,14 @@
 from jax import lax
 from jax.experimental import pallas as pl
 from jax.experimental.pallas import tpu as pltpu
-from jax.sharding import Mesh
 from jax.sharding import PartitionSpec as P
 
 TH = 16
 TW = 32
 MAXS = 8
 ITERS = 2
-TA = ("ta_0", "ta_1", "ta_2")
-YZ = ("ta_1", "ta_2")
-YZX = ("ta_1", "ta_2", "ta_0")
-TA_ROW = ("ta_0", "ta_1", "ta_2", "row")
+TA = "ta"
+TA_ROW = ("ta", "row")
 
 FRAMES = 8
 H = 128
@@ -27,6 +24,7 @@
 PIXELS = TH * TW
 PLANE = 32
 PLANES = 4
+LINE = 8
 MESSAGE = PIXELS + LANES
 ID_LANE = 64
 HIGHEST = lax.Precision.HIGHEST
@@ -39,6 +37,15 @@
     spread = places[:, None] - places[None, :]
     kernel = np.exp(-spread * spread / np.float32(32.0)).astype(np.float32)
     return (kernel / np.sum(kernel, axis=0, keepdims=True, dtype=np.float32)).astype(jnp.bfloat16)
+
+
+def far_end(r):
+    return (r // LINE + 2) % 4 * LINE + (r % LINE + 4) % LINE
+
+
+NEAR_PLANES = [[PLANE * x + r for r in range(PLANE)] for x in range(PLANES)]
+FAR_PLANES = [[PLANE * x + far_end(r) for r in range(PLANE)] for x in range(PLANES)]
+FAR_ALL = [[PLANE * ((r + 2) % PLANES) + far_end(r // PLANES) for r in range(TILES)]]
 
 
 def iota(shape, dim):
@@ -148,7 +155,8 @@
                 )
                 for m in range(4):
                     column = 4 * p + m
-                    at = (16 * lax.rem(ty, 2) + column) * 4 + ty // 2
+                    yz = LINE * (2 - 2 * lax.rem(ty, 2) + column // LINE) + (column + 4) % LINE
+                    at = PLANES * yz + lax.rem(ty // 2 + 2, PLANES)
                     out_ref[at, :, q * LANES : (q + 1) * LANES] = tiles[m].astype(jnp.bfloat16)
         return carry
 
@@ -184,7 +192,7 @@
         extra = owners
         for k, part in enumerate(parts):
             extra = jnp.where(lane // FRAMES == k, pltpu.roll(part, (FRAMES * (k - w)) % LANES, 1), extra)
-        for to in (w, w + PLANE // 2):
+        for to in (far_end(w), far_end(w + PLANE // 2)):
             out_ref[to, :, :PIXELS] = footprints
             out_ref[to, :, PIXELS:] = extra.astype(jnp.bfloat16)
 
@@ -218,8 +226,7 @@
         kx, first = at // 2, many * (at % 2)
         message = (here_ref, left_ref, far_ref, right_ref)[kx][first : first + many]
         source = lax.rem(x + PLANES - kx, PLANES)
-        tile = pl.multiple_of(PLANE * source + first, many)
-        frames = [tiled_ref[PLANES * (first + k) + source] for k in range(many)]
+        frames = [tiled_ref[PLANES * (first + k) + lax.rem(source + 2, PLANES)] for k in range(many)]
         prints = message[:, :, :PIXELS].reshape(rows, PIXELS)
         extra = message[:, :, PIXELS:].astype(jnp.float32).reshape(rows, LANES)
         found = lax.dot_general(
@@ -237,7 +244,9 @@
             terms_ref[span, k * width + NEURONS : (k + 1) * width] = two
         piece = jnp.sum(jnp.where(own_row, extra.reshape(many, SLOTS, LANES), 0.0), axis=1)
         piece = piece + (pltpu.roll(piece, LANES - FRAMES, 1) + pltpu.roll(piece, LANES - 2 * FRAMES, 1))
-        out_ref[pl.ds(tile, many), width:] = piece
+        for k in range(0, many, LINE):
+            tile = pl.multiple_of(PLANE * source + far_end(first + k) // LINE * LINE, LINE)
+            out_ref[pl.ds(tile, LINE), width:] = pltpu.roll(piece[k : k + LINE], LINE // 2, 0)
     sums = dot32(select_ref[...], terms_ref[...])
     out_ref[:, :width] = sums[:, :width] + (sums[:, width : 2 * width] + sums[:, 2 * width :])
 
@@ -347,7 +356,13 @@
 
 
 def store_kernel(arrived_ref, out_ref, sems):
-    copies = [pltpu.make_async_copy(arrived_ref.at[:, x], out_ref.at[x], sems.at[x]) for x in range(PLANES)]
+    copies = []
+    for x in range(PLANES):
+        for y in range(2):
+            for z in range(2):
+                source = arrived_ref.at[y, :, z, :, (x + 2) % PLANES]
+                target = out_ref.at[x, 1 - y, :, 1 - z]
+                copies.append(pltpu.make_async_copy(source, target, sems.at[len(copies)]))
     for copy in copies:
         copy.start()
     for copy in copies:
@@ -357,45 +372,48 @@
 def store(arrived):
     return pl.pallas_call(
         store_kernel,
-        out_shape=jax.ShapeDtypeStruct((PLANES, PLANE, FRAMES, PIXELS), jnp.bfloat16),
+        out_shape=jax.ShapeDtypeStruct((PLANES, 2, 2, 2, 4, FRAMES, PIXELS), jnp.bfloat16),
         in_specs=[VMEM],
         out_specs=pl.BlockSpec(memory_space=pl.ANY),
-        scratch_shapes=[pltpu.SemaphoreType.DMA((PLANES,))],
+        scratch_shapes=[pltpu.SemaphoreType.DMA((4 * PLANES,))],
         cost_estimate=pl.CostEstimate(flops=500_000_000, bytes_accessed=2_000_000, transcendentals=0),
         compiler_params=pltpu.CompilerParams(vmem_limit_bytes=4 << 20),
         name="store",
-    )(arrived.reshape(PLANE, PLANES, FRAMES, PIXELS))
-
-
-def moved(array, axis, by):
-    count = lax.axis_size(axis)
-    return lax.ppermute(array, axis, [(i, (i + by) % count) for i in range(count)])
+    )(arrived.reshape(2, 2, 2, 4, PLANES, FRAMES, PIXELS))
+
+
+def moved(array, by):
+    return lax.ppermute(array, TA, [(t, (t + PLANE * by) % TILES) for t in range(TILES)])
+
+
+def exchanged(array, ranks):
+    return lax.all_to_all(array, TA, 0, 0, tiled=True, axis_index_groups=ranks)
 
 
 def local(movie, shifts, footprint, support, neuron_ids, owner_order, start_traces):
-    where = jnp.stack([lax.axis_index(axis) for axis in ("ta_0", "ta_1", "row")]).astype(jnp.int32)
+    at = lax.axis_index(TA)
+    where = jnp.stack([at // PLANE, at % PLANE // LINE, lax.axis_index("row")]).astype(jnp.int32)
     packed = pack(neuron_ids[0], owner_order, footprint[0, 0], support[0, 0], start_traces.reshape(8, LANES))
-    here = lax.all_to_all(packed, YZ, 0, 0, tiled=True)
+    here = exchanged(packed, FAR_PLANES)
     registered = register(movie[0], shifts[0])
     tiled = smooth(registered)
-    arrived = lax.all_to_all(tiled, YZX, split_axis=0, concat_axis=0, tiled=True)
-    left, far, right = [moved(here, "ta_0", by) for by in range(1, PLANES)]
+    arrived = exchanged(tiled, FAR_ALL)
+    left, far, right = [moved(here, by) for by in range(1, PLANES)]
     mine = project(where, tiled, here, left, far, right)
-    other = moved(mine, "row", 1)
+    other = lax.ppermute(mine, "row", [(0, 1), (1, 0)])
     pieces = solve(where, mine, other)
-    pieces = [pieces[0]] + [moved(pieces[k], "ta_0", k) for k in range(1, PLANES)]
+    pieces = [pieces[0]] + [moved(pieces[k], k) for k in range(1, PLANES)]
     pieces = merge(where, pieces)
-    pieces = lax.all_to_all(pieces.reshape(PLANE, 1, LANES), YZ, 0, 0, tiled=True)
+    pieces = exchanged(pieces.reshape(PLANE, 1, LANES), NEAR_PLANES)
     tile_movie = store(arrived)
     traces = join(pieces.reshape(PLANE, LANES))
     return (tile_movie.reshape(1, 1, -1, PIXELS), traces)
 
 
 def solution(mesh):
-    finer = Mesh(mesh.devices.reshape(4, 4, 8, mesh.shape["row"]), TA_ROW)
     return jax.shard_map(
         local,
-        mesh=finer,
+        mesh=mesh,
         in_specs=(
             P("row", TA, None, None),
             P("row", TA, None, None),

time: 112 us -> 111 us (level)
  waiting for transfers between devices: 48.6 us -> 41.2 us
  starting transfers between devices: 27.2 us -> 34.2 us
    all_to_all x2, waiting for transfers between devices: 36.1 us -> 26.5 us  [exchanged(): return lax.all_to_all(array, TA, 0, 0, tiled=True, axis_index_groups=ranks)]
    all_to_all x2, starting transfers between devices: 19.2 us -> 26.2 us  [exchanged(): return lax.all_to_all(array, TA, 0, 0, tiled=True, axis_index_groups=ranks)]
    ppermute x7, waiting for transfers between devices: 12.5 us -> 14.7 us  [the longest x6 12.8 us: moved(): lax.ppermute(array, TA, [(t, (t + PLANE * by) % TILES) for t in range(TIL...]
  transfers between devices with their start and end apart: 9 -> 9, of which waited for: 9 -> 8; matrix products, arithmetic and copies ran while one was open for 0% -> 0% of each run, Pallas kernels for 6% -> 6%
where the time goes in v10:
time: 111 us
  waiting for transfers between devices  41.2 us (37%)
  starting transfers between devices  34.2 us (31%)
  Pallas kernels  17 us (15%)
  blocking collectives  17 us (15%)
    all_to_all x2, waiting for transfers between devices, exchanged(): return lax.all_to_all(array, TA, 0, 0, tiled=True, axis_index_groups=ranks)  26.5 us
    all_to_all x2, starting transfers between devices, exchanged(): return lax.all_to_all(array, TA, 0, 0, tiled=True, axis_index_groups=ranks)  26.2 us
    all_to_all x1, blocking collectives, exchanged(): return lax.all_to_all(array, TA, 0, 0, tiled=True, axis_index_groups=ranks)  17 us
    ppermute x6, waiting for transfers between devices, moved(): lax.ppermute(array, TA, [(t, (t + PLANE * by) % TILES) for t in range(TIL...  12.8 us
    ppermute x6, starting transfers between devices, moved(): lax.ppermute(array, TA, [(t, (t + PLANE * by) % TILES) for t in range(TIL...  7.95 us
    pallas_call x1, Pallas kernels, project(): pl.pallas_call(project_kernel, out_shape=jax.ShapeDtypeStruct((NEURONS, N...  4.7 us
    pallas_call x1, Pallas kernels, smooth(): pl.pallas_call(smooth_kernel, out_shape=jax.ShapeDtypeStruct((TILES, FRAM...  4.55 us
  transfers between devices with their start and end apart: 9, of which 8 were waited for; matrix products, arithmetic and copies ran while one was open for 0% of the time, Pallas kernels for 6%

profile of v10, /device:TPU:8, one launch (start us, length us, event | category | flops | bytes accessed | tf_op | source)
XLA Modules:
  0.0 111.0 jit_solution(16725396253849242226)
XLA Ops:
  0.6 1.7 %pack.1 = bf16[32,8,640]{2,1,0:T(8,128)(2,1)} custom-call(s32[1,8]{1,0:T(1,128)} %bitcast.24, s32[256]{0:T(256)} %order_ref.1, bf16[8,512]{1,0:T(8,128)(2,1)} %bitcast.22, s32[8,512]{1,0:T(8,128)} %bitcast.21, f32[8,128]{1,0:T(8,128)} %bitcast.23), custom_call_target="tpu_custom_call" | custom-call | flops 200000000 | bytes 200000 | tf_op jit(solution)/shard_map/pack/pallas_call | solution.py:201
  2.3 12.3 %all-to-all-start.1 = ((bf16[32,8,640]{2,1,0:T(8,128)(2,1)}), bf16[32,8,640]{2,1,0:T(8,128)(2,1)S(1)}, u32[]{:S(2)}, u32[]{:S(2)}) async-start(bf16[32,8,640]{2,1,0:T(8,128)(2,1)} %pack.1), calls=%async_computation.1 | async-start | bytes 655360 | tf_op jit(solution)/shard_map/all_to_all | solution.py:390
  14.7 0.7 copy-done.3
  15.6 1.8 %register.1.registered_ref = bf16[8,128,512]{2,1,0:T(8,128)(2,1)S(1)} custom-call(s32[8,4,2]{2,1,0:T(4,128)S(1)} %copy.14.shifts_ref, bf16[8,128,512]{2,1,0:T(8,128)(2,1)S(1)} %bitcast.18), custom_call_target="tpu_custom_call" | custom-call | flops 2000000000 | bytes 2000000 | tf_op jit(solution)/shard_map/register/pallas_call | solution.py:108
  17.4 6.2 %all-to-all-done.1.here_ref = bf16[32,8,640]{2,1,0:T(8,128)(2,1)S(1)} async-done(((bf16[32,8,640]{2,1,0:T(8,128)(2,1)}), bf16[32,8,640]{2,1,0:T(8,128)(2,1)S(1)}, u32[]{:S(2)}, u32[]{:S(2)}) %all-to-all-start.1) | async-done | bytes 327712 | tf_op jit(solution)/shard_map/all_to_all | solution.py:390
  23.6 2.8 %collective-permute-start.2 = (bf16[32,8,640]{2,1,0:T(8,128)(2,1)S(1)}, bf16[32,8,640]{2,1,0:T(8,128)(2,1)S(1)}, u32[]{:S(2)}, u32[]{:S(2)}) collective-permute-start(bf16[32,8,640]{2,1,0:T(8,128)(2,1)S(1)} %all-to-all-done.1.here_ref), channel_id=1, source_target_pairs={{0,192},{2,194},{4,196},{6,198},{8,200},{10,202},{12,204},{14,206}... | collective-permute-start | bytes 983048 | tf_op jit(solution)/shard_map/ppermute | solution.py:386
  26.3 0.8 collective-permute-start.1
  27.1 0.9 collective-permute-start
  28.0 4.6 %smooth.1.tiled_ref = bf16[128,8,512]{2,1,0:T(8,128)(2,1)} custom-call(bf16[8,128,512]{2,1,0:T(8,128)(2,1)S(1)} %register.1.registered_ref, bf16[512,512]{1,0:T(8,128)(2,1)S(1)} %copy-done.1, bf16[128,128]{1,0:T(8,128)(2,1)S(1)} %copy-done.2), custom_call_target="tpu_custom_call" | custom-call | flops 4000000000 | bytes 3000000 | tf_op jit(solution)/shard_map/smooth/pallas_call | solution.py:167
  32.6 6.6 %collective-permute-done.2.right_ref = bf16[32,8,640]{2,1,0:T(8,128)(2,1)S(1)} collective-permute-done((bf16[32,8,640]{2,1,0:T(8,128)(2,1)S(1)}, bf16[32,8,640]{2,1,0:T(8,128)(2,1)S(1)}, u32[]{:S(2)}, u32[]{:S(2)}) %collective-permute-start.2) | collective-permute-done | bytes 327712 | tf_op jit(solution)/shard_map/ppermute | solution.py:386
  39.2 3.7 %collective-permute-done.left_ref = bf16[32,8,640]{2,1,0:T(8,128)(2,1)S(1)} collective-permute-done((bf16[32,8,640]{2,1,0:T(8,128)(2,1)S(1)}, bf16[32,8,640]{2,1,0:T(8,128)(2,1)S(1)}, u32[]{:S(2)}, u32[]{:S(2)}) %collective-permute-start) | collective-permute-done | bytes 327712 | tf_op jit(solution)/shard_map/ppermute | solution.py:386
  42.8 4.7 %project.1.mine_ref = f32[256,512]{1,0:T(8,128)S(1)} custom-call(s32[3]{0:T(128)S(1)} %pad_add_fusion.where_ref, bf16[128,8,512]{2,1,0:T(8,128)(2,1)} %smooth.1.tiled_ref, bf16[32,8,640]{2,1,0:T(8,128)(2,1)S(1)} %all-to-all-done.1.here_ref, bf16[32,8,640]{2,1,0:T(8,128)(2,1)S(1)} %collective-permute-done.left_ref, ...), custom_call_target="tpu_custom_call" | custom-call | flops 2000000000 | bytes 3000000 | tf_op jit(solution)/shard_map/project/pallas_call | solution.py:256
  47.7 1.9 %collective-permute-done.3.other_ref = f32[256,512]{1,0:T(8,128)S(1)} collective-permute-done((f32[256,512]{1,0:T(8,128)S(1)}, f32[256,512]{1,0:T(8,128)S(1)}, u32[]{:S(2)}, u32[]{:S(2)}) %collective-permute-start.3) | collective-permute-done | bytes 524320 | tf_op jit(solution)/shard_map/ppermute | solution.py:403
  49.5 1.9 %solve.1 = (f32[32,128]{1,0:T(8,128)S(1)}, f32[32,128]{1,0:T(8,128)S(1)}, f32[32,128]{1,0:T(8,128)S(1)}, f32[32,128]{1,0:T(8,128)S(1)}) custom-call(s32[3]{0:T(128)S(1)} %pad_add_fusion.where_ref, f32[256,512]{1,0:T(8,128)S(1)} %project.1.mine_ref, f32[256,512]{1,0:T(8,128)S(1)} %collective-permute-done.3.other_ref), custom_call_target="tpu_custom_call" | custom-call | flops 2000000000 | bytes 1000000 | tf_op jit(solution)/shard_map/solve/pallas_call | solution.py:300
  51.5 2.1 %collective-permute-start.5 = (f32[32,128]{1,0:T(8,128)S(1)}, f32[32,128]{1,0:T(8,128)S(1)}, u32[]{:S(2)}, u32[]{:S(2)}) collective-permute-start(f32[32,128]{1,0:T(8,128)S(1)} %get-tuple-element.8), channel_id=1, source_target_pairs={{0,128},{2,130},{4,132},{6,134},{8,136},{10,138},{12,140},{14,142}... | collective-permute-start | bytes 49160 | tf_op jit(solution)/shard_map/ppermute | solution.py:386
  53.6 1.4 %collective-permute-start.6 = (f32[32,128]{1,0:T(8,128)S(1)}, f32[32,128]{1,0:T(8,128)S(1)}, u32[]{:S(2)}, u32[]{:S(2)}) collective-permute-start(f32[32,128]{1,0:T(8,128)S(1)} %get-tuple-element.9), channel_id=1, source_target_pairs={{0,192},{2,194},{4,196},{6,198},{8,200},{10,202},{12,204},{14,206}... | collective-permute-start | bytes 49160 | tf_op jit(solution)/shard_map/ppermute | solution.py:386
  55.0 1.5 %collective-permute-done.4.refs_1_ = f32[32,128]{1,0:T(8,128)S(1)} collective-permute-done((f32[32,128]{1,0:T(8,128)S(1)}, f32[32,128]{1,0:T(8,128)S(1)}, u32[]{:S(2)}, u32[]{:S(2)}) %collective-permute-start.4) | collective-permute-done | bytes 16416 | tf_op jit(solution)/shard_map/ppermute | solution.py:386
  56.9 0.6 collective-permute-done.6.refs_3_
  57.5 0.6 merge.1
  58.1 17.0 %all_to_all.15 = f32[32,1,128]{2,1,0:T(1,128)S(1)} all-to-all(f32[32,1,128]{2,1,0:T(1,128)S(1)} %bitcast.17), channel_id=1, replica_groups={{0,2,4,6,8,10,12,14,16,18,20,22,24,26,28,30,32,34,36,38,40,42,44,46,48,..., dimensions={0} | all-to-all | bytes 32768 | tf_op jit(solution)/shard_map/all_to_all | solution.py:390
  75.1 13.8 %all-to-all-start = ((bf16[128,8,512]{2,1,0:T(8,128)(2,1)}), bf16[128,8,512]{2,1,0:T(8,128)(2,1)S(1)}, u32[]{:S(2)}, u32[]{:S(2)}) async-start(bf16[128,8,512]{2,1,0:T(8,128)(2,1)} %smooth.1.tiled_ref), calls=%async_computation | async-start | bytes 2097152 | tf_op jit(solution)/shard_map/all_to_all | solution.py:390
  88.9 0.7 join.1
  89.6 20.3 %all-to-all-done = bf16[128,8,512]{2,1,0:T(8,128)(2,1)S(1)} async-done(((bf16[128,8,512]{2,1,0:T(8,128)(2,1)}), bf16[128,8,512]{2,1,0:T(8,128)(2,1)S(1)}, u32[]{:S(2)}, u32[]{:S(2)}) %all-to-all-start) | async-done | bytes 1048608 | tf_op jit(solution)/shard_map/all_to_all | solution.py:390
  109.9 1.1 store.1
  (13 shorter events, 0.8 us)
Async XLA Ops:
  0.6 14.9 %copy-start = (bf16[1,8,128,512]{3,2,1,0:T(8,128)(2,1)S(1)}, bf16[1,8,128,512]{3,2,1,0:T(8,128)(2,1)}, u32[]{:S(2)}) copy-start(bf16[1,8,128,512]{3,2,1,0:T(8,128)(2,1)} %param.9) | copy-start | bytes 3145732
  2.3 21.3 %all-to-all-start.1 = ((bf16[32,8,640]{2,1,0:T(8,128)(2,1)}), bf16[32,8,640]{2,1,0:T(8,128)(2,1)S(1)}, u32[]{:S(2)}, u32[]{:S(2)}) async-start(bf16[32,8,640]{2,1,0:T(8,128)(2,1)} %pack.1), calls=%async_computation.1 | async-start | bytes 655360 | tf_op jit(solution)/shard_map/all_to_all | solution.py:390
  14.7 0.7 copy-start.3
  15.6 12.4 %copy-start.1 = (bf16[512,512]{1,0:T(8,128)(2,1)S(1)}, bf16[512,512]{1,0:T(8,128)(2,1)}, u32[]{:S(2)}) copy-start(bf16[512,512]{1,0:T(8,128)(2,1)} %constant.49.clone.wide_ref) | copy-start | bytes 1572868
  15.6 12.4 %copy-start.2 = (bf16[128,128]{1,0:T(8,128)(2,1)S(1)}, bf16[128,128]{1,0:T(8,128)(2,1)}, u32[]{:S(2)}) copy-start(bf16[128,128]{1,0:T(8,128)(2,1)} %constant.50.clone.tall_ref) | copy-start | bytes 98308
  23.6 15.6 %collective-permute-start.2 = (bf16[32,8,640]{2,1,0:T(8,128)(2,1)S(1)}, bf16[32,8,640]{2,1,0:T(8,128)(2,1)S(1)}, u32[]{:S(2)}, u32[]{:S(2)}) collective-permute-start(bf16[32,8,640]{2,1,0:T(8,128)(2,1)S(1)} %all-to-all-done.1.here_ref), channel_id=1, source_target_pairs={{0,192},{2,194},{4,196},{6,198},{8,200},{10,202},{12,204},{14,206}... | collective-permute-start | bytes 983048 | tf_op jit(solution)/shard_map/ppermute | solution.py:386
  26.3 12.9 %collective-permute-start.1 = (bf16[32,8,640]{2,1,0:T(8,128)(2,1)S(1)}, bf16[32,8,640]{2,1,0:T(8,128)(2,1)S(1)}, u32[]{:S(2)}, u32[]{:S(2)}) collective-permute-start(bf16[32,8,640]{2,1,0:T(8,128)(2,1)S(1)} %all-to-all-done.1.here_ref), channel_id=1, source_target_pairs={{0,128},{2,130},{4,132},{6,134},{8,136},{10,138},{12,140},{14,142}... | collective-permute-start | bytes 983048 | tf_op jit(solution)/shard_map/ppermute | solution.py:386
  27.1 15.7 %collective-permute-start = (bf16[32,8,640]{2,1,0:T(8,128)(2,1)S(1)}, bf16[32,8,640]{2,1,0:T(8,128)(2,1)S(1)}, u32[]{:S(2)}, u32[]{:S(2)}) collective-permute-start(bf16[32,8,640]{2,1,0:T(8,128)(2,1)S(1)} %all-to-all-done.1.here_ref), channel_id=1, source_target_pairs={{0,64},{2,66},{4,68},{6,70},{8,72},{10,74},{12,76},{14,78},{16,80}... | collective-permute-start | bytes 983048 | tf_op jit(solution)/shard_map/ppermute | solution.py:386
  47.5 2.0 %collective-permute-start.3 = (f32[256,512]{1,0:T(8,128)S(1)}, f32[256,512]{1,0:T(8,128)S(1)}, u32[]{:S(2)}, u32[]{:S(2)}) collective-permute-start(f32[256,512]{1,0:T(8,128)S(1)} %project.1.mine_ref), channel_id=1, source_target_pairs={{0,1},{1,0},{2,3},{3,2},{4,5},{5,4},{6,7},{7,6},{8,9},{9,8},{10,11... | collective-permute-start | bytes 1572872 | tf_op jit(solution)/shard_map/ppermute | solution.py:403
  51.5 5.0 %collective-permute-start.4 = (f32[32,128]{1,0:T(8,128)S(1)}, f32[32,128]{1,0:T(8,128)S(1)}, u32[]{:S(2)}, u32[]{:S(2)}) collective-permute-start(f32[32,128]{1,0:T(8,128)S(1)} %get-tuple-element.7), channel_id=1, source_target_pairs={{0,64},{2,66},{4,68},{6,70},{8,72},{10,74},{12,76},{14,78},{16,80}... | collective-permute-start | bytes 49160 | tf_op jit(solution)/shard_map/ppermute | solution.py:386
  51.5 5.3 %collective-permute-start.5 = (f32[32,128]{1,0:T(8,128)S(1)}, f32[32,128]{1,0:T(8,128)S(1)}, u32[]{:S(2)}, u32[]{:S(2)}) collective-permute-start(f32[32,128]{1,0:T(8,128)S(1)} %get-tuple-element.8), channel_id=1, source_target_pairs={{0,128},{2,130},{4,132},{6,134},{8,136},{10,138},{12,140},{14,142}... | collective-permute-start | bytes 49160 | tf_op jit(solution)/shard_map/ppermute | solution.py:386
  53.6 3.9 %collective-permute-start.6 = (f32[32,128]{1,0:T(8,128)S(1)}, f32[32,128]{1,0:T(8,128)S(1)}, u32[]{:S(2)}, u32[]{:S(2)}) collective-permute-start(f32[32,128]{1,0:T(8,128)S(1)} %get-tuple-element.9), channel_id=1, source_target_pairs={{0,192},{2,194},{4,196},{6,198},{8,200},{10,202},{12,204},{14,206}... | collective-permute-start | bytes 49160 | tf_op jit(solution)/shard_map/ppermute | solution.py:386
  75.1 34.8 %all-to-all-start = ((bf16[128,8,512]{2,1,0:T(8,128)(2,1)}), bf16[128,8,512]{2,1,0:T(8,128)(2,1)S(1)}, u32[]{:S(2)}, u32[]{:S(2)}) async-start(bf16[128,8,512]{2,1,0:T(8,128)(2,1)} %smooth.1.tiled_ref), calls=%async_computation | async-start | bytes 2097152 | tf_op jit(solution)/shard_map/all_to_all | solution.py:390

commit v11 on v10

--- a/solution.py
+++ b/solution.py
@@ -43,7 +43,6 @@
     return (r // LINE + 2) % 4 * LINE + (r % LINE + 4) % LINE
 
 
-NEAR_PLANES = [[PLANE * x + r for r in range(PLANE)] for x in range(PLANES)]
 FAR_PLANES = [[PLANE * x + far_end(r) for r in range(PLANE)] for x in range(PLANES)]
 FAR_ALL = [[PLANE * ((r + 2) % PLANES) + far_end(r // PLANES) for r in range(TILES)]]
 
@@ -309,12 +308,17 @@
     )(where, mine, other)
 
 
+def ranked(rows):
+    groups = [far_end(r) // LINE * LINE for r in range(0, PLANE, LINE)]
+    return jnp.concatenate([pltpu.roll(rows[g : g + LINE], LINE // 2, 0) for g in groups], axis=0)
+
+
 def merge_kernel(where_ref, *refs):
     group = lax.rem(iota((PLANE, LANES), 1) // FRAMES, PLANES)
     merged = refs[0][...]
     for k in range(1, PLANES):
         merged = jnp.where(group == lax.rem(where_ref[0] + PLANES - k, PLANES), refs[k][...], merged)
-    refs[PLANES][...] = merged
+    refs[PLANES][...] = ranked(merged)
 
 
 def merge(where, pieces):
@@ -331,7 +335,7 @@
 
 def join_kernel(pieces_ref, out_ref):
     near = LANES // FRAMES
-    pieces = pieces_ref[...]
+    pieces = ranked(pieces_ref[...])
     rolled = [pieces] + [pltpu.roll(pieces, FRAMES * j, 1) for j in range(1, PLANES)]
     group = iota((near, LANES), 1) // FRAMES
     inside = group == iota((near, LANES), 0)
@@ -404,7 +408,7 @@
     pieces = solve(where, mine, other)
     pieces = [pieces[0]] + [moved(pieces[k], k) for k in range(1, PLANES)]
     pieces = merge(where, pieces)
-    pieces = exchanged(pieces.reshape(PLANE, 1, LANES), NEAR_PLANES)
+    pieces = exchanged(pieces.reshape(PLANE, 1, LANES), FAR_PLANES)
     tile_movie = store(arrived)
     traces = join(pieces.reshape(PLANE, LANES))
     return (tile_movie.reshape(1, 1, -1, PIXELS), traces)

time: 111 us -> 107 us (0.964)
  blocking collectives: 17 us -> 13.1 us
    all_to_all x1, blocking collectives: 17 us -> 13.1 us  [exchanged(): return lax.all_to_all(array, TA, 0, 0, tiled=True, axis_index_groups=ranks)]
  transfers between devices with their start and end apart: 9 -> 9, of which waited for: 8 -> 8; matrix products, arithmetic and copies ran while one was open for 0% -> 0% of each run, Pallas kernels for 6% -> 7%
where the time goes in v11:
time: 107 us
  waiting for transfers between devices  41.2 us (39%)
  starting transfers between devices  34 us (32%)
  Pallas kernels  17 us (16%)
  blocking collectives  13.1 us (12%)
    all_to_all x2, waiting for transfers between devices, exchanged(): return lax.all_to_all(array, TA, 0, 0, tiled=True, axis_index_groups=ranks)  26.5 us
    all_to_all x2, starting transfers between devices, exchanged(): return lax.all_to_all(array, TA, 0, 0, tiled=True, axis_index_groups=ranks)  26 us
    all_to_all x1, blocking collectives, exchanged(): return lax.all_to_all(array, TA, 0, 0, tiled=True, axis_index_groups=ranks)  13.1 us
    ppermute x6, waiting for transfers between devices, moved(): lax.ppermute(array, TA, [(t, (t + PLANE * by) % TILES) for t in range(TIL...  12.8 us
    ppermute x6, starting transfers between devices, moved(): lax.ppermute(array, TA, [(t, (t + PLANE * by) % TILES) for t in range(TIL...  7.95 us
    pallas_call x1, Pallas kernels, project(): pl.pallas_call(project_kernel, out_shape=jax.ShapeDtypeStruct((NEURONS, N...  4.7 us
    pallas_call x1, Pallas kernels, smooth(): pl.pallas_call(smooth_kernel, out_shape=jax.ShapeDtypeStruct((TILES, FRAM...  4.55 us
  transfers between devices with their start and end apart: 9, of which 8 were waited for; matrix products, arithmetic and copies ran while one was open for 0% of the time, Pallas kernels for 7%

profile of v11, /device:TPU:8, one launch (start us, length us, event | category | flops | bytes accessed | tf_op | source)
XLA Modules:
  0.0 107.0 jit_solution(15939144974559968419)
XLA Ops:
  0.6 1.7 %pack.1 = bf16[32,8,640]{2,1,0:T(8,128)(2,1)} custom-call(s32[1,8]{1,0:T(1,128)} %bitcast.24, s32[256]{0:T(256)} %order_ref.1, bf16[8,512]{1,0:T(8,128)(2,1)} %bitcast.22, s32[8,512]{1,0:T(8,128)} %bitcast.21, f32[8,128]{1,0:T(8,128)} %bitcast.23), custom_call_target="tpu_custom_call" | custom-call | flops 200000000 | bytes 200000 | tf_op jit(solution)/shard_map/pack/pallas_call | solution.py:200
  2.3 12.3 %all-to-all-start.1 = ((bf16[32,8,640]{2,1,0:T(8,128)(2,1)}), bf16[32,8,640]{2,1,0:T(8,128)(2,1)S(1)}, u32[]{:S(2)}, u32[]{:S(2)}) async-start(bf16[32,8,640]{2,1,0:T(8,128)(2,1)} %pack.1), calls=%async_computation.1 | async-start | bytes 655360 | tf_op jit(solution)/shard_map/all_to_all | solution.py:394
  14.7 0.7 copy-done.3
  15.6 1.8 %register.1.registered_ref = bf16[8,128,512]{2,1,0:T(8,128)(2,1)S(1)} custom-call(s32[8,4,2]{2,1,0:T(4,128)S(1)} %copy.14.shifts_ref, bf16[8,128,512]{2,1,0:T(8,128)(2,1)S(1)} %bitcast.18), custom_call_target="tpu_custom_call" | custom-call | flops 2000000000 | bytes 2000000 | tf_op jit(solution)/shard_map/register/pallas_call | solution.py:107
  17.4 6.2 %all-to-all-done.1.here_ref = bf16[32,8,640]{2,1,0:T(8,128)(2,1)S(1)} async-done(((bf16[32,8,640]{2,1,0:T(8,128)(2,1)}), bf16[32,8,640]{2,1,0:T(8,128)(2,1)S(1)}, u32[]{:S(2)}, u32[]{:S(2)}) %all-to-all-start.1) | async-done | bytes 327712 | tf_op jit(solution)/shard_map/all_to_all | solution.py:394
  23.6 2.8 %collective-permute-start.2 = (bf16[32,8,640]{2,1,0:T(8,128)(2,1)S(1)}, bf16[32,8,640]{2,1,0:T(8,128)(2,1)S(1)}, u32[]{:S(2)}, u32[]{:S(2)}) collective-permute-start(bf16[32,8,640]{2,1,0:T(8,128)(2,1)S(1)} %all-to-all-done.1.here_ref), channel_id=1, source_target_pairs={{0,192},{2,194},{4,196},{6,198},{8,200},{10,202},{12,204},{14,206}... | collective-permute-start | bytes 983048 | tf_op jit(solution)/shard_map/ppermute | solution.py:390
  26.3 0.8 collective-permute-start.1
  27.1 0.9 collective-permute-start
  28.0 4.6 %smooth.1.tiled_ref = bf16[128,8,512]{2,1,0:T(8,128)(2,1)} custom-call(bf16[8,128,512]{2,1,0:T(8,128)(2,1)S(1)} %register.1.registered_ref, bf16[512,512]{1,0:T(8,128)(2,1)S(1)} %copy-done.1, bf16[128,128]{1,0:T(8,128)(2,1)S(1)} %copy-done.2), custom_call_target="tpu_custom_call" | custom-call | flops 4000000000 | bytes 3000000 | tf_op jit(solution)/shard_map/smooth/pallas_call | solution.py:166
  32.6 6.6 %collective-permute-done.2.right_ref = bf16[32,8,640]{2,1,0:T(8,128)(2,1)S(1)} collective-permute-done((bf16[32,8,640]{2,1,0:T(8,128)(2,1)S(1)}, bf16[32,8,640]{2,1,0:T(8,128)(2,1)S(1)}, u32[]{:S(2)}, u32[]{:S(2)}) %collective-permute-start.2) | collective-permute-done | bytes 327712 | tf_op jit(solution)/shard_map/ppermute | solution.py:390
  39.2 3.7 %collective-permute-done.left_ref = bf16[32,8,640]{2,1,0:T(8,128)(2,1)S(1)} collective-permute-done((bf16[32,8,640]{2,1,0:T(8,128)(2,1)S(1)}, bf16[32,8,640]{2,1,0:T(8,128)(2,1)S(1)}, u32[]{:S(2)}, u32[]{:S(2)}) %collective-permute-start) | collective-permute-done | bytes 327712 | tf_op jit(solution)/shard_map/ppermute | solution.py:390
  42.8 4.7 %project.1.mine_ref = f32[256,512]{1,0:T(8,128)S(1)} custom-call(s32[3]{0:T(128)S(1)} %pad_add_fusion.where_ref, bf16[128,8,512]{2,1,0:T(8,128)(2,1)} %smooth.1.tiled_ref, bf16[32,8,640]{2,1,0:T(8,128)(2,1)S(1)} %all-to-all-done.1.here_ref, bf16[32,8,640]{2,1,0:T(8,128)(2,1)S(1)} %collective-permute-done.left_ref, ...), custom_call_target="tpu_custom_call" | custom-call | flops 2000000000 | bytes 3000000 | tf_op jit(solution)/shard_map/project/pallas_call | solution.py:255
  47.7 1.9 %collective-permute-done.3.other_ref = f32[256,512]{1,0:T(8,128)S(1)} collective-permute-done((f32[256,512]{1,0:T(8,128)S(1)}, f32[256,512]{1,0:T(8,128)S(1)}, u32[]{:S(2)}, u32[]{:S(2)}) %collective-permute-start.3) | collective-permute-done | bytes 524320 | tf_op jit(solution)/shard_map/ppermute | solution.py:407
  49.5 1.9 %solve.1 = (f32[32,128]{1,0:T(8,128)S(1)}, f32[32,128]{1,0:T(8,128)S(1)}, f32[32,128]{1,0:T(8,128)S(1)}, f32[32,128]{1,0:T(8,128)S(1)}) custom-call(s32[3]{0:T(128)S(1)} %pad_add_fusion.where_ref, f32[256,512]{1,0:T(8,128)S(1)} %project.1.mine_ref, f32[256,512]{1,0:T(8,128)S(1)} %collective-permute-done.3.other_ref), custom_call_target="tpu_custom_call" | custom-call | flops 2000000000 | bytes 1000000 | tf_op jit(solution)/shard_map/solve/pallas_call | solution.py:299
  51.5 2.1 %collective-permute-start.5 = (f32[32,128]{1,0:T(8,128)S(1)}, f32[32,128]{1,0:T(8,128)S(1)}, u32[]{:S(2)}, u32[]{:S(2)}) collective-permute-start(f32[32,128]{1,0:T(8,128)S(1)} %get-tuple-element.8), channel_id=1, source_target_pairs={{0,128},{2,130},{4,132},{6,134},{8,136},{10,138},{12,140},{14,142}... | collective-permute-start | bytes 49160 | tf_op jit(solution)/shard_map/ppermute | solution.py:390
  53.6 1.4 %collective-permute-start.6 = (f32[32,128]{1,0:T(8,128)S(1)}, f32[32,128]{1,0:T(8,128)S(1)}, u32[]{:S(2)}, u32[]{:S(2)}) collective-permute-start(f32[32,128]{1,0:T(8,128)S(1)} %get-tuple-element.9), channel_id=1, source_target_pairs={{0,192},{2,194},{4,196},{6,198},{8,200},{10,202},{12,204},{14,206}... | collective-permute-start | bytes 49160 | tf_op jit(solution)/shard_map/ppermute | solution.py:390
  55.0 1.5 %collective-permute-done.4.refs_1_ = f32[32,128]{1,0:T(8,128)S(1)} collective-permute-done((f32[32,128]{1,0:T(8,128)S(1)}, f32[32,128]{1,0:T(8,128)S(1)}, u32[]{:S(2)}, u32[]{:S(2)}) %collective-permute-start.4) | collective-permute-done | bytes 16416 | tf_op jit(solution)/shard_map/ppermute | solution.py:390
  56.9 0.6 collective-permute-done.6.refs_3_
  57.5 0.6 merge.1
  58.1 13.1 %all_to_all.15 = f32[32,1,128]{2,1,0:T(1,128)S(1)} all-to-all(f32[32,1,128]{2,1,0:T(1,128)S(1)} %bitcast.17), channel_id=1, replica_groups={{40,42,44,46,32,34,36,38,56,58,60,62,48,50,52,54,8,10,12,14,0,2,4,6,24,..., dimensions={0} | all-to-all | bytes 32768 | tf_op jit(solution)/shard_map/all_to_all | solution.py:394
  71.2 13.6 %all-to-all-start = ((bf16[128,8,512]{2,1,0:T(8,128)(2,1)}), bf16[128,8,512]{2,1,0:T(8,128)(2,1)S(1)}, u32[]{:S(2)}, u32[]{:S(2)}) async-start(bf16[128,8,512]{2,1,0:T(8,128)(2,1)} %smooth.1.tiled_ref), calls=%async_computation | async-start | bytes 2097152 | tf_op jit(solution)/shard_map/all_to_all | solution.py:394
  84.9 0.7 join.1
  85.6 20.3 %all-to-all-done = bf16[128,8,512]{2,1,0:T(8,128)(2,1)S(1)} async-done(((bf16[128,8,512]{2,1,0:T(8,128)(2,1)}), bf16[128,8,512]{2,1,0:T(8,128)(2,1)S(1)}, u32[]{:S(2)}, u32[]{:S(2)}) %all-to-all-start) | async-done | bytes 1048608 | tf_op jit(solution)/shard_map/all_to_all | solution.py:394
  105.9 1.1 %store.1 = bf16[4,2,2,2,4,8,512]{6,5,4,3,2,1,0:T(8,128)(2,1)} custom-call(bf16[2,2,2,4,4,8,512]{6,5,4,3,2,1,0:T(8,128)(2,1)S(1)} %bitcast.15), custom_call_target="tpu_custom_call" | custom-call | flops 500000000 | bytes 2000000 | tf_op jit(solution)/shard_map/store/pallas_call | solution.py:377
  (13 shorter events, 0.8 us)
Async XLA Ops:
  0.6 14.9 %copy-start = (bf16[1,8,128,512]{3,2,1,0:T(8,128)(2,1)S(1)}, bf16[1,8,128,512]{3,2,1,0:T(8,128)(2,1)}, u32[]{:S(2)}) copy-start(bf16[1,8,128,512]{3,2,1,0:T(8,128)(2,1)} %param.9) | copy-start | bytes 3145732
  2.3 21.3 %all-to-all-start.1 = ((bf16[32,8,640]{2,1,0:T(8,128)(2,1)}), bf16[32,8,640]{2,1,0:T(8,128)(2,1)S(1)}, u32[]{:S(2)}, u32[]{:S(2)}) async-start(bf16[32,8,640]{2,1,0:T(8,128)(2,1)} %pack.1), calls=%async_computation.1 | async-start | bytes 655360 | tf_op jit(solution)/shard_map/all_to_all | solution.py:394
  14.7 0.7 copy-start.3
  15.6 12.4 %copy-start.1 = (bf16[512,512]{1,0:T(8,128)(2,1)S(1)}, bf16[512,512]{1,0:T(8,128)(2,1)}, u32[]{:S(2)}) copy-start(bf16[512,512]{1,0:T(8,128)(2,1)} %constant.49.clone.wide_ref) | copy-start | bytes 1572868
  15.6 12.4 %copy-start.2 = (bf16[128,128]{1,0:T(8,128)(2,1)S(1)}, bf16[128,128]{1,0:T(8,128)(2,1)}, u32[]{:S(2)}) copy-start(bf16[128,128]{1,0:T(8,128)(2,1)} %constant.50.clone.tall_ref) | copy-start | bytes 98308
  23.6 15.6 %collective-permute-start.2 = (bf16[32,8,640]{2,1,0:T(8,128)(2,1)S(1)}, bf16[32,8,640]{2,1,0:T(8,128)(2,1)S(1)}, u32[]{:S(2)}, u32[]{:S(2)}) collective-permute-start(bf16[32,8,640]{2,1,0:T(8,128)(2,1)S(1)} %all-to-all-done.1.here_ref), channel_id=1, source_target_pairs={{0,192},{2,194},{4,196},{6,198},{8,200},{10,202},{12,204},{14,206}... | collective-permute-start | bytes 983048 | tf_op jit(solution)/shard_map/ppermute | solution.py:390
  26.3 12.9 %collective-permute-start.1 = (bf16[32,8,640]{2,1,0:T(8,128)(2,1)S(1)}, bf16[32,8,640]{2,1,0:T(8,128)(2,1)S(1)}, u32[]{:S(2)}, u32[]{:S(2)}) collective-permute-start(bf16[32,8,640]{2,1,0:T(8,128)(2,1)S(1)} %all-to-all-done.1.here_ref), channel_id=1, source_target_pairs={{0,128},{2,130},{4,132},{6,134},{8,136},{10,138},{12,140},{14,142}... | collective-permute-start | bytes 983048 | tf_op jit(solution)/shard_map/ppermute | solution.py:390
  27.1 15.7 %collective-permute-start = (bf16[32,8,640]{2,1,0:T(8,128)(2,1)S(1)}, bf16[32,8,640]{2,1,0:T(8,128)(2,1)S(1)}, u32[]{:S(2)}, u32[]{:S(2)}) collective-permute-start(bf16[32,8,640]{2,1,0:T(8,128)(2,1)S(1)} %all-to-all-done.1.here_ref), channel_id=1, source_target_pairs={{0,64},{2,66},{4,68},{6,70},{8,72},{10,74},{12,76},{14,78},{16,80}... | collective-permute-start | bytes 983048 | tf_op jit(solution)/shard_map/ppermute | solution.py:390
  47.5 2.0 %collective-permute-start.3 = (f32[256,512]{1,0:T(8,128)S(1)}, f32[256,512]{1,0:T(8,128)S(1)}, u32[]{:S(2)}, u32[]{:S(2)}) collective-permute-start(f32[256,512]{1,0:T(8,128)S(1)} %project.1.mine_ref), channel_id=1, source_target_pairs={{0,1},{1,0},{2,3},{3,2},{4,5},{5,4},{6,7},{7,6},{8,9},{9,8},{10,11... | collective-permute-start | bytes 1572872 | tf_op jit(solution)/shard_map/ppermute | solution.py:407
  51.5 5.0 %collective-permute-start.4 = (f32[32,128]{1,0:T(8,128)S(1)}, f32[32,128]{1,0:T(8,128)S(1)}, u32[]{:S(2)}, u32[]{:S(2)}) collective-permute-start(f32[32,128]{1,0:T(8,128)S(1)} %get-tuple-element.7), channel_id=1, source_target_pairs={{0,64},{2,66},{4,68},{6,70},{8,72},{10,74},{12,76},{14,78},{16,80}... | collective-permute-start | bytes 49160 | tf_op jit(solution)/shard_map/ppermute | solution.py:390
  51.5 5.3 %collective-permute-start.5 = (f32[32,128]{1,0:T(8,128)S(1)}, f32[32,128]{1,0:T(8,128)S(1)}, u32[]{:S(2)}, u32[]{:S(2)}) collective-permute-start(f32[32,128]{1,0:T(8,128)S(1)} %get-tuple-element.8), channel_id=1, source_target_pairs={{0,128},{2,130},{4,132},{6,134},{8,136},{10,138},{12,140},{14,142}... | collective-permute-start | bytes 49160 | tf_op jit(solution)/shard_map/ppermute | solution.py:390
  53.6 3.9 %collective-permute-start.6 = (f32[32,128]{1,0:T(8,128)S(1)}, f32[32,128]{1,0:T(8,128)S(1)}, u32[]{:S(2)}, u32[]{:S(2)}) collective-permute-start(f32[32,128]{1,0:T(8,128)S(1)} %get-tuple-element.9), channel_id=1, source_target_pairs={{0,192},{2,194},{4,196},{6,198},{8,200},{10,202},{12,204},{14,206}... | collective-permute-start | bytes 49160 | tf_op jit(solution)/shard_map/ppermute | solution.py:390
  71.2 34.7 %all-to-all-start = ((bf16[128,8,512]{2,1,0:T(8,128)(2,1)}), bf16[128,8,512]{2,1,0:T(8,128)(2,1)S(1)}, u32[]{:S(2)}, u32[]{:S(2)}) async-start(bf16[128,8,512]{2,1,0:T(8,128)(2,1)} %smooth.1.tiled_ref), calls=%async_computation | async-start | bytes 2097152 | tf_op jit(solution)/shard_map/all_to_all | solution.py:394

commit v12 on v11

--- a/solution.py
+++ b/solution.py
@@ -44,7 +44,7 @@
 
 
 FAR_PLANES = [[PLANE * x + far_end(r) for r in range(PLANE)] for x in range(PLANES)]
-FAR_ALL = [[PLANE * ((r + 2) % PLANES) + far_end(r // PLANES) for r in range(TILES)]]
+FAR_ALL = [[PLANE * (r % PLANES) + far_end(r // PLANES) for r in range(TILES)]]
 
 
 def iota(shape, dim):
@@ -155,7 +155,7 @@
                 for m in range(4):
                     column = 4 * p + m
                     yz = LINE * (2 - 2 * lax.rem(ty, 2) + column // LINE) + (column + 4) % LINE
-                    at = PLANES * yz + lax.rem(ty // 2 + 2, PLANES)
+                    at = PLANES * yz + ty // 2
                     out_ref[at, :, q * LANES : (q + 1) * LANES] = tiles[m].astype(jnp.bfloat16)
         return carry
 
@@ -225,7 +225,7 @@
         kx, first = at // 2, many * (at % 2)
         message = (here_ref, left_ref, far_ref, right_ref)[kx][first : first + many]
         source = lax.rem(x + PLANES - kx, PLANES)
-        frames = [tiled_ref[PLANES * (first + k) + lax.rem(source + 2, PLANES)] for k in range(many)]
+        frames = [tiled_ref[PLANES * (first + k) + source] for k in range(many)]
         prints = message[:, :, :PIXELS].reshape(rows, PIXELS)
         extra = message[:, :, PIXELS:].astype(jnp.float32).reshape(rows, LANES)
         found = lax.dot_general(
@@ -364,7 +364,7 @@
     for x in range(PLANES):
         for y in range(2):
             for z in range(2):
-                source = arrived_ref.at[y, :, z, :, (x + 2) % PLANES]
+                source = arrived_ref.at[y, :, z, :, x]
                 target = out_ref.at[x, 1 - y, :, 1 - z]
                 copies.append(pltpu.make_async_copy(source, target, sems.at[len(copies)]))
     for copy in copies:

time: 107 us -> 108 us (level)
  the two profiles are of different devices: /device:TPU:8 before, /device:TPU:1 now
where the time goes in v12:
time: 108 us; the launch traced here: 107 us
  waiting for transfers between devices  43 us (40%)
  starting transfers between devices  34.2 us (32%)
  Pallas kernels  17 us (16%)
  blocking collectives  10.9 us (10%)
    all_to_all x2, starting transfers between devices, exchanged(): return lax.all_to_all(array, TA, 0, 0, tiled=True, axis_index_groups=ranks)  27.3 us
    all_to_all x2, waiting for transfers between devices, exchanged(): return lax.all_to_all(array, TA, 0, 0, tiled=True, axis_index_groups=ranks)  26.8 us
    ppermute x6, waiting for transfers between devices, moved(): lax.ppermute(array, TA, [(t, (t + PLANE * by) % TILES) for t in range(TIL...  14.6 us
    all_to_all x1, blocking collectives, exchanged(): return lax.all_to_all(array, TA, 0, 0, tiled=True, axis_index_groups=ranks)  10.9 us
    ppermute x6, starting transfers between devices, moved(): lax.ppermute(array, TA, [(t, (t + PLANE * by) % TILES) for t in range(TIL...  6.35 us
    pallas_call x1, Pallas kernels, project(): pl.pallas_call(project_kernel, out_shape=jax.ShapeDtypeStruct((NEURONS, N...  4.7 us
    pallas_call x1, Pallas kernels, smooth(): pl.pallas_call(smooth_kernel, out_shape=jax.ShapeDtypeStruct((TILES, FRAM...  4.55 us
  transfers between devices with their start and end apart: 9, of which 9 were waited for; matrix products, arithmetic and copies ran while one was open for 0% of the time, Pallas kernels for 7%

profile of v12, /device:TPU:1, one launch (start us, length us, event | category | flops | bytes accessed | tf_op | source)
XLA Modules:
  0.0 106.7 jit_solution(11925771179455283126)
XLA Ops:
  0.6 1.7 %pack.1 = bf16[32,8,640]{2,1,0:T(8,128)(2,1)} custom-call(s32[1,8]{1,0:T(1,128)} %bitcast.24, s32[256]{0:T(256)} %order_ref.1, bf16[8,512]{1,0:T(8,128)(2,1)} %bitcast.22, s32[8,512]{1,0:T(8,128)} %bitcast.21, f32[8,128]{1,0:T(8,128)} %bitcast.23), custom_call_target="tpu_custom_call" | custom-call | flops 200000000 | bytes 200000 | tf_op jit(solution)/shard_map/pack/pallas_call | solution.py:200
  2.3 14.2 %all-to-all-start.1 = ((bf16[32,8,640]{2,1,0:T(8,128)(2,1)}), bf16[32,8,640]{2,1,0:T(8,128)(2,1)S(1)}, u32[]{:S(2)}, u32[]{:S(2)}) async-start(bf16[32,8,640]{2,1,0:T(8,128)(2,1)} %pack.1), calls=%async_computation.1 | async-start | bytes 655360 | tf_op jit(solution)/shard_map/all_to_all | solution.py:394
  16.5 0.7 copy-done.3
  17.4 1.8 %register.1.registered_ref = bf16[8,128,512]{2,1,0:T(8,128)(2,1)S(1)} custom-call(s32[8,4,2]{2,1,0:T(4,128)S(1)} %copy.14.shifts_ref, bf16[8,128,512]{2,1,0:T(8,128)(2,1)S(1)} %bitcast.18), custom_call_target="tpu_custom_call" | custom-call | flops 2000000000 | bytes 2000000 | tf_op jit(solution)/shard_map/register/pallas_call | solution.py:107
  19.2 4.9 %all-to-all-done.1.here_ref = bf16[32,8,640]{2,1,0:T(8,128)(2,1)S(1)} async-done(((bf16[32,8,640]{2,1,0:T(8,128)(2,1)}), bf16[32,8,640]{2,1,0:T(8,128)(2,1)S(1)}, u32[]{:S(2)}, u32[]{:S(2)}) %all-to-all-start.1) | async-done | bytes 327712 | tf_op jit(solution)/shard_map/all_to_all | solution.py:394
  24.1 2.5 %collective-permute-start.2 = (bf16[32,8,640]{2,1,0:T(8,128)(2,1)S(1)}, bf16[32,8,640]{2,1,0:T(8,128)(2,1)S(1)}, u32[]{:S(2)}, u32[]{:S(2)}) collective-permute-start(bf16[32,8,640]{2,1,0:T(8,128)(2,1)S(1)} %all-to-all-done.1.here_ref), channel_id=1, source_target_pairs={{0,192},{2,194},{4,196},{6,198},{8,200},{10,202},{12,204},{14,206}... | collective-permute-start | bytes 983048 | tf_op jit(solution)/shard_map/ppermute | solution.py:390
  27.1 0.6 collective-permute-start
  27.7 4.6 %smooth.1.tiled_ref = bf16[128,8,512]{2,1,0:T(8,128)(2,1)} custom-call(bf16[8,128,512]{2,1,0:T(8,128)(2,1)S(1)} %register.1.registered_ref, bf16[512,512]{1,0:T(8,128)(2,1)S(1)} %copy-done.1, bf16[128,128]{1,0:T(8,128)(2,1)S(1)} %copy-done.2), custom_call_target="tpu_custom_call" | custom-call | flops 4000000000 | bytes 3000000 | tf_op jit(solution)/shard_map/smooth/pallas_call | solution.py:166
  32.3 1.1 %collective-permute-done.2.right_ref = bf16[32,8,640]{2,1,0:T(8,128)(2,1)S(1)} collective-permute-done((bf16[32,8,640]{2,1,0:T(8,128)(2,1)S(1)}, bf16[32,8,640]{2,1,0:T(8,128)(2,1)S(1)}, u32[]{:S(2)}, u32[]{:S(2)}) %collective-permute-start.2) | collective-permute-done | bytes 327712 | tf_op jit(solution)/shard_map/ppermute | solution.py:390
  33.4 2.7 %collective-permute-done.1.far_ref = bf16[32,8,640]{2,1,0:T(8,128)(2,1)S(1)} collective-permute-done((bf16[32,8,640]{2,1,0:T(8,128)(2,1)S(1)}, bf16[32,8,640]{2,1,0:T(8,128)(2,1)S(1)}, u32[]{:S(2)}, u32[]{:S(2)}) %collective-permute-start.1) | collective-permute-done | bytes 327712 | tf_op jit(solution)/shard_map/ppermute | solution.py:390
  36.1 8.7 %collective-permute-done.left_ref = bf16[32,8,640]{2,1,0:T(8,128)(2,1)S(1)} collective-permute-done((bf16[32,8,640]{2,1,0:T(8,128)(2,1)S(1)}, bf16[32,8,640]{2,1,0:T(8,128)(2,1)S(1)}, u32[]{:S(2)}, u32[]{:S(2)}) %collective-permute-start) | collective-permute-done | bytes 327712 | tf_op jit(solution)/shard_map/ppermute | solution.py:390
  44.8 4.7 %project.1.mine_ref = f32[256,512]{1,0:T(8,128)S(1)} custom-call(s32[3]{0:T(128)S(1)} %pad_add_fusion.where_ref, bf16[128,8,512]{2,1,0:T(8,128)(2,1)} %smooth.1.tiled_ref, bf16[32,8,640]{2,1,0:T(8,128)(2,1)S(1)} %all-to-all-done.1.here_ref, bf16[32,8,640]{2,1,0:T(8,128)(2,1)S(1)} %collective-permute-done.left_ref, ...), custom_call_target="tpu_custom_call" | custom-call | flops 2000000000 | bytes 3000000 | tf_op jit(solution)/shard_map/project/pallas_call | solution.py:255
  49.5 0.6 collective-permute-start.3
  50.1 1.5 %collective-permute-done.3.other_ref = f32[256,512]{1,0:T(8,128)S(1)} collective-permute-done((f32[256,512]{1,0:T(8,128)S(1)}, f32[256,512]{1,0:T(8,128)S(1)}, u32[]{:S(2)}, u32[]{:S(2)}) %collective-permute-start.3) | collective-permute-done | bytes 524320 | tf_op jit(solution)/shard_map/ppermute | solution.py:407
  51.6 1.9 %solve.1 = (f32[32,128]{1,0:T(8,128)S(1)}, f32[32,128]{1,0:T(8,128)S(1)}, f32[32,128]{1,0:T(8,128)S(1)}, f32[32,128]{1,0:T(8,128)S(1)}) custom-call(s32[3]{0:T(128)S(1)} %pad_add_fusion.where_ref, f32[256,512]{1,0:T(8,128)S(1)} %project.1.mine_ref, f32[256,512]{1,0:T(8,128)S(1)} %collective-permute-done.3.other_ref), custom_call_target="tpu_custom_call" | custom-call | flops 2000000000 | bytes 1000000 | tf_op jit(solution)/shard_map/solve/pallas_call | solution.py:299
  53.6 1.5 %collective-permute-start.5 = (f32[32,128]{1,0:T(8,128)S(1)}, f32[32,128]{1,0:T(8,128)S(1)}, u32[]{:S(2)}, u32[]{:S(2)}) collective-permute-start(f32[32,128]{1,0:T(8,128)S(1)} %get-tuple-element.8), channel_id=1, source_target_pairs={{0,128},{2,130},{4,132},{6,134},{8,136},{10,138},{12,140},{14,142}... | collective-permute-start | bytes 49160 | tf_op jit(solution)/shard_map/ppermute | solution.py:390
  55.1 1.2 %collective-permute-start.6 = (f32[32,128]{1,0:T(8,128)S(1)}, f32[32,128]{1,0:T(8,128)S(1)}, u32[]{:S(2)}, u32[]{:S(2)}) collective-permute-start(f32[32,128]{1,0:T(8,128)S(1)} %get-tuple-element.9), channel_id=1, source_target_pairs={{0,192},{2,194},{4,196},{6,198},{8,200},{10,202},{12,204},{14,206}... | collective-permute-start | bytes 49160 | tf_op jit(solution)/shard_map/ppermute | solution.py:390
  56.3 1.1 %collective-permute-done.4.refs_1_ = f32[32,128]{1,0:T(8,128)S(1)} collective-permute-done((f32[32,128]{1,0:T(8,128)S(1)}, f32[32,128]{1,0:T(8,128)S(1)}, u32[]{:S(2)}, u32[]{:S(2)}) %collective-permute-start.4) | collective-permute-done | bytes 16416 | tf_op jit(solution)/shard_map/ppermute | solution.py:390
  57.8 0.7 collective-permute-done.6.refs_3_
  59.0 10.9 %all_to_all.15 = f32[32,1,128]{2,1,0:T(1,128)S(1)} all-to-all(f32[32,1,128]{2,1,0:T(1,128)S(1)} %bitcast.17), channel_id=1, replica_groups={{40,42,44,46,32,34,36,38,56,58,60,62,48,50,52,54,8,10,12,14,0,2,4,6,24,..., dimensions={0} | all-to-all | bytes 32768 | tf_op jit(solution)/shard_map/all_to_all | solution.py:394
  69.9 13.1 %all-to-all-start = ((bf16[128,8,512]{2,1,0:T(8,128)(2,1)}), bf16[128,8,512]{2,1,0:T(8,128)(2,1)S(1)}, u32[]{:S(2)}, u32[]{:S(2)}) async-start(bf16[128,8,512]{2,1,0:T(8,128)(2,1)} %smooth.1.tiled_ref), calls=%async_computation | async-start | bytes 2097152 | tf_op jit(solution)/shard_map/all_to_all | solution.py:394
  83.0 0.7 join.1
  83.7 21.9 %all-to-all-done = bf16[128,8,512]{2,1,0:T(8,128)(2,1)S(1)} async-done(((bf16[128,8,512]{2,1,0:T(8,128)(2,1)}), bf16[128,8,512]{2,1,0:T(8,128)(2,1)S(1)}, u32[]{:S(2)}, u32[]{:S(2)}) %all-to-all-start) | async-done | bytes 1048608 | tf_op jit(solution)/shard_map/all_to_all | solution.py:394
  105.6 1.1 %store.1 = bf16[4,2,2,2,4,8,512]{6,5,4,3,2,1,0:T(8,128)(2,1)} custom-call(bf16[2,2,2,4,4,8,512]{6,5,4,3,2,1,0:T(8,128)(2,1)S(1)} %bitcast.15), custom_call_target="tpu_custom_call" | custom-call | flops 500000000 | bytes 2000000 | tf_op jit(solution)/shard_map/store/pallas_call | solution.py:377
  (13 shorter events, 1.7 us)
Async XLA Ops:
  0.6 16.8 %copy-start = (bf16[1,8,128,512]{3,2,1,0:T(8,128)(2,1)S(1)}, bf16[1,8,128,512]{3,2,1,0:T(8,128)(2,1)}, u32[]{:S(2)}) copy-start(bf16[1,8,128,512]{3,2,1,0:T(8,128)(2,1)} %param.9) | copy-start | bytes 3145732
  2.3 21.8 %all-to-all-start.1 = ((bf16[32,8,640]{2,1,0:T(8,128)(2,1)}), bf16[32,8,640]{2,1,0:T(8,128)(2,1)S(1)}, u32[]{:S(2)}, u32[]{:S(2)}) async-start(bf16[32,8,640]{2,1,0:T(8,128)(2,1)} %pack.1), calls=%async_computation.1 | async-start | bytes 655360 | tf_op jit(solution)/shard_map/all_to_all | solution.py:394
  16.5 0.7 copy-start.3
  17.4 10.3 %copy-start.1 = (bf16[512,512]{1,0:T(8,128)(2,1)S(1)}, bf16[512,512]{1,0:T(8,128)(2,1)}, u32[]{:S(2)}) copy-start(bf16[512,512]{1,0:T(8,128)(2,1)} %constant.49.clone.wide_ref) | copy-start | bytes 1572868
  17.4 10.3 %copy-start.2 = (bf16[128,128]{1,0:T(8,128)(2,1)S(1)}, bf16[128,128]{1,0:T(8,128)(2,1)}, u32[]{:S(2)}) copy-start(bf16[128,128]{1,0:T(8,128)(2,1)} %constant.50.clone.tall_ref) | copy-start | bytes 98308
  24.1 9.3 %collective-permute-start.2 = (bf16[32,8,640]{2,1,0:T(8,128)(2,1)S(1)}, bf16[32,8,640]{2,1,0:T(8,128)(2,1)S(1)}, u32[]{:S(2)}, u32[]{:S(2)}) collective-permute-start(bf16[32,8,640]{2,1,0:T(8,128)(2,1)S(1)} %all-to-all-done.1.here_ref), channel_id=1, source_target_pairs={{0,192},{2,194},{4,196},{6,198},{8,200},{10,202},{12,204},{14,206}... | collective-permute-start | bytes 983048 | tf_op jit(solution)/shard_map/ppermute | solution.py:390
  26.6 9.5 %collective-permute-start.1 = (bf16[32,8,640]{2,1,0:T(8,128)(2,1)S(1)}, bf16[32,8,640]{2,1,0:T(8,128)(2,1)S(1)}, u32[]{:S(2)}, u32[]{:S(2)}) collective-permute-start(bf16[32,8,640]{2,1,0:T(8,128)(2,1)S(1)} %all-to-all-done.1.here_ref), channel_id=1, source_target_pairs={{0,128},{2,130},{4,132},{6,134},{8,136},{10,138},{12,140},{14,142}... | collective-permute-start | bytes 983048 | tf_op jit(solution)/shard_map/ppermute | solution.py:390
  27.1 17.6 %collective-permute-start = (bf16[32,8,640]{2,1,0:T(8,128)(2,1)S(1)}, bf16[32,8,640]{2,1,0:T(8,128)(2,1)S(1)}, u32[]{:S(2)}, u32[]{:S(2)}) collective-permute-start(bf16[32,8,640]{2,1,0:T(8,128)(2,1)S(1)} %all-to-all-done.1.here_ref), channel_id=1, source_target_pairs={{0,64},{2,66},{4,68},{6,70},{8,72},{10,74},{12,76},{14,78},{16,80}... | collective-permute-start | bytes 983048 | tf_op jit(solution)/shard_map/ppermute | solution.py:390
  49.5 2.1 %collective-permute-start.3 = (f32[256,512]{1,0:T(8,128)S(1)}, f32[256,512]{1,0:T(8,128)S(1)}, u32[]{:S(2)}, u32[]{:S(2)}) collective-permute-start(f32[256,512]{1,0:T(8,128)S(1)} %project.1.mine_ref), channel_id=1, source_target_pairs={{0,1},{1,0},{2,3},{3,2},{4,5},{5,4},{6,7},{7,6},{8,9},{9,8},{10,11... | collective-permute-start | bytes 1572872 | tf_op jit(solution)/shard_map/ppermute | solution.py:407
  53.5 3.9 %collective-permute-start.4 = (f32[32,128]{1,0:T(8,128)S(1)}, f32[32,128]{1,0:T(8,128)S(1)}, u32[]{:S(2)}, u32[]{:S(2)}) collective-permute-start(f32[32,128]{1,0:T(8,128)S(1)} %get-tuple-element.7), channel_id=1, source_target_pairs={{0,64},{2,66},{4,68},{6,70},{8,72},{10,74},{12,76},{14,78},{16,80}... | collective-permute-start | bytes 49160 | tf_op jit(solution)/shard_map/ppermute | solution.py:390
  53.6 4.2 %collective-permute-start.5 = (f32[32,128]{1,0:T(8,128)S(1)}, f32[32,128]{1,0:T(8,128)S(1)}, u32[]{:S(2)}, u32[]{:S(2)}) collective-permute-start(f32[32,128]{1,0:T(8,128)S(1)} %get-tuple-element.8), channel_id=1, source_target_pairs={{0,128},{2,130},{4,132},{6,134},{8,136},{10,138},{12,140},{14,142}... | collective-permute-start | bytes 49160 | tf_op jit(solution)/shard_map/ppermute | solution.py:390
  55.1 3.3 %collective-permute-start.6 = (f32[32,128]{1,0:T(8,128)S(1)}, f32[32,128]{1,0:T(8,128)S(1)}, u32[]{:S(2)}, u32[]{:S(2)}) collective-permute-start(f32[32,128]{1,0:T(8,128)S(1)} %get-tuple-element.9), channel_id=1, source_target_pairs={{0,192},{2,194},{4,196},{6,198},{8,200},{10,202},{12,204},{14,206}... | collective-permute-start | bytes 49160 | tf_op jit(solution)/shard_map/ppermute | solution.py:390
  69.9 35.7 %all-to-all-start = ((bf16[128,8,512]{2,1,0:T(8,128)(2,1)}), bf16[128,8,512]{2,1,0:T(8,128)(2,1)S(1)}, u32[]{:S(2)}, u32[]{:S(2)}) async-start(bf16[128,8,512]{2,1,0:T(8,128)(2,1)} %smooth.1.tiled_ref), calls=%async_computation | async-start | bytes 2097152 | tf_op jit(solution)/shard_map/all_to_all | solution.py:394
